TPU v7x, 1024 devices: a whole 4x8x16 slice. The times are simulated.
1024 devices in a mesh: section: 32 (over y, z_hi), expert: 32 (over z_lo, x, core).
Axes of the slice: x: 4, y: 8, z: 16 (z_hi: 4, z_lo: 4; z = z_hi * 4 + z_lo), core: 2. Of those that a mesh axis runs over, the one named last changes fastest.
Arguments:
- grad_out: bfloat16 [32, 4096, 3584], P('section', 'expert'), may hold values from -6 to 6
- hidden_act: bfloat16 [32, 4096, 1024], P('section', 'expert'), may hold values from -0.29882812 to 0.29882812
- scores: float32 [32, 4096, 32], P('section', 'expert'), may hold values from -8 to 8
- expert_ids: int32 [32, 4096], P('section', 'expert'), may hold values from 0 to 31, as said below
- slot_ids: int32 [32, 4096], P('section', 'expert'), may hold values from 0 to 6, as said below
- counts: int32 [32, 32, 32], P('section'), may hold values from 0 to 7, as said below
- down_weight: bfloat16 [32, 1024, 3584], P('expert'), may hold values from -0.1875 to 0.1875
- router: bfloat16 [32, 3584], replicated, may hold values from -0.8984375 to 0.8984375
Outputs:
- act_grad: bfloat16 [32, 4096, 1024], P('section', 'expert')
- score_grad: float32 [32, 4096, 32], P('section', 'expert')
- upstream_grad: bfloat16 [32, 4096, 3584], P('section', 'expert')
Inputs may be any that keep to these rules, and one draw needn't show every extreme that they name: `expert_ids`: the 128 tokens of one device name each expert at most 7 times; in every section one expert gets exactly 7 tokens from every device. `slot_ids`: a token's slot is the number of earlier tokens of its device that name the same expert. counts[s, e] is at most the number of tokens of device s of the section that name expert e, and may be smaller; routes whose slot is not below it are dropped; for the expert that gets 7 tokens from every device it is 7.
All inputs are finite; a program needn't handle non-finite values.
Results may differ from a plain program's by a relative error of at most 0.009.
Values may be sent and summed in bfloat16 or wider, within the bound.
No kernel may reach another device: no remote copies, remote signals or barrier semaphores. Data moves between devices by JAX's collectives and lax.ppermute only.
A program may use at most 32 MiB of HBM per device.

v0:
```python
import jax
import jax.numpy as jnp
from jax import lax
from jax.sharding import PartitionSpec as P

route_scale = 2.5


def passed_along(block, axis, distance):
    devices = range(lax.axis_size(axis))
    route = [(i - distance, i) for i in devices if i - distance in devices]
    return lax.ppermute(block, axis, route)


def place_rows(values, target, slot_total):
    shape = (slot_total,) + values.shape[1:]
    return jnp.zeros(shape, values.dtype).at[target].set(values, mode="drop")


def on_device(grad_out, hidden_act, scores, expert_ids, slot_ids, counts, down_weight, router):
    token_rows = grad_out[0]
    hidden_rows = hidden_act[0]
    logits = scores[0]
    chosen = expert_ids[0]
    places = slot_ids[0]
    count_table = counts[0]
    weight = down_weight[0]
    tok_rows, model_width = token_rows.shape
    hidden_width = hidden_rows.shape[1]
    experts = logits.shape[1]
    groups = lax.axis_size("expert")
    capacity = max(2, 7 * tok_rows // (4 * groups))
    slot_total = groups * capacity
    own_index = lax.axis_index("expert")
    early_rows = passed_along(token_rows, "section", -1)
    own_counts = lax.dynamic_index_in_dim(count_table, own_index, 0, keepdims=False)
    onehot = chosen[:, None] == jnp.arange(experts, dtype=jnp.int32)[None, :]
    own_limit = jnp.sum(jnp.where(onehot, own_counts[None, :], 0), axis=1)
    is_live = places < own_limit
    chosen_logit = jnp.sum(jnp.where(onehot, logits, 0.0), axis=1)
    sigmoid_vals = jax.nn.sigmoid(chosen_logit)
    gate_bf = (route_scale * sigmoid_vals).astype(jnp.bfloat16)
    masked = jnp.where(is_live[:, None], token_rows, jnp.zeros_like(token_rows))
    target = chosen * capacity + places
    safe_target = jnp.where(is_live, target, 0)
    send_grads = place_rows(masked, target, slot_total).reshape(groups, capacity, model_width)
    got_grads = lax.all_to_all(send_grads, "expert", split_axis=0, concat_axis=0, tiled=True)
    senders = got_grads.shape[0]
    width_items = got_grads.shape[1]
    flat_grads = got_grads.reshape(senders * width_items, model_width)
    back_rows = lax.dot_general(
        flat_grads, weight, (((1,), (1,)), ((), ())), preferred_element_type=jnp.float32
    )
    done_rows = back_rows.reshape(senders, width_items, hidden_width)
    returned = lax.all_to_all(done_rows, "expert", split_axis=0, concat_axis=0, tiled=True)
    own_back = jnp.where(
        is_live[:, None], returned.reshape(slot_total, hidden_width)[safe_target], 0.0
    )
    act_grad = (gate_bf.astype(jnp.float32)[:, None] * own_back).astype(jnp.bfloat16)
    route_grad = jnp.sum(hidden_rows.astype(jnp.float32) * own_back, axis=1)
    slope_term = route_grad * route_scale * sigmoid_vals * (1.0 - sigmoid_vals)
    score_grad = jnp.where(onehot, slope_term[:, None], 0.0)
    score_bf = score_grad.astype(jnp.bfloat16)
    late_scores = passed_along(score_bf, "section", -1)
    upstream = (
        early_rows.astype(jnp.float32)
        + jnp.dot(late_scores, router, preferred_element_type=jnp.float32)
    ).astype(jnp.bfloat16)
    return (act_grad[None], score_grad[None], upstream[None])


def solution(mesh):
    in_specs = (
        P("section", "expert", None),
        P("section", "expert", None),
        P("section", "expert", None),
        P("section", "expert"),
        P("section", "expert"),
        P("section", None, None),
        P("expert", None, None),
        P(),
    )
    out_specs = (
        P("section", "expert", None),
        P("section", "expert", None),
        P("section", "expert", None),
    )
    return jax.shard_map(
        on_device, mesh=mesh, in_specs=in_specs, out_specs=out_specs, check_vma=False
    )
```

profile of v0, /device:TPU:268, one launch (start us, length us, event | category | flops | bytes accessed | tf_op | source)
XLA Modules:
  0.0 188.5 jit_solution(8450137618146924676)
XLA Ops:
  0.6 0.0 copy-start
  0.6 0.7 dynamic-slice_bitcast_fusion
  1.4 0.7 select_reduce_fusion
  2.1 0.7 bitcast_compare_fusion
  2.8 0.7 fusion.15
  3.5 3.9 %scatter_custom_fusion = bf16[224,3584]{1,0:T(8,128)(2,1)} fusion(s32[128]{0:T(128)S(1)} %get-tuple-element.6, pred[128]{0:T(512)(128)(4,1)S(1)} %bitcast_compare_fusion, bf16[]{:T(256)} %constant.6.clone.1, bf16[1,128,3584]{2,1,0:T(8,128)(2,1)} %param.8), kind=kCustom, calls=%fused_computation.7 | custom fusion | flops 458752 | bytes 2524672 | tf_op jit(solution)/shard_map/scatter | solution.py:17
  7.4 1.7 reshape.214
  9.1 53.0 %all_to_all.10 = bf16[32,7,3584]{2,1,0:T(8,128)(2,1)S(1)} all-to-all(bf16[32,7,3584]{2,1,0:T(8,128)(2,1)S(1)} %reshape.214), channel_id=1, replica_groups=mesh['section'=32,'expert'=32] {'expert'}, dimensions={0} | all-to-all | bytes 3211264 | tf_op jit(solution)/shard_map/all_to_all | solution.py:47
  62.1 5.4 %fusion = f32[32,7,1024]{2,0,1:T(8,128)S(1)} fusion(bf16[1,1024,3584]{2,1,0:T(8,128)(2,1)} %param.14, bf16[32,7,3584]{2,1,0:T(8,128)(2,1)S(1)} %all_to_all.10), kind=kOutput, calls=%fused_computation.2 | convolution fusion | flops 1644167168 | bytes 9863168 | tf_op jit(solution)/shard_map/dot_general | solution.py:51
  67.5 0.0 copy-start.1
  67.5 0.0 copy-start.3
  67.5 0.0 copy-start.4
  67.6 1.5 copy.14
  69.1 5.8 %all-to-all-start.1 = ((f32[32,7,1024]{2,1,0:T(8,128)}), f32[32,7,1024]{2,1,0:T(8,128)S(1)}, u32[]{:S(2)}, u32[]{:S(2)}) async-start(f32[32,7,1024]{2,1,0:T(8,128)} %copy.14), calls=%async_computation.1 | async-start | bytes 2097152 | tf_op jit(solution)/shard_map/all_to_all | solution.py:55
  74.9 0.0 copy-done.1
  74.9 1.9 %collective-permute-start = (bf16[128,3584]{1,0:T(8,128)(2,1)S(1)}, bf16[128,3584]{1,0:T(8,128)(2,1)}, u32[]{:S(2)}, u32[]{:S(2)}) collective-permute-start(bf16[128,3584]{1,0:T(8,128)(2,1)S(1)} %bitcast.54), channel_id=1, source_target_pairs={{32,0},{64,32},{96,64},{128,96},{160,128},{192,160},{224,192},{256... | collective-permute-start | bytes 2752520 | tf_op jit(solution)/shard_map/ppermute | solution.py:12
  76.9 0.0 copy-done.3
  76.9 0.0 copy-done.4
  76.9 83.6 %all-to-all-done.1 = f32[32,7,1024]{2,1,0:T(8,128)S(1)} async-done(((f32[32,7,1024]{2,1,0:T(8,128)}), f32[32,7,1024]{2,1,0:T(8,128)S(1)}, u32[]{:S(2)}, u32[]{:S(2)}) %all-to-all-start.1) | async-done | bytes 917536 | tf_op jit(solution)/shard_map/all_to_all | solution.py:55
  160.6 0.1 reshape.215
  160.7 0.0 copy-start.2
  160.7 0.8 gather_fusion
  161.5 0.1 copy-done.2
  161.7 0.2 fusion.8
  161.9 1.9 %collective-permute-start.1 = (bf16[128,32]{0,1:T(8,128)(2,1)S(1)}, bf16[128,32]{0,1:T(8,128)(2,1)S(1)}, u32[]{:S(2)}, u32[]{:S(2)}) collective-permute-start(bf16[128,32]{0,1:T(8,128)(2,1)S(1)} %select_convert_fusion), channel_id=1, source_target_pairs={{32,0},{64,32},{96,64},{128,96},{160,128},{192,160},{224,192},{256... | collective-permute-start | bytes 24584 | tf_op jit(solution)/shard_map/ppermute | solution.py:12
  163.8 0.8 fusion.10
  164.7 0.6 fusion.13
  165.3 0.0 collective-permute-done
  165.3 20.7 %collective-permute-done.1 = bf16[128,32]{0,1:T(8,128)(2,1)S(1)} collective-permute-done((bf16[128,32]{0,1:T(8,128)(2,1)S(1)}, bf16[128,32]{0,1:T(8,128)(2,1)S(1)}, u32[]{:S(2)}, u32[]{:S(2)}) %collective-permute-start.1) | collective-permute-done | bytes 8224 | tf_op jit(solution)/shard_map/ppermute | solution.py:12
  185.9 0.0 copy-done
  185.9 2.5 %fusion.3 = bf16[1,128,3584]{2,1,0:T(8,128)(2,1)} fusion(bf16[128,3584]{1,0:T(8,128)(2,1)} %collective-permute-done, bf16[128,32]{0,1:T(8,128)(2,1)S(1)} %collective-permute-done.1, bf16[32,3584]{1,0:T(8,128)(2,1)S(1)} %copy-done), kind=kOutput, calls=%fused_computation.6 | convolution fusion | flops 30736384 | bytes 2072576 | tf_op jit(solution)/shard_map/dot_general | solution.py:67
  (5 shorter events, 0.1 us)
Async XLA Ops:
  0.6 185.3 %copy-start = (bf16[32,3584]{1,0:T(8,128)(2,1)S(1)}, bf16[32,3584]{1,0:T(8,128)(2,1)}, u32[]{:S(2)}) copy-start(bf16[32,3584]{1,0:T(8,128)(2,1)} %param.15) | copy-start | bytes 688132
  67.5 7.4 %copy-start.1 = (bf16[1,128,3584]{2,1,0:T(8,128)(2,1)S(1)}, bf16[1,128,3584]{2,1,0:T(8,128)(2,1)}, u32[]{:S(2)}) copy-start(bf16[1,128,3584]{2,1,0:T(8,128)(2,1)} %param.8) | copy-start | bytes 2752516
  67.5 9.4 %copy-start.3 = (f32[1,128,32]{1,2,0:T(8,128)S(1)}, f32[1,128,32]{1,2,0:T(8,128)}, u32[]{:S(2)}) copy-start(f32[1,128,32]{1,2,0:T(8,128)} %param.10) | copy-start | bytes 49156
  67.5 9.4 %copy-start.4 = (s32[1,128]{1,0:T(1,128)S(1)}, s32[1,128]{1,0:T(1,128)}, u32[]{:S(2)}) copy-start(s32[1,128]{1,0:T(1,128)} %param.11) | copy-start | bytes 1540
  69.1 91.5 %all-to-all-start.1 = ((f32[32,7,1024]{2,1,0:T(8,128)}), f32[32,7,1024]{2,1,0:T(8,128)S(1)}, u32[]{:S(2)}, u32[]{:S(2)}) async-start(f32[32,7,1024]{2,1,0:T(8,128)} %copy.14), calls=%async_computation.1 | async-start | bytes 2097152 | tf_op jit(solution)/shard_map/all_to_all | solution.py:55
  74.9 90.3 %collective-permute-start = (bf16[128,3584]{1,0:T(8,128)(2,1)S(1)}, bf16[128,3584]{1,0:T(8,128)(2,1)}, u32[]{:S(2)}, u32[]{:S(2)}) collective-permute-start(bf16[128,3584]{1,0:T(8,128)(2,1)S(1)} %bitcast.54), channel_id=1, source_target_pairs={{32,0},{64,32},{96,64},{128,96},{160,128},{192,160},{224,192},{256... | collective-permute-start | bytes 2752520 | tf_op jit(solution)/shard_map/ppermute | solution.py:12
  160.7 1.0 copy-start.2
  161.9 24.0 %collective-permute-start.1 = (bf16[128,32]{0,1:T(8,128)(2,1)S(1)}, bf16[128,32]{0,1:T(8,128)(2,1)S(1)}, u32[]{:S(2)}, u32[]{:S(2)}) collective-permute-start(bf16[128,32]{0,1:T(8,128)(2,1)S(1)} %select_convert_fusion), channel_id=1, source_target_pairs={{32,0},{64,32},{96,64},{128,96},{160,128},{192,160},{224,192},{256... | collective-permute-start | bytes 24584 | tf_op jit(solution)/shard_map/ppermute | solution.py:12
where the time goes:
time: 189 us; the launch traced here: 188 us
  waiting for transfers between devices  104 us (55%)
  blocking collectives  53 us (28%)
  starting transfers between devices  9.68 us (5%)
  matrix products  7.96 us (4%)
  other arithmetic  7.74 us (4%)
  local copies, waits for them, and re-layouts  5.06 us (3%)
    all_to_all x1, waiting for transfers between devices, on_device(): lax.all_to_all(done_rows, 'expert', split_axis=0, concat_axis=0, tiled=True)  83.6 us
    all_to_all x1, blocking collectives, on_device(): lax.all_to_all(send_grads, 'expert', split_axis=0, concat_axis=0, tiled=T...  53 us
    ppermute x2, waiting for transfers between devices, passed_along(): return lax.ppermute(block, axis, route)  20.7 us
    all_to_all x1, starting transfers between devices, on_device(): lax.all_to_all(done_rows, 'expert', split_axis=0, concat_axis=0, tiled=True)  5.84 us
    dot_general x1, matrix products, on_device(): lax.dot_general(flat_grads, weight, (((1,), (1,)), ((), ())), preferred_e...  5.44 us
    scatter x1, other arithmetic, place_rows(): return jnp.zeros(shape, values.dtype).at[target].set(values, mode='drop')  3.95 us
    ppermute x2, starting transfers between devices, passed_along(): return lax.ppermute(block, axis, route)  3.84 us
  transfers between devices with their start and end apart: 3, of which 2 were waited for; matrix products, arithmetic and copies ran while one was open for 1% of the time, Pallas kernels for 0%

commit v1 on v0

v1 whole, which is shorter than its diff:
```python
import jax
import jax.numpy as jnp
from jax import lax
from jax.experimental import pallas as pl
from jax.experimental.pallas import tpu as pltpu
from jax.sharding import Mesh, PartitionSpec as P

route_scale = 2.5
slots = 8
axes = ("y", "zh", "zl", "x", "c")
group = ("x", "c")

NT = (((1,), (1,)), ((), ()))


def prep_kernel(own_ref, chosen_ref, places_ref, counts_ref, tok_ref, near_ref, up_ref, early_ref, late_ref, meta_ref):
    tokens = tok_ref.shape[0]
    half = early_ref.shape[0]
    experts = counts_ref.shape[0]
    rows = near_ref.shape[0]
    own = own_ref[0]
    own_z = own_ref[1]
    chosen = chosen_ref[...]
    places = places_ref[...]
    onehot = lax.broadcasted_iota(jnp.int32, (experts, tokens), 0) == chosen
    own_row = lax.broadcasted_iota(jnp.int32, counts_ref.shape, 0) == own
    own_counts = jnp.where(own_row, counts_ref[...], 0).astype(jnp.float32).astype(jnp.bfloat16)
    picked = jnp.dot(own_counts, onehot.astype(jnp.float32).astype(jnp.bfloat16), preferred_element_type=jnp.float32)
    limit = jnp.sum(picked, axis=0, keepdims=True)
    live = places.astype(jnp.float32) < limit
    offset = (lax.shift_right_logical(chosen, 3) - own_z) & 3
    slot = (chosen & 7) * slots + places
    back_target = jnp.where(live, offset * rows + slot, -1)

    def slot_of(k):
        return jnp.where(live & (offset == k), slot, -1)

    order = lax.broadcasted_iota(jnp.int32, (1, tokens), 1)
    key = (jnp.where(live & (offset == 2), 0, tokens) + order).astype(jnp.float32)
    key_rows = jnp.broadcast_to(key, (tokens, tokens))
    rank = jnp.sum((key_rows.T < key_rows).astype(jnp.float32), axis=0, keepdims=True)
    perm = (lax.broadcasted_iota(jnp.int32, (tokens, tokens), 0) == rank.astype(jnp.int32)).astype(jnp.float32).astype(jnp.bfloat16)
    one_down = slot_of(3).astype(jnp.float32)
    two_down = slot_of(2).astype(jnp.float32)
    row_id = lax.broadcasted_iota(jnp.int32, (8, tokens), 0)
    pair = jnp.where(row_id == 0, one_down, jnp.where(row_id == 1, two_down, 0.0)).astype(jnp.bfloat16)
    moved = lax.dot_general(pair, perm, NT, preferred_element_type=jnp.float32)
    meta = jnp.where(row_id < 2, moved, jnp.where(row_id == 2, rank, back_target.astype(jnp.float32)))
    meta_ref[...] = meta.astype(jnp.int32)

    tok = tok_ref[...]
    slot_id = lax.broadcasted_iota(jnp.int32, (rows, tokens), 0)
    up = (slot_id == slot_of(1)).astype(jnp.float32).astype(jnp.bfloat16)
    up_ref[...] = jnp.dot(up, tok, preferred_element_type=jnp.float32).astype(jnp.bfloat16)
    ordered = jnp.dot(perm, tok, preferred_element_type=jnp.float32).astype(jnp.bfloat16)
    early_ref[...] = ordered[:half]
    late_ref[...] = ordered[half:]
    near = (slot_id == slot_of(0)).astype(jnp.float32).astype(jnp.bfloat16)
    near_ref[...] = jnp.dot(near, tok, preferred_element_type=jnp.float32).astype(jnp.bfloat16)


def pack_both_kernel(meta_ref, early_ref, late_ref, out_ref):
    rows = out_ref.shape[0]
    half = early_ref.shape[0]
    tokens = 2 * half
    pick = lax.broadcasted_iota(jnp.int32, (rows, tokens), 0) == meta_ref[0:1, :]
    pick = pick.astype(jnp.float32).astype(jnp.bfloat16)
    out = jnp.dot(pick[:, :half], early_ref[...], preferred_element_type=jnp.float32)
    out = out + jnp.dot(pick[:, half:], late_ref[...], preferred_element_type=jnp.float32)
    out_ref[...] = out.astype(jnp.bfloat16)


def pack_early_kernel(meta_ref, early_ref, out_ref):
    rows = out_ref.shape[0]
    half = early_ref.shape[0]
    pick = lax.broadcasted_iota(jnp.int32, (rows, half), 0) == meta_ref[1:2, :half]
    pick = pick.astype(jnp.float32).astype(jnp.bfloat16)
    out_ref[...] = jnp.dot(pick, early_ref[...], preferred_element_type=jnp.float32).astype(jnp.bfloat16)


def back_kernel(meta_ref, chosen_ref, scores_ref, hidden_ref, r0_ref, r1_ref, r2_ref, r3_ref, act_ref, score_ref, score_bf_ref):
    tokens = hidden_ref.shape[0]
    experts = scores_ref.shape[0]
    rows = r0_ref.shape[0]
    target = jnp.broadcast_to(meta_ref[3:4, :].astype(jnp.float32), (tokens, tokens)).T[:, :1].astype(jnp.int32)
    own_back = jnp.zeros(hidden_ref.shape, jnp.float32)
    for k, ref in enumerate((r0_ref, r1_ref, r2_ref, r3_ref)):
        lane = lax.broadcasted_iota(jnp.int32, (tokens, rows), 1) + k * rows
        pick = (lane == target).astype(jnp.float32).astype(jnp.bfloat16)
        own_back = own_back + jnp.dot(pick, ref[...], preferred_element_type=jnp.float32)
    onehot = lax.broadcasted_iota(jnp.int32, (experts, tokens), 0) == chosen_ref[...]
    logit = jnp.sum(jnp.where(onehot, scores_ref[...], 0.0), axis=0, keepdims=True)
    sigmoid_vals = jax.nn.sigmoid(logit)
    gate = (route_scale * sigmoid_vals).astype(jnp.bfloat16).astype(jnp.float32)
    gate_col = jnp.broadcast_to(gate, (tokens, tokens)).T[:, :1]
    act_ref[...] = (gate_col * own_back).astype(jnp.bfloat16)
    route = jnp.sum(hidden_ref[...].astype(jnp.float32) * own_back, axis=1, keepdims=True)
    route_row = jnp.broadcast_to(route, (tokens, tokens)).T[:1, :]
    slope = route_row * route_scale * sigmoid_vals * (1.0 - sigmoid_vals)
    score = jnp.where(onehot, slope, 0.0)
    score_ref[...] = score
    score_bf_ref[...] = score.astype(jnp.bfloat16)


def up_kernel(meta_ref, early_ref, late_ref, score_ref, router_ref, out_ref):
    half = early_ref.shape[0]
    tokens = 2 * half
    rank = jnp.broadcast_to(meta_ref[2:3, :].astype(jnp.float32), (tokens, tokens)).T.astype(jnp.int32)
    pick = (lax.broadcasted_iota(jnp.int32, (tokens, tokens), 1) == rank).astype(jnp.float32).astype(jnp.bfloat16)
    scores = score_ref[...].astype(jnp.float32).T.astype(jnp.bfloat16)
    out = jnp.dot(pick[:, :half], early_ref[...], preferred_element_type=jnp.float32)
    out = out + jnp.dot(pick[:, half:], late_ref[...], preferred_element_type=jnp.float32)
    out = out + jnp.dot(scores, router_ref[...], preferred_element_type=jnp.float32)
    out_ref[...] = out.astype(jnp.bfloat16)


def whole(count):
    return [pl.BlockSpec(memory_space=pltpu.VMEM)] * count


def sds(shape, dtype=jnp.bfloat16):
    return jax.ShapeDtypeStruct(shape, dtype)


def on_device(dims, grad_out, hidden_act, scores, expert_ids, slot_ids, counts, down_weight, router):
    ny, nz, nzl, nxc = dims
    tok = grad_out[0]
    tokens, width = tok.shape
    hidden_width = hidden_act.shape[2]
    half = tokens // 2
    rows = nxc * slots
    weight = down_weight[0]
    own = lax.axis_index(("zl", "x", "c"))
    own_ids = jnp.stack([own, lax.axis_index("zl")]).astype(jnp.int32)

    def shift(value, distance, turn, skip=False):
        route = []
        for y in range(ny):
            for z in range(nz):
                if skip and y * nz + z < 4:
                    continue
                to_z = (z + distance) % nz
                to_y = (y + (z + distance) // nz) % ny if turn else y
                for j in range(nxc):
                    route.append(((y * nz + z) * nxc + j, (to_y * nz + to_z) * nxc + j))
        return lax.ppermute(value, axes, route)

    def last_hop(value):
        route = []
        for y in range(ny):
            for z in range(nz):
                at = y * nz + z
                start = (at + 3) % (ny * nz)
                if start < nzl:
                    continue
                to = (at - 1) % (ny * nz)
                for j in range(nxc):
                    route.append((at * nxc + j, to * nxc + j))
        return lax.ppermute(value, axes, route)

    def to_previous(value):
        route = [(s * nxc + j, (s - nzl) * nxc + j) for s in range(nzl, ny * nz) for j in range(nxc)]
        return lax.ppermute(value, axes, route)

    def exchange(value):
        cut = value.reshape(nxc, slots, value.shape[1])
        return lax.all_to_all(cut, group, split_axis=0, concat_axis=0, tiled=True).reshape(value.shape)

    def serve(value):
        return lax.dot_general(value, weight, NT, preferred_element_type=jnp.float32).astype(jnp.bfloat16)

    near, up, early, late, meta = pl.pallas_call(
        prep_kernel,
        out_shape=(sds((rows, width)), sds((rows, width)), sds((half, width)), sds((half, width)), sds((8, tokens), jnp.int32)),
        in_specs=[pl.BlockSpec(memory_space=pltpu.SMEM)] + whole(4),
        out_specs=tuple(whole(5)),
    )(own_ids, expert_ids, slot_ids, counts[0], tok)
    up_got = shift(up, 1, False)
    early1 = shift(early, -1, True)
    late1 = shift(late, -1, True)
    meta1 = shift(meta, -1, True)
    early2 = shift(early1, -1, True)
    late2 = shift(late1, -1, True)
    meta2 = shift(meta1, -1, True)
    meta4 = to_previous(meta)
    early3 = shift(early2, -1, True)
    late3 = shift(late2, -1, True)
    early4 = last_hop(early3)
    late4 = last_hop(late3)
    one = pl.pallas_call(
        pack_both_kernel, out_shape=sds((rows, width)), in_specs=whole(3), out_specs=whole(1)[0]
    )(meta1, early1, late1)
    two = pl.pallas_call(
        pack_early_kernel, out_shape=sds((rows, width)), in_specs=whole(2), out_specs=whole(1)[0]
    )(meta2, early2)
    near_rows = exchange(near)
    up_rows = exchange(up_got)
    one_rows = exchange(one)
    two_rows = exchange(two)
    near_back = serve(near_rows)
    up_back = serve(up_rows)
    one_back = serve(one_rows)
    two_back = serve(two_rows)
    r0 = exchange(near_back)
    r1 = exchange(up_back)
    r3 = exchange(one_back)
    r2 = exchange(two_back)
    r1 = shift(r1, -1, False)
    r3 = shift(r3, 1, True)
    r2 = shift(r2, 2, True)
    act, score, score_bf = pl.pallas_call(
        back_kernel,
        out_shape=(sds((tokens, hidden_width)), sds((scores.shape[2], tokens), jnp.float32), sds((scores.shape[2], tokens))),
        in_specs=whole(8),
        out_specs=tuple(whole(3)),
    )(meta, expert_ids, scores[0].T, hidden_act[0], r0, r1, r2, r3)
    late_score = to_previous(score_bf)
    upstream = pl.pallas_call(
        up_kernel, out_shape=sds((tokens, width)), in_specs=whole(5), out_specs=whole(1)[0]
    )(meta4, early4, late4, late_score, router)
    return act[None], score.T[None], upstream[None]


def solution(mesh):
    cut = Mesh(mesh.devices.reshape(8, 4, 4, 4, 2), axes)
    dims = (8, 16, 4, 8)
    section = ("y", "zh")
    expert = ("zl", "x", "c")
    rows = P(section, expert, None)
    in_specs = (rows, rows, rows, P(section, expert), P(section, expert), P(section, None, None), P(expert, None, None), P())

    def body(*arrays):
        return on_device(dims, *arrays)

    return jax.shard_map(body, mesh=cut, in_specs=in_specs, out_specs=(rows, rows, rows), check_vma=False)
```

time: 189 us -> 186 us (0.984)
  the two profiles are of different devices: /device:TPU:268 before, /device:TPU:160 now
where the time goes in v1:
time: 186 us; the launch traced here: 184 us
  starting transfers between devices  108 us (58%)
  matrix products  23.6 us (13%)
  waiting for transfers between devices  22.3 us (12%)
  Pallas kernels  13.2 us (7%)
  blocking collectives  10.8 us (6%)
  local copies, waits for them, and re-layouts  4.97 us (3%)
    ppermute x12, starting transfers between devices, shift(): return lax.ppermute(value, axes, route)  52.3 us
    all_to_all x7, starting transfers between devices, exchange(): lax.all_to_all(cut, group, split_axis=0, concat_axis=0, tiled=True)  30.2 us
    dot_general x4, matrix products, serve(): lax.dot_general(value, weight, NT, preferred_element_type=jnp.float32)  23.6 us
    ppermute x2, starting transfers between devices, to_previous(): return lax.ppermute(value, axes, route)  17.2 us
    all_to_all x1, blocking collectives, exchange(): lax.all_to_all(cut, group, split_axis=0, concat_axis=0, tiled=True)  10.8 us
    ppermute x2, starting transfers between devices, last_hop(): return lax.ppermute(value, axes, route)  8.19 us
    ppermute x12, waiting for transfers between devices, shift(): return lax.ppermute(value, axes, route)  7.71 us
    ppermute x2, waiting for transfers between devices, to_previous(): return lax.ppermute(value, axes, route)  7.48 us
  transfers between devices with their start and end apart: 23, of which 5 were waited for; matrix products, arithmetic and copies ran while one was open for 13% of the time, Pallas kernels for 4%

profile of v1, /device:TPU:160, one launch (start us, length us, event | category | flops | bytes accessed | tf_op | source)
XLA Modules:
  0.0 184.3 jit_solution(9368988206336005666)
XLA Ops:
  0.6 0.6 pad_add_fusion.own_ref
  1.3 3.1 %shard_map.103 = (bf16[64,3584]{1,0:T(8,128)(2,1)}, bf16[64,3584]{1,0:T(8,128)(2,1)}, bf16[64,3584]{1,0:T(8,128)(2,1)}, bf16[64,3584]{1,0:T(8,128)(2,1)}, s32[8,128]{1,0:T(8,128)}) custom-call(s32[2]{0:T(128)} %pad_add_fusion.own_ref, s32[1,128]{1,0:T(1,128)} %chosen_ref.3, s32[1,128]{1,0:T(1,128)} %places_ref.1, s32[32,32]{1,0:T(8,128)} %bitcast.75, ...), custom_call_target="tpu_custom_call" | custom-call | tf_op jit(solution)/shard_map/pallas_call | solution.py:172
  4.3 4.3 %collective-permute-start = (bf16[64,3584]{1,0:T(8,128)(2,1)}, bf16[64,3584]{1,0:T(8,128)(2,1)}, u32[]{:S(2)}, u32[]{:S(2)}) collective-permute-start(bf16[64,3584]{1,0:T(8,128)(2,1)} %get-tuple-element.13), channel_id=1, source_target_pairs={{0,8},{1,9},{2,10},{3,11},{4,12},{5,13},{6,14},{7,15},{8,16},{9,17... | collective-permute-start | bytes 1376264 | tf_op jit(solution)/shard_map/ppermute | solution.py:146
  8.6 1.9 %collective-permute-start.4 = (bf16[64,3584]{1,0:T(8,128)(2,1)}, bf16[64,3584]{1,0:T(8,128)(2,1)S(1)}, u32[]{:S(2)}, u32[]{:S(2)}) collective-permute-start(bf16[64,3584]{1,0:T(8,128)(2,1)} %get-tuple-element.14), channel_id=1, source_target_pairs={{0,1016},{1,1017},{2,1018},{3,1019},{4,1020},{5,1021},{6,1022},{7,... | collective-permute-start | bytes 1376264 | tf_op jit(solution)/shard_map/ppermute | solution.py:146
  10.5 1.9 %collective-permute-start.7 = (bf16[64,3584]{1,0:T(8,128)(2,1)}, bf16[64,3584]{1,0:T(8,128)(2,1)S(1)}, u32[]{:S(2)}, u32[]{:S(2)}) collective-permute-start(bf16[64,3584]{1,0:T(8,128)(2,1)} %get-tuple-element.15), channel_id=1, source_target_pairs={{0,1016},{1,1017},{2,1018},{3,1019},{4,1020},{5,1021},{6,1022},{7,... | collective-permute-start | bytes 1376264 | tf_op jit(solution)/shard_map/ppermute | solution.py:146
  12.5 6.3 %collective-permute-done = bf16[64,3584]{1,0:T(8,128)(2,1)} collective-permute-done((bf16[64,3584]{1,0:T(8,128)(2,1)}, bf16[64,3584]{1,0:T(8,128)(2,1)}, u32[]{:S(2)}, u32[]{:S(2)}) %collective-permute-start) | collective-permute-done | bytes 458784 | tf_op jit(solution)/shard_map/ppermute | solution.py:146
  18.8 4.3 %all-to-all-start.2 = ((bf16[8,8,3584]{2,1,0:T(8,128)(2,1)}), bf16[8,8,3584]{2,1,0:T(8,128)(2,1)S(1)}, u32[]{:S(2)}, u32[]{:S(2)}) async-start(bf16[8,8,3584]{2,1,0:T(8,128)(2,1)} %bitcast.12), calls=%async_computation.2 | async-start | bytes 917504 | tf_op jit(solution)/shard_map/all_to_all | solution.py:167
  23.1 8.7 %collective-permute-start.2 = (s32[8,128]{1,0:T(8,128)}, s32[8,128]{1,0:T(8,128)S(1)}, u32[]{:S(2)}, u32[]{:S(2)}) collective-permute-start(s32[8,128]{1,0:T(8,128)} %get-tuple-element.11.meta_ref), channel_id=1, source_target_pairs={{0,1016},{1,1017},{2,1018},{3,1019},{4,1020},{5,1021},{6,1022},{7,... | collective-permute-start | bytes 12296 | tf_op jit(solution)/shard_map/ppermute | solution.py:146
  31.8 0.0 collective-permute-done.4.early_ref
  31.8 9.0 %collective-permute-start.5 = (bf16[64,3584]{1,0:T(8,128)(2,1)S(1)}, bf16[64,3584]{1,0:T(8,128)(2,1)S(1)}, u32[]{:S(2)}, u32[]{:S(2)}) collective-permute-start(bf16[64,3584]{1,0:T(8,128)(2,1)S(1)} %collective-permute-done.4.early_ref), channel_id=1, source_target_pairs={{0,1016},{1,1017},{2,1018},{3,1019},{4,1020},{5,1021},{6,1022},{7,... | collective-permute-start | bytes 1376264 | tf_op jit(solution)/shard_map/ppermute | solution.py:146
  40.8 0.0 collective-permute-done.2.meta_ref
  40.8 0.0 copy-start.12
  40.9 0.0 collective-permute-done.7.late_ref
  40.9 0.6 copy-done.12
  41.4 0.8 copy-done.2
  42.2 2.4 %shard_map.105 = bf16[64,3584]{1,0:T(8,128)(2,1)} custom-call(s32[8,128]{1,0:T(8,128)} %copy-done.12, bf16[64,3584]{1,0:T(8,128)(2,1)} %copy-done.4, bf16[64,3584]{1,0:T(8,128)(2,1)} %copy-done.2), custom_call_target="tpu_custom_call" | custom-call | tf_op jit(solution)/shard_map/pallas_call | solution.py:190
  44.6 4.9 %all-to-all-start.6 = ((bf16[8,8,3584]{2,1,0:T(8,128)(2,1)}), bf16[8,8,3584]{2,1,0:T(8,128)(2,1)S(1)}, u32[]{:S(2)}, u32[]{:S(2)}) async-start(bf16[8,8,3584]{2,1,0:T(8,128)(2,1)} %bitcast.67), calls=%async_computation.6 | async-start | bytes 917504 | tf_op jit(solution)/shard_map/all_to_all | solution.py:167
  49.5 6.1 %fusion.26 = bf16[8,8,1024]{2,1,0:T(8,128)(2,1)} fusion(bf16[1,1024,3584]{2,1,0:T(8,128)(2,1)} %param.14, bf16[8,8,3584]{2,1,0:T(8,128)(2,1)S(1)} %all-to-all-done.2), kind=kOutput, calls=%fused_computation.14 | convolution fusion | flops 469827584 | bytes 7929856 | tf_op jit(solution)/shard_map/dot_general | solution.py:170
  55.6 3.6 %all-to-all-done.6 = bf16[8,8,3584]{2,1,0:T(8,128)(2,1)S(1)} async-done(((bf16[8,8,3584]{2,1,0:T(8,128)(2,1)}), bf16[8,8,3584]{2,1,0:T(8,128)(2,1)S(1)}, u32[]{:S(2)}, u32[]{:S(2)}) %all-to-all-start.6) | async-done | bytes 458784 | tf_op jit(solution)/shard_map/all_to_all | solution.py:167
  59.2 3.4 %all-to-all-start.3 = ((bf16[8,8,1024]{2,1,0:T(8,128)(2,1)}), bf16[8,8,1024]{2,1,0:T(8,128)(2,1)S(1)}, u32[]{:S(2)}, u32[]{:S(2)}) async-start(bf16[8,8,1024]{2,1,0:T(8,128)(2,1)} %fusion.26), calls=%async_computation.3 | async-start | bytes 262144 | tf_op jit(solution)/shard_map/all_to_all | solution.py:167
  62.6 3.5 %collective-permute-start.3 = (s32[8,128]{1,0:T(8,128)S(1)}, s32[8,128]{1,0:T(8,128)S(1)}, u32[]{:S(2)}, u32[]{:S(2)}) collective-permute-start(s32[8,128]{1,0:T(8,128)S(1)} %copy-done.13), channel_id=1, source_target_pairs={{0,1016},{1,1017},{2,1018},{3,1019},{4,1020},{5,1021},{6,1022},{7,... | collective-permute-start | bytes 12296 | tf_op jit(solution)/shard_map/ppermute | solution.py:146
  66.1 2.7 %collective-permute-start.12 = (bf16[64,3584]{1,0:T(8,128)(2,1)S(1)}, bf16[64,3584]{1,0:T(8,128)(2,1)}, u32[]{:S(2)}, u32[]{:S(2)}) collective-permute-start(bf16[64,3584]{1,0:T(8,128)(2,1)S(1)} %copy-done.3), channel_id=1, source_target_pairs={{0,1016},{1,1017},{2,1018},{3,1019},{4,1020},{5,1021},{6,1022},{7,... | collective-permute-start | bytes 1376264 | tf_op jit(solution)/shard_map/ppermute | solution.py:146
  68.8 0.0 copy-start.15
  68.8 0.0 collective-permute-done.5.early_ref
  68.8 0.6 copy-done.15
  69.4 0.8 copy-done
  70.2 2.1 %shard_map.104 = bf16[64,3584]{1,0:T(8,128)(2,1)} custom-call(s32[8,128]{1,0:T(8,128)} %copy-done.15, bf16[64,3584]{1,0:T(8,128)(2,1)} %copy-done), custom_call_target="tpu_custom_call" | custom-call | tf_op jit(solution)/shard_map/pallas_call | solution.py:193
  72.2 0.0 all-to-all-done.3
  72.2 4.7 %all-to-all-start.4 = ((bf16[8,8,3584]{2,1,0:T(8,128)(2,1)}), bf16[8,8,3584]{2,1,0:T(8,128)(2,1)S(1)}, u32[]{:S(2)}, u32[]{:S(2)}) async-start(bf16[8,8,3584]{2,1,0:T(8,128)(2,1)} %bitcast.66), calls=%async_computation.4 | async-start | bytes 917504 | tf_op jit(solution)/shard_map/all_to_all | solution.py:167
  76.9 6.1 %fusion.20 = bf16[8,8,1024]{2,1,0:T(8,128)(2,1)} fusion(bf16[1,1024,3584]{2,1,0:T(8,128)(2,1)} %param.14, bf16[8,8,3584]{2,1,0:T(8,128)(2,1)S(1)} %all-to-all-done.6), kind=kOutput, calls=%fused_computation.12 | convolution fusion | flops 469827584 | bytes 7929856 | tf_op jit(solution)/shard_map/dot_general | solution.py:170
  83.0 3.5 %all-to-all-done.4 = bf16[8,8,3584]{2,1,0:T(8,128)(2,1)S(1)} async-done(((bf16[8,8,3584]{2,1,0:T(8,128)(2,1)}), bf16[8,8,3584]{2,1,0:T(8,128)(2,1)S(1)}, u32[]{:S(2)}, u32[]{:S(2)}) %all-to-all-start.4) | async-done | bytes 458784 | tf_op jit(solution)/shard_map/all_to_all | solution.py:167
  86.5 3.4 %all-to-all-start.7 = ((bf16[8,8,1024]{2,1,0:T(8,128)(2,1)}), bf16[8,8,1024]{2,1,0:T(8,128)(2,1)S(1)}, u32[]{:S(2)}, u32[]{:S(2)}) async-start(bf16[8,8,1024]{2,1,0:T(8,128)(2,1)} %fusion.20), calls=%async_computation.7 | async-start | bytes 262144 | tf_op jit(solution)/shard_map/all_to_all | solution.py:167
  89.9 6.0 %fusion.23 = bf16[8,8,1024]{2,1,0:T(8,128)(2,1)} fusion(bf16[1,1024,3584]{2,1,0:T(8,128)(2,1)} %param.14, bf16[8,8,3584]{2,1,0:T(8,128)(2,1)S(1)} %all-to-all-done.4), kind=kOutput, calls=%fused_computation.13 | convolution fusion | flops 469827584 | bytes 7929856 | tf_op jit(solution)/shard_map/dot_general | solution.py:170
  96.0 4.7 %all-to-all-start.5 = ((bf16[8,8,1024]{2,1,0:T(8,128)(2,1)}), bf16[8,8,1024]{2,1,0:T(8,128)(2,1)S(1)}, u32[]{:S(2)}, u32[]{:S(2)}) async-start(bf16[8,8,1024]{2,1,0:T(8,128)(2,1)} %fusion.23), calls=%async_computation.5 | async-start | bytes 262144 | tf_op jit(solution)/shard_map/all_to_all | solution.py:167
  100.7 7.7 %collective-permute-start.10 = (bf16[64,3584]{1,0:T(8,128)(2,1)S(1)}, bf16[64,3584]{1,0:T(8,128)(2,1)S(1)}, u32[]{:S(2)}, u32[]{:S(2)}) collective-permute-start(bf16[64,3584]{1,0:T(8,128)(2,1)S(1)} %copy-done.1), channel_id=1, source_target_pairs={{0,1016},{1,1017},{2,1018},{3,1019},{4,1020},{5,1021},{6,1022},{7,... | collective-permute-start | bytes 1376264 | tf_op jit(solution)/shard_map/ppermute | solution.py:146
  108.4 0.0 collective-permute-done.12
  108.4 1.9 %collective-permute-start.13 = (bf16[64,3584]{1,0:T(8,128)(2,1)}, bf16[64,3584]{1,0:T(8,128)(2,1)S(1)}, u32[]{:S(2)}, u32[]{:S(2)}) collective-permute-start(bf16[64,3584]{1,0:T(8,128)(2,1)} %collective-permute-done.12), channel_id=1, source_target_pairs={{0,1016},{1,1017},{2,1018},{3,1019},{4,1020},{5,1021},{6,1022},{7,... | collective-permute-start | bytes 1376264 | tf_op jit(solution)/shard_map/ppermute | solution.py:146
  110.3 0.0 all-to-all-done.5
  110.4 4.8 %all-to-all-start = ((bf16[8,8,3584]{2,1,0:T(8,128)(2,1)}), bf16[8,8,3584]{2,1,0:T(8,128)(2,1)S(1)}, u32[]{:S(2)}, u32[]{:S(2)}) async-start(bf16[8,8,3584]{2,1,0:T(8,128)(2,1)} %bitcast.7), calls=%async_computation | async-start | bytes 917504 | tf_op jit(solution)/shard_map/all_to_all | solution.py:167
  115.2 6.8 %collective-permute-start.1 = (bf16[64,1024]{1,0:T(8,128)(2,1)S(1)}, bf16[64,1024]{1,0:T(8,128)(2,1)S(1)}, u32[]{:S(2)}, u32[]{:S(2)}) collective-permute-start(bf16[64,1024]{1,0:T(8,128)(2,1)S(1)} %bitcast.72), channel_id=1, source_target_pairs={{0,120},{1,121},{2,122},{3,123},{4,124},{5,125},{6,126},{7,127},{8... | collective-permute-start | bytes 393224 | tf_op jit(solution)/shard_map/ppermute | solution.py:146
  122.0 1.9 %collective-permute-start.8 = (bf16[64,1024]{1,0:T(8,128)(2,1)S(1)}, bf16[64,1024]{1,0:T(8,128)(2,1)S(1)}, u32[]{:S(2)}, u32[]{:S(2)}) collective-permute-start(bf16[64,1024]{1,0:T(8,128)(2,1)S(1)} %bitcast.73), channel_id=1, source_target_pairs={{0,8},{1,9},{2,10},{3,11},{4,12},{5,13},{6,14},{7,15},{8,16},{9,17... | collective-permute-start | bytes 393224 | tf_op jit(solution)/shard_map/ppermute | solution.py:146
  123.9 0.0 collective-permute-done.10
  123.9 3.9 %collective-permute-start.11 = (bf16[64,3584]{1,0:T(8,128)(2,1)S(1)}, bf16[64,3584]{1,0:T(8,128)(2,1)S(1)}, u32[]{:S(2)}, u32[]{:S(2)}) collective-permute-start(bf16[64,3584]{1,0:T(8,128)(2,1)S(1)} %collective-permute-done.10), channel_id=1, source_target_pairs={{8,0},{9,1},{10,2},{11,3},{12,4},{13,5},{14,6},{15,7},{16,8},{17,9... | collective-permute-start | bytes 1376264 | tf_op jit(solution)/shard_map/ppermute | solution.py:159
  127.9 1.4 collective-permute-done.13
  129.2 4.3 %collective-permute-start.14 = (bf16[64,3584]{1,0:T(8,128)(2,1)S(1)}, bf16[64,3584]{1,0:T(8,128)(2,1)S(1)}, u32[]{:S(2)}, u32[]{:S(2)}) collective-permute-start(bf16[64,3584]{1,0:T(8,128)(2,1)S(1)} %collective-permute-done.13), channel_id=1, source_target_pairs={{8,0},{9,1},{10,2},{11,3},{12,4},{13,5},{14,6},{15,7},{16,8},{17,9... | collective-permute-start | bytes 1376264 | tf_op jit(solution)/shard_map/ppermute | solution.py:159
  133.5 1.9 %collective-permute-start.6 = (bf16[64,1024]{1,0:T(8,128)(2,1)S(1)}, bf16[64,1024]{1,0:T(8,128)(2,1)S(1)}, u32[]{:S(2)}, u32[]{:S(2)}) collective-permute-start(bf16[64,1024]{1,0:T(8,128)(2,1)S(1)} %bitcast.74), channel_id=1, source_target_pairs={{0,16},{1,17},{2,18},{3,19},{4,20},{5,21},{6,22},{7,23},{8,24},{9,... | collective-permute-start | bytes 393224 | tf_op jit(solution)/shard_map/ppermute | solution.py:146
  135.4 0.0 all-to-all-done
  135.4 5.4 %fusion.29 = bf16[8,8,1024]{2,1,0:T(8,128)(2,1)S(1)} fusion(bf16[1,1024,3584]{2,1,0:T(8,128)(2,1)} %param.14, bf16[8,8,3584]{2,1,0:T(8,128)(2,1)S(1)} %all-to-all-done), kind=kOutput, calls=%fused_computation.15 | convolution fusion | flops 469827584 | bytes 7929856 | tf_op jit(solution)/shard_map/dot_general | solution.py:170
  140.8 10.8 %all_to_all.40 = bf16[8,8,1024]{2,1,0:T(8,128)(2,1)} all-to-all(bf16[8,8,1024]{2,1,0:T(8,128)(2,1)S(1)} %fusion.29), channel_id=1, replica_groups=mesh['y'=8,'zh'=4,'zl'=4,'x'=4,'c'=2] {'x','c'}, dimensions={0} | all-to-all | bytes 262144 | tf_op jit(solution)/shard_map/all_to_all | solution.py:167
  151.6 0.0 collective-permute-done.1.r1_ref
  151.6 0.0 collective-permute-done.8.r3_ref
  151.7 0.6 copy-done.7
  152.3 0.0 copy-done.8
  152.3 0.1 copy-done.9
  152.4 2.5 %shard_map.106 = (bf16[128,1024]{1,0:T(8,128)(2,1)}, f32[32,128]{1,0:T(8,128)}, bf16[32,128]{1,0:T(8,128)(2,1)}) custom-call(s32[8,128]{1,0:T(8,128)} %get-tuple-element.11.meta_ref, s32[1,128]{1,0:T(1,128)} %chosen_ref.3, f32[32,128]{1,0:T(8,128)} %bitcast.76, bf16[128,1024]{1,0:T(8,128)(2,1)} %bitcast.71, bf16[64,1024]{1,0:T(8,128)(2,1)} %bitcast.70, ...), custom_call_target="tpu_custom_call" | custom-call | tf_op jit(solution)/shard_map/pallas_call | solution.py:211
  154.9 15.3 %collective-permute-start.15 = (bf16[32,128]{1,0:T(8,128)(2,1)}, bf16[32,128]{1,0:T(8,128)(2,1)S(1)}, u32[]{:S(2)}, u32[]{:S(2)}) collective-permute-start(bf16[32,128]{1,0:T(8,128)(2,1)} %get-tuple-element.18), channel_id=1, source_target_pairs={{32,0},{33,1},{34,2},{35,3},{36,4},{37,5},{38,6},{39,7},{40,8},{41... | collective-permute-start | bytes 24584 | tf_op jit(solution)/shard_map/ppermute | solution.py:163
  170.2 1.9 %collective-permute-start.9 = (s32[8,128]{1,0:T(8,128)S(1)}, s32[8,128]{1,0:T(8,128)S(1)}, u32[]{:S(2)}, u32[]{:S(2)}) collective-permute-start(s32[8,128]{1,0:T(8,128)S(1)} %copy-done.11), channel_id=1, source_target_pairs={{32,0},{33,1},{34,2},{35,3},{36,4},{37,5},{38,6},{39,7},{40,8},{41... | collective-permute-start | bytes 12296 | tf_op jit(solution)/shard_map/ppermute | solution.py:163
  172.1 7.5 %collective-permute-done.9.meta_ref = s32[8,128]{1,0:T(8,128)S(1)} collective-permute-done((s32[8,128]{1,0:T(8,128)S(1)}, s32[8,128]{1,0:T(8,128)S(1)}, u32[]{:S(2)}, u32[]{:S(2)}) %collective-permute-start.9) | collective-permute-done | bytes 4128 | tf_op jit(solution)/shard_map/ppermute | solution.py:163
  179.6 0.0 collective-permute-done.11.early_ref
  179.7 0.5 copy-done.14
  180.2 0.0 copy-done.10
  180.2 0.2 copy-done.5
  180.4 0.8 copy-done.6
  181.2 3.1 %shard_map.107 = bf16[128,3584]{1,0:T(8,128)(2,1)} custom-call(s32[8,128]{1,0:T(8,128)} %copy-done.14, bf16[64,3584]{1,0:T(8,128)(2,1)} %copy-done.5, bf16[64,3584]{1,0:T(8,128)(2,1)} %copy-done.6, bf16[32,128]{1,0:T(8,128)(2,1)} %copy-done.10, bf16[32,3584]{1,0:T(8,128)(2,1)} %router_ref.1), custom_call_target="tpu_custom_call" | custom-call | tf_op jit(solution)/shard_map/pallas_call | solution.py:218
  (25 shorter events, 0.1 us)
Async XLA Ops:
  4.3 14.5 %collective-permute-start = (bf16[64,3584]{1,0:T(8,128)(2,1)}, bf16[64,3584]{1,0:T(8,128)(2,1)}, u32[]{:S(2)}, u32[]{:S(2)}) collective-permute-start(bf16[64,3584]{1,0:T(8,128)(2,1)} %get-tuple-element.13), channel_id=1, source_target_pairs={{0,8},{1,9},{2,10},{3,11},{4,12},{5,13},{6,14},{7,15},{8,16},{9,17... | collective-permute-start | bytes 1376264 | tf_op jit(solution)/shard_map/ppermute | solution.py:146
  8.6 23.2 %collective-permute-start.4 = (bf16[64,3584]{1,0:T(8,128)(2,1)}, bf16[64,3584]{1,0:T(8,128)(2,1)S(1)}, u32[]{:S(2)}, u32[]{:S(2)}) collective-permute-start(bf16[64,3584]{1,0:T(8,128)(2,1)} %get-tuple-element.14), channel_id=1, source_target_pairs={{0,1016},{1,1017},{2,1018},{3,1019},{4,1020},{5,1021},{6,1022},{7,... | collective-permute-start | bytes 1376264 | tf_op jit(solution)/shard_map/ppermute | solution.py:146
  10.5 30.3 %collective-permute-start.7 = (bf16[64,3584]{1,0:T(8,128)(2,1)}, bf16[64,3584]{1,0:T(8,128)(2,1)S(1)}, u32[]{:S(2)}, u32[]{:S(2)}) collective-permute-start(bf16[64,3584]{1,0:T(8,128)(2,1)} %get-tuple-element.15), channel_id=1, source_target_pairs={{0,1016},{1,1017},{2,1018},{3,1019},{4,1020},{5,1021},{6,1022},{7,... | collective-permute-start | bytes 1376264 | tf_op jit(solution)/shard_map/ppermute | solution.py:146
  18.8 25.8 %all-to-all-start.2 = ((bf16[8,8,3584]{2,1,0:T(8,128)(2,1)}), bf16[8,8,3584]{2,1,0:T(8,128)(2,1)S(1)}, u32[]{:S(2)}, u32[]{:S(2)}) async-start(bf16[8,8,3584]{2,1,0:T(8,128)(2,1)} %bitcast.12), calls=%async_computation.2 | async-start | bytes 917504 | tf_op jit(solution)/shard_map/all_to_all | solution.py:167
  23.1 17.7 %collective-permute-start.2 = (s32[8,128]{1,0:T(8,128)}, s32[8,128]{1,0:T(8,128)S(1)}, u32[]{:S(2)}, u32[]{:S(2)}) collective-permute-start(s32[8,128]{1,0:T(8,128)} %get-tuple-element.11.meta_ref), channel_id=1, source_target_pairs={{0,1016},{1,1017},{2,1018},{3,1019},{4,1020},{5,1021},{6,1022},{7,... | collective-permute-start | bytes 12296 | tf_op jit(solution)/shard_map/ppermute | solution.py:146
  31.8 9.0 %copy-start.4 = (bf16[64,3584]{1,0:T(8,128)(2,1)}, bf16[64,3584]{1,0:T(8,128)(2,1)S(1)}, u32[]{:S(2)}) copy-start(bf16[64,3584]{1,0:T(8,128)(2,1)S(1)} %collective-permute-done.4.early_ref) | copy-start | bytes 1376260
  31.8 37.0 %collective-permute-start.5 = (bf16[64,3584]{1,0:T(8,128)(2,1)S(1)}, bf16[64,3584]{1,0:T(8,128)(2,1)S(1)}, u32[]{:S(2)}, u32[]{:S(2)}) collective-permute-start(bf16[64,3584]{1,0:T(8,128)(2,1)S(1)} %collective-permute-done.4.early_ref), channel_id=1, source_target_pairs={{0,1016},{1,1017},{2,1018},{3,1019},{4,1020},{5,1021},{6,1022},{7,... | collective-permute-start | bytes 1376264 | tf_op jit(solution)/shard_map/ppermute | solution.py:146
  40.8 0.6 copy-start.12
  41.4 0.8 copy-start.2
  44.6 17.9 %copy-start.13 = (s32[8,128]{1,0:T(8,128)S(1)}, s32[8,128]{1,0:T(8,128)}, u32[]{:S(2)}) copy-start(s32[8,128]{1,0:T(8,128)} %copy-done.12) | copy-start | bytes 12292
  44.6 21.5 %copy-start.3 = (bf16[64,3584]{1,0:T(8,128)(2,1)S(1)}, bf16[64,3584]{1,0:T(8,128)(2,1)}, u32[]{:S(2)}) copy-start(bf16[64,3584]{1,0:T(8,128)(2,1)} %copy-done.2) | copy-start | bytes 1376260
  44.6 14.6 %all-to-all-start.6 = ((bf16[8,8,3584]{2,1,0:T(8,128)(2,1)}), bf16[8,8,3584]{2,1,0:T(8,128)(2,1)S(1)}, u32[]{:S(2)}, u32[]{:S(2)}) async-start(bf16[8,8,3584]{2,1,0:T(8,128)(2,1)} %bitcast.67), calls=%async_computation.6 | async-start | bytes 917504 | tf_op jit(solution)/shard_map/all_to_all | solution.py:167
  59.2 13.1 %all-to-all-start.3 = ((bf16[8,8,1024]{2,1,0:T(8,128)(2,1)}), bf16[8,8,1024]{2,1,0:T(8,128)(2,1)S(1)}, u32[]{:S(2)}, u32[]{:S(2)}) async-start(bf16[8,8,1024]{2,1,0:T(8,128)(2,1)} %fusion.26), calls=%async_computation.3 | async-start | bytes 262144 | tf_op jit(solution)/shard_map/all_to_all | solution.py:167
  62.6 6.2 %collective-permute-start.3 = (s32[8,128]{1,0:T(8,128)S(1)}, s32[8,128]{1,0:T(8,128)S(1)}, u32[]{:S(2)}, u32[]{:S(2)}) collective-permute-start(s32[8,128]{1,0:T(8,128)S(1)} %copy-done.13), channel_id=1, source_target_pairs={{0,1016},{1,1017},{2,1018},{3,1019},{4,1020},{5,1021},{6,1022},{7,... | collective-permute-start | bytes 12296 | tf_op jit(solution)/shard_map/ppermute | solution.py:146
  66.1 42.3 %collective-permute-start.12 = (bf16[64,3584]{1,0:T(8,128)(2,1)S(1)}, bf16[64,3584]{1,0:T(8,128)(2,1)}, u32[]{:S(2)}, u32[]{:S(2)}) collective-permute-start(bf16[64,3584]{1,0:T(8,128)(2,1)S(1)} %copy-done.3), channel_id=1, source_target_pairs={{0,1016},{1,1017},{2,1018},{3,1019},{4,1020},{5,1021},{6,1022},{7,... | collective-permute-start | bytes 1376264 | tf_op jit(solution)/shard_map/ppermute | solution.py:146
  68.8 0.6 copy-start.15
  69.4 0.8 copy-start
  72.2 14.3 %all-to-all-start.4 = ((bf16[8,8,3584]{2,1,0:T(8,128)(2,1)}), bf16[8,8,3584]{2,1,0:T(8,128)(2,1)S(1)}, u32[]{:S(2)}, u32[]{:S(2)}) async-start(bf16[8,8,3584]{2,1,0:T(8,128)(2,1)} %bitcast.66), calls=%async_computation.4 | async-start | bytes 917504 | tf_op jit(solution)/shard_map/all_to_all | solution.py:167
  76.9 23.8 %copy-start.1 = (bf16[64,3584]{1,0:T(8,128)(2,1)S(1)}, bf16[64,3584]{1,0:T(8,128)(2,1)}, u32[]{:S(2)}) copy-start(bf16[64,3584]{1,0:T(8,128)(2,1)} %copy-done) | copy-start | bytes 1376260
  86.5 9.4 %all-to-all-start.7 = ((bf16[8,8,1024]{2,1,0:T(8,128)(2,1)}), bf16[8,8,1024]{2,1,0:T(8,128)(2,1)S(1)}, u32[]{:S(2)}, u32[]{:S(2)}) async-start(bf16[8,8,1024]{2,1,0:T(8,128)(2,1)} %fusion.20), calls=%async_computation.7 | async-start | bytes 262144 | tf_op jit(solution)/shard_map/all_to_all | solution.py:167
  89.9 80.3 %copy-start.11 = (s32[8,128]{1,0:T(8,128)S(1)}, s32[8,128]{1,0:T(8,128)}, u32[]{:S(2)}) copy-start(s32[8,128]{1,0:T(8,128)} %get-tuple-element.11.meta_ref) | copy-start | bytes 12292
  96.0 14.4 %all-to-all-start.5 = ((bf16[8,8,1024]{2,1,0:T(8,128)(2,1)}), bf16[8,8,1024]{2,1,0:T(8,128)(2,1)S(1)}, u32[]{:S(2)}, u32[]{:S(2)}) async-start(bf16[8,8,1024]{2,1,0:T(8,128)(2,1)} %fusion.23), calls=%async_computation.5 | async-start | bytes 262144 | tf_op jit(solution)/shard_map/all_to_all | solution.py:167
  100.7 23.2 %collective-permute-start.10 = (bf16[64,3584]{1,0:T(8,128)(2,1)S(1)}, bf16[64,3584]{1,0:T(8,128)(2,1)S(1)}, u32[]{:S(2)}, u32[]{:S(2)}) collective-permute-start(bf16[64,3584]{1,0:T(8,128)(2,1)S(1)} %copy-done.1), channel_id=1, source_target_pairs={{0,1016},{1,1017},{2,1018},{3,1019},{4,1020},{5,1021},{6,1022},{7,... | collective-permute-start | bytes 1376264 | tf_op jit(solution)/shard_map/ppermute | solution.py:146
  108.4 20.8 %collective-permute-start.13 = (bf16[64,3584]{1,0:T(8,128)(2,1)}, bf16[64,3584]{1,0:T(8,128)(2,1)S(1)}, u32[]{:S(2)}, u32[]{:S(2)}) collective-permute-start(bf16[64,3584]{1,0:T(8,128)(2,1)} %collective-permute-done.12), channel_id=1, source_target_pairs={{0,1016},{1,1017},{2,1018},{3,1019},{4,1020},{5,1021},{6,1022},{7,... | collective-permute-start | bytes 1376264 | tf_op jit(solution)/shard_map/ppermute | solution.py:146
  110.4 25.1 %all-to-all-start = ((bf16[8,8,3584]{2,1,0:T(8,128)(2,1)}), bf16[8,8,3584]{2,1,0:T(8,128)(2,1)S(1)}, u32[]{:S(2)}, u32[]{:S(2)}) async-start(bf16[8,8,3584]{2,1,0:T(8,128)(2,1)} %bitcast.7), calls=%async_computation | async-start | bytes 917504 | tf_op jit(solution)/shard_map/all_to_all | solution.py:167
  115.2 36.5 %collective-permute-start.1 = (bf16[64,1024]{1,0:T(8,128)(2,1)S(1)}, bf16[64,1024]{1,0:T(8,128)(2,1)S(1)}, u32[]{:S(2)}, u32[]{:S(2)}) collective-permute-start(bf16[64,1024]{1,0:T(8,128)(2,1)S(1)} %bitcast.72), channel_id=1, source_target_pairs={{0,120},{1,121},{2,122},{3,123},{4,124},{5,125},{6,126},{7,127},{8... | collective-permute-start | bytes 393224 | tf_op jit(solution)/shard_map/ppermute | solution.py:146
  122.0 29.6 %collective-permute-start.8 = (bf16[64,1024]{1,0:T(8,128)(2,1)S(1)}, bf16[64,1024]{1,0:T(8,128)(2,1)S(1)}, u32[]{:S(2)}, u32[]{:S(2)}) collective-permute-start(bf16[64,1024]{1,0:T(8,128)(2,1)S(1)} %bitcast.73), channel_id=1, source_target_pairs={{0,8},{1,9},{2,10},{3,11},{4,12},{5,13},{6,14},{7,15},{8,16},{9,17... | collective-permute-start | bytes 393224 | tf_op jit(solution)/shard_map/ppermute | solution.py:146
  123.9 55.7 %collective-permute-start.11 = (bf16[64,3584]{1,0:T(8,128)(2,1)S(1)}, bf16[64,3584]{1,0:T(8,128)(2,1)S(1)}, u32[]{:S(2)}, u32[]{:S(2)}) collective-permute-start(bf16[64,3584]{1,0:T(8,128)(2,1)S(1)} %collective-permute-done.10), channel_id=1, source_target_pairs={{8,0},{9,1},{10,2},{11,3},{12,4},{13,5},{14,6},{15,7},{16,8},{17,9... | collective-permute-start | bytes 1376264 | tf_op jit(solution)/shard_map/ppermute | solution.py:159
  129.2 50.4 %collective-permute-start.14 = (bf16[64,3584]{1,0:T(8,128)(2,1)S(1)}, bf16[64,3584]{1,0:T(8,128)(2,1)S(1)}, u32[]{:S(2)}, u32[]{:S(2)}) collective-permute-start(bf16[64,3584]{1,0:T(8,128)(2,1)S(1)} %collective-permute-done.13), channel_id=1, source_target_pairs={{8,0},{9,1},{10,2},{11,3},{12,4},{13,5},{14,6},{15,7},{16,8},{17,9... | collective-permute-start | bytes 1376264 | tf_op jit(solution)/shard_map/ppermute | solution.py:159
  133.5 18.2 %collective-permute-start.6 = (bf16[64,1024]{1,0:T(8,128)(2,1)S(1)}, bf16[64,1024]{1,0:T(8,128)(2,1)S(1)}, u32[]{:S(2)}, u32[]{:S(2)}) collective-permute-start(bf16[64,1024]{1,0:T(8,128)(2,1)S(1)} %bitcast.74), channel_id=1, source_target_pairs={{0,16},{1,17},{2,18},{3,19},{4,20},{5,21},{6,22},{7,23},{8,24},{9,... | collective-permute-start | bytes 393224 | tf_op jit(solution)/shard_map/ppermute | solution.py:146
  151.6 0.7 copy-start.7
  151.7 0.7 copy-start.8
  151.7 0.7 copy-start.9
  154.9 24.7 %collective-permute-start.15 = (bf16[32,128]{1,0:T(8,128)(2,1)}, bf16[32,128]{1,0:T(8,128)(2,1)S(1)}, u32[]{:S(2)}, u32[]{:S(2)}) collective-permute-start(bf16[32,128]{1,0:T(8,128)(2,1)} %get-tuple-element.18), channel_id=1, source_target_pairs={{32,0},{33,1},{34,2},{35,3},{36,4},{37,5},{38,6},{39,7},{40,8},{41... | collective-permute-start | bytes 24584 | tf_op jit(solution)/shard_map/ppermute | solution.py:163
  170.2 9.4 %collective-permute-start.9 = (s32[8,128]{1,0:T(8,128)S(1)}, s32[8,128]{1,0:T(8,128)S(1)}, u32[]{:S(2)}, u32[]{:S(2)}) collective-permute-start(s32[8,128]{1,0:T(8,128)S(1)} %copy-done.11), channel_id=1, source_target_pairs={{32,0},{33,1},{34,2},{35,3},{36,4},{37,5},{38,6},{39,7},{40,8},{41... | collective-permute-start | bytes 12296 | tf_op jit(solution)/shard_map/ppermute | solution.py:163
  179.6 0.6 copy-start.14
  179.6 0.6 copy-start.10
  179.6 0.8 copy-start.5
  180.4 0.8 copy-start.6

commit v2 on v1

v2 whole, which is shorter than its diff:
```python
import jax
import jax.numpy as jnp
from jax import lax
from jax.experimental import pallas as pl
from jax.experimental.pallas import tpu as pltpu
from jax.sharding import Mesh, PartitionSpec as P


route_scale = 2.5
slots = 8
axes = ("y", "zh", "zl", "x", "c")
group = ("x", "c")
expert_axes = ("zl", "x", "c")

NT = (((1,), (1,)), ((), ()))


def as_pick(mask):
    return mask.astype(jnp.float32).astype(jnp.bfloat16)


def column(row, count):
    return jnp.broadcast_to(row, (count, row.shape[1])).T[:, :1]


def prep_kernel(chosen_ref, places_ref, counts_ref, tok_ref, near_ref, up_ref, early_ref, late_ref, meta_ref):
    tokens, width = tok_ref.shape
    half = late_ref.shape[0]
    experts = counts_ref.shape[0]
    rows = near_ref.shape[0]
    own = lax.axis_index(expert_axes)
    own_z = lax.axis_index("zl")
    chosen = chosen_ref[...]
    places = places_ref[...]
    onehot = lax.broadcasted_iota(jnp.int32, (experts, tokens), 0) == chosen
    own_row = lax.broadcasted_iota(jnp.int32, counts_ref.shape, 0) == own
    own_counts = jnp.where(own_row, counts_ref[...], 0).astype(jnp.float32).astype(jnp.bfloat16)
    picked = jnp.dot(own_counts, as_pick(onehot), preferred_element_type=jnp.float32)
    limit = jnp.sum(picked, axis=0, keepdims=True)
    live = places.astype(jnp.float32) < limit
    offset = (lax.shift_right_logical(chosen, 3) - own_z) & 3
    dest = chosen & 7

    def slot_of(k, pitch, base):
        return jnp.where(live & (offset == k), dest * pitch + base + places, -1)

    order = lax.broadcasted_iota(jnp.int32, (1, tokens), 1)
    key = (jnp.where(live & (offset == 2), 0, tokens) + order).astype(jnp.float32)
    key_rows = jnp.broadcast_to(key, (tokens, tokens))
    rank = jnp.sum((key_rows.T < key_rows).astype(jnp.float32), axis=0, keepdims=True)
    perm = as_pick(lax.broadcasted_iota(jnp.int32, (tokens, tokens), 0) == rank.astype(jnp.int32))
    row_id = lax.broadcasted_iota(jnp.int32, (8, tokens), 0)
    one_down = slot_of(3, 2 * slots, 0).astype(jnp.float32)
    two_down = slot_of(2, 2 * slots, slots).astype(jnp.float32)
    pair = jnp.where(row_id == 0, one_down, jnp.where(row_id == 1, two_down, 0.0)).astype(jnp.bfloat16)
    moved = lax.dot_general(pair, perm, NT, preferred_element_type=jnp.float32)

    tok = tok_ref[...]
    ordered = jnp.dot(perm, tok, preferred_element_type=jnp.float32).astype(jnp.bfloat16)
    early_ref[:half] = ordered[:half]
    early_ref[half:] = jnp.zeros((8, width), jnp.bfloat16)
    table = jnp.where(row_id < 2, moved, jnp.where(row_id == 2, rank, 0.0)).astype(jnp.bfloat16)
    early_ref[half:, :tokens] = table
    late_ref[...] = ordered[half:]
    slot_id = lax.broadcasted_iota(jnp.int32, (rows, tokens), 0)
    up_ref[...] = jnp.dot(as_pick(slot_id == slot_of(1, slots, 0)), tok, preferred_element_type=jnp.float32).astype(jnp.bfloat16)
    near_ref[...] = jnp.dot(as_pick(slot_id == slot_of(0, slots, 0)), tok, preferred_element_type=jnp.float32).astype(jnp.bfloat16)
    back = jnp.where(row_id == 0, slot_of(0, 2 * slots, 0), -1)
    for k in (1, 2, 3):
        back = jnp.where(row_id == k, slot_of(k, slots, 0), back)
    meta_ref[...] = back


def pack_kernel(early1_ref, late1_ref, early2_ref, out_ref):
    rows = out_ref.shape[0]
    half, _ = late1_ref.shape
    tokens = 2 * half
    row = lax.broadcasted_iota(jnp.int32, (rows, tokens), 0)
    one = early1_ref[half:, :tokens].astype(jnp.float32)[0:1, :].astype(jnp.int32)
    two = early2_ref[half:, :tokens].astype(jnp.float32)[1:2, :].astype(jnp.int32)
    pick_one = as_pick(row == one)
    pick_two = as_pick(row == two)
    out = jnp.dot(pick_one[:, :half], early1_ref[:half], preferred_element_type=jnp.float32)
    out = out + jnp.dot(pick_one[:, half:], late1_ref[...], preferred_element_type=jnp.float32)
    out = out + jnp.dot(pick_two[:, :half], early2_ref[:half], preferred_element_type=jnp.float32)
    out_ref[...] = out.astype(jnp.bfloat16)


def back_kernel(meta_ref, chosen_ref, scores_ref, hidden_ref, r0_ref, r1_ref, r2_ref, r3_ref, act_ref, score_ref, score_bf_ref):
    tokens = hidden_ref.shape[0]
    experts = scores_ref.shape[0]
    own_back = jnp.zeros(hidden_ref.shape, jnp.float32)
    for k, ref in enumerate((r0_ref, r1_ref, r2_ref, r3_ref)):
        target = column(meta_ref[k:k + 1, :].astype(jnp.float32), tokens).astype(jnp.int32)
        pick = as_pick(lax.broadcasted_iota(jnp.int32, (tokens, ref.shape[0]), 1) == target)
        own_back = own_back + jnp.dot(pick, ref[...], preferred_element_type=jnp.float32)
    onehot = lax.broadcasted_iota(jnp.int32, (experts, tokens), 0) == chosen_ref[...]
    logit = jnp.sum(jnp.where(onehot, scores_ref[...], 0.0), axis=0, keepdims=True)
    sigmoid_vals = jax.nn.sigmoid(logit)
    gate = (route_scale * sigmoid_vals).astype(jnp.bfloat16).astype(jnp.float32)
    act_ref[...] = (column(gate, tokens) * own_back).astype(jnp.bfloat16)
    route = jnp.sum(hidden_ref[...].astype(jnp.float32) * own_back, axis=1, keepdims=True)
    route_row = jnp.broadcast_to(route, (tokens, tokens)).T[:1, :]
    slope = route_row * route_scale * sigmoid_vals * (1.0 - sigmoid_vals)
    score = jnp.where(onehot, slope, 0.0)
    score_ref[...] = score
    score_bf_ref[...] = score.astype(jnp.bfloat16)


def up_kernel(early_ref, late_ref, score_ref, router_ref, out_ref):
    half = late_ref.shape[0]
    tokens = 2 * half
    rank = column(early_ref[half:, :tokens].astype(jnp.float32)[2:3, :], tokens).astype(jnp.int32)
    pick = as_pick(lax.broadcasted_iota(jnp.int32, (tokens, tokens), 1) == rank)
    scores = score_ref[...].astype(jnp.float32).T.astype(jnp.bfloat16)
    out = jnp.dot(pick[:, :half], early_ref[:half], preferred_element_type=jnp.float32)
    out = out + jnp.dot(pick[:, half:], late_ref[...], preferred_element_type=jnp.float32)
    out = out + jnp.dot(scores, router_ref[...], preferred_element_type=jnp.float32)
    out_ref[...] = out.astype(jnp.bfloat16)


def whole(count):
    return [pl.BlockSpec(memory_space=pltpu.VMEM)] * count


def sds(shape, dtype=jnp.bfloat16):
    return jax.ShapeDtypeStruct(shape, dtype)


def on_device(dims, grad_out, hidden_act, scores, expert_ids, slot_ids, counts, down_weight, router):
    ny, nz, nzl, nxc = dims
    tok = grad_out[0]
    tokens, width = tok.shape
    hidden_width = hidden_act.shape[2]
    half = tokens // 2
    rows = nxc * slots
    places = ny * nz
    weight = down_weight[0]

    def lanes(pairs):
        return [(a * nxc + j, b * nxc + j) for a, b in pairs for j in range(nxc)]

    def along_z(value, distance):
        pairs = [(y * nz + z, y * nz + (z + distance) % nz) for y in range(ny) for z in range(nz)]
        return lax.ppermute(value, axes, lanes(pairs))

    def along_path(value, distance):
        return lax.ppermute(value, axes, lanes([(a, (a + distance) % places) for a in range(places)]))

    def to_end(value, left):
        pairs = [(a, (a - left) % places) for a in range(places) if (a + nzl - left) % places >= nzl]
        return lax.ppermute(value, axes, lanes(pairs))

    def exchange(value):
        return lax.all_to_all(value, group, split_axis=0, concat_axis=0, tiled=True)

    def serve(value):
        flat = value.reshape(nxc * 2 * slots, width)
        out = lax.dot_general(flat, weight, NT, preferred_element_type=jnp.float32).astype(jnp.bfloat16)
        return out.reshape(nxc, 2 * slots, hidden_width)

    def cut(value, k):
        return value[:, k * slots:(k + 1) * slots].reshape(rows, hidden_width)

    near, up, early, late, meta = pl.pallas_call(
        prep_kernel,
        out_shape=(sds((rows, width)), sds((rows, width)), sds((half + 8, width)), sds((half, width)), sds((8, tokens), jnp.int32)),
        in_specs=whole(4),
        out_specs=tuple(whole(5)),
    )(expert_ids, slot_ids, counts[0], tok)
    early1 = along_path(early, -1)
    up_got = along_z(up, 1)
    late1 = along_path(late, -1)
    early2 = along_path(early1, -1)
    first = jnp.concatenate([near.reshape(nxc, slots, width), up_got.reshape(nxc, slots, width)], axis=1)
    first = exchange(first)
    late4 = to_end(late1, 3)
    second = pl.pallas_call(
        pack_kernel, out_shape=sds((2 * rows, width)), in_specs=whole(3), out_specs=whole(1)[0]
    )(early1, late1, early2)
    second = exchange(second.reshape(nxc, 2 * slots, width))
    early4 = to_end(early2, 2)
    first_back = serve(first)
    first_got = exchange(first_back)
    second_back = serve(second)
    second_got = exchange(second_back)
    r1 = cut(first_got, 1)
    r1 = along_z(r1, -1)
    r3 = cut(second_got, 0)
    r2 = cut(second_got, 1)
    r2 = along_path(r2, 2)
    r3 = along_path(r3, 1)
    act, score, score_bf = pl.pallas_call(
        back_kernel,
        out_shape=(sds((tokens, hidden_width)), sds((scores.shape[2], tokens), jnp.float32), sds((scores.shape[2], tokens))),
        in_specs=whole(8),
        out_specs=tuple(whole(3)),
    )(meta, expert_ids, scores[0].T, hidden_act[0], first_got.reshape(2 * rows, hidden_width), r1, r2, r3)
    late_score = to_end(score_bf, nzl)
    upstream = pl.pallas_call(
        up_kernel, out_shape=sds((tokens, width)), in_specs=whole(4), out_specs=whole(1)[0]
    )(early4, late4, late_score, router)
    return act[None], score.T[None], upstream[None]


def solution(mesh):
    cut_mesh = Mesh(mesh.devices.reshape(8, 4, 4, 4, 2), axes)
    dims = (8, 16, 4, 8)
    section = ("y", "zh")
    rows = P(section, expert_axes, None)
    in_specs = (rows, rows, rows, P(section, expert_axes), P(section, expert_axes), P(section, None, None), P(expert_axes, None, None), P())

    def body(*arrays):
        return on_device(dims, *arrays)

    return jax.shard_map(body, mesh=cut_mesh, in_specs=in_specs, out_specs=(rows, rows, rows), check_vma=False)
```

time: 186 us -> 154 us (0.83)
  the two profiles are of different devices: /device:TPU:160 before, /device:TPU:50 now
where the time goes in v2:
time: 154 us; the launch traced here: 153 us
  starting transfers between devices  68.5 us (44%)
  waiting for transfers between devices  53.9 us (35%)
  matrix products  12.4 us (8%)
  Pallas kernels  12.1 us (8%)
  local copies, waits for them, and re-layouts  2.93 us (2%)
  other arithmetic  2 us (1%)
    ppermute x5, starting transfers between devices, along_path(): lax.ppermute(value, axes, lanes([(a, (a + distance) % places) for a in ra...  28.9 us
    ppermute x2, waiting for transfers between devices, along_z(): return lax.ppermute(value, axes, lanes(pairs))  26.4 us
    all_to_all x4, starting transfers between devices, exchange(): return lax.all_to_all(value, group, split_axis=0, concat_axis=0, tiled=True)  19.2 us
    ppermute x5, waiting for transfers between devices, along_path(): lax.ppermute(value, axes, lanes([(a, (a + distance) % places) for a in ra...  18.7 us
    ppermute x3, starting transfers between devices, to_end(): return lax.ppermute(value, axes, lanes(pairs))  12.8 us
    dot_general x2, matrix products, serve(): lax.dot_general(flat, weight, NT, preferred_element_type=jnp.float32)  12.4 us
    ppermute x2, starting transfers between devices, along_z(): return lax.ppermute(value, axes, lanes(pairs))  7.58 us
    ppermute x3, waiting for transfers between devices, to_end(): return lax.ppermute(value, axes, lanes(pairs))  5.97 us
  transfers between devices with their start and end apart: 14, of which 5 were waited for; matrix products, arithmetic and copies ran while one was open for 9% of the time, Pallas kernels for 4%

profile of v2, /device:TPU:50, one launch (start us, length us, event | category | flops | bytes accessed | tf_op | source)
XLA Modules:
  0.0 152.6 jit_solution(12158029222150775747)
XLA Ops:
  0.6 3.1 %shard_map.103 = (bf16[64,3584]{1,0:T(8,128)(2,1)}, bf16[64,3584]{1,0:T(8,128)(2,1)}, bf16[72,3584]{1,0:T(8,128)(2,1)}, bf16[64,3584]{1,0:T(8,128)(2,1)}, s32[8,128]{1,0:T(8,128)}) custom-call(s32[1,128]{1,0:T(1,128)} %chosen_ref.3, s32[1,128]{1,0:T(1,128)} %places_ref.1, s32[32,32]{1,0:T(8,128)} %bitcast.45, bf16[128,3584]{1,0:T(8,128)(2,1)} %bitcast.40), custom_call_target="tpu_custom_call" | custom-call | tf_op jit(solution)/shard_map/pallas_call | solution.py:165
  3.8 4.3 %collective-permute-start = (bf16[64,3584]{1,0:T(8,128)(2,1)}, bf16[64,3584]{1,0:T(8,128)(2,1)S(1)}, u32[]{:S(2)}, u32[]{:S(2)}) collective-permute-start(bf16[64,3584]{1,0:T(8,128)(2,1)} %get-tuple-element.13), channel_id=1, source_target_pairs={{0,8},{1,9},{2,10},{3,11},{4,12},{5,13},{6,14},{7,15},{8,16},{9,17... | collective-permute-start | bytes 1376264 | tf_op jit(solution)/shard_map/ppermute | solution.py:145
  8.0 16.6 %collective-permute-start.2 = (bf16[72,3584]{1,0:T(8,128)(2,1)}, bf16[72,3584]{1,0:T(8,128)(2,1)S(1)}, u32[]{:S(2)}, u32[]{:S(2)}) collective-permute-start(bf16[72,3584]{1,0:T(8,128)(2,1)} %get-tuple-element.14), channel_id=1, source_target_pairs={{0,1016},{1,1017},{2,1018},{3,1019},{4,1020},{5,1021},{6,1022},{7,... | collective-permute-start | bytes 1548296 | tf_op jit(solution)/shard_map/ppermute | solution.py:148
  24.7 8.0 %collective-permute-done = bf16[64,3584]{1,0:T(8,128)(2,1)S(1)} collective-permute-done((bf16[64,3584]{1,0:T(8,128)(2,1)}, bf16[64,3584]{1,0:T(8,128)(2,1)S(1)}, u32[]{:S(2)}, u32[]{:S(2)}) %collective-permute-start) | collective-permute-done | bytes 458784 | tf_op jit(solution)/shard_map/ppermute | solution.py:145
  32.7 2.0 %pad_maximum_fusion = bf16[8,16,3584]{2,1,0:T(8,128)(2,1)} fusion(bf16[8,8,3584]{2,1,0:T(8,128)(2,1)S(1)} %bitcast.43, bf16[8,8,3584]{2,1,0:T(8,128)(2,1)} %bitcast.42), kind=kLoop, calls=%fused_computation.6 | loop fusion | flops 1835008 | bytes 1835008 | tf_op jit(solution)/shard_map/concatenate | solution.py:175
  34.7 4.8 %all-to-all-start = ((bf16[8,16,3584]{2,1,0:T(8,128)(2,1)}), bf16[8,16,3584]{2,1,0:T(8,128)(2,1)S(1)}, u32[]{:S(2)}, u32[]{:S(2)}) async-start(bf16[8,16,3584]{2,1,0:T(8,128)(2,1)} %pad_maximum_fusion), calls=%async_computation | async-start | bytes 1835008 | tf_op jit(solution)/shard_map/all_to_all | solution.py:155
  39.5 0.0 collective-permute-done.2.early1_ref
  39.5 0.0 copy-start.2
  39.5 4.4 %collective-permute-start.4 = (bf16[72,3584]{1,0:T(8,128)(2,1)S(1)}, bf16[72,3584]{1,0:T(8,128)(2,1)S(1)}, u32[]{:S(2)}, u32[]{:S(2)}) collective-permute-start(bf16[72,3584]{1,0:T(8,128)(2,1)S(1)} %collective-permute-done.2.early1_ref), channel_id=1, source_target_pairs={{0,1016},{1,1017},{2,1018},{3,1019},{4,1020},{5,1021},{6,1022},{7,... | collective-permute-start | bytes 1548296 | tf_op jit(solution)/shard_map/ppermute | solution.py:148
  44.0 2.5 %collective-permute-start.3 = (bf16[64,3584]{1,0:T(8,128)(2,1)}, bf16[64,3584]{1,0:T(8,128)(2,1)S(1)}, u32[]{:S(2)}, u32[]{:S(2)}) collective-permute-start(bf16[64,3584]{1,0:T(8,128)(2,1)} %get-tuple-element.15), channel_id=1, source_target_pairs={{0,1016},{1,1017},{2,1018},{3,1019},{4,1020},{5,1021},{6,1022},{7,... | collective-permute-start | bytes 1376264 | tf_op jit(solution)/shard_map/ppermute | solution.py:148
  46.4 18.7 %collective-permute-done.3.late1_ref = bf16[64,3584]{1,0:T(8,128)(2,1)S(1)} collective-permute-done((bf16[64,3584]{1,0:T(8,128)(2,1)}, bf16[64,3584]{1,0:T(8,128)(2,1)S(1)}, u32[]{:S(2)}, u32[]{:S(2)}) %collective-permute-start.3) | collective-permute-done | bytes 458784 | tf_op jit(solution)/shard_map/ppermute | solution.py:148
  65.2 0.0 copy-start.4
  65.2 0.0 collective-permute-done.4.early2_ref
  65.2 0.0 copy-done.2
  65.2 0.8 copy-done.4
  66.0 0.0 copy-start.1
  66.0 0.8 copy-done.1
  66.7 3.2 %shard_map.104 = bf16[128,3584]{1,0:T(8,128)(2,1)} custom-call(bf16[72,3584]{1,0:T(8,128)(2,1)} %copy-done.2, bf16[64,3584]{1,0:T(8,128)(2,1)} %copy-done.4, bf16[72,3584]{1,0:T(8,128)(2,1)} %copy-done.1), custom_call_target="tpu_custom_call" | custom-call | tf_op jit(solution)/shard_map/pallas_call | solution.py:178
  69.9 0.0 all-to-all-done
  70.0 4.8 %all-to-all-start.2 = ((bf16[8,16,3584]{2,1,0:T(8,128)(2,1)}), bf16[8,16,3584]{2,1,0:T(8,128)(2,1)S(1)}, u32[]{:S(2)}, u32[]{:S(2)}) async-start(bf16[8,16,3584]{2,1,0:T(8,128)(2,1)} %bitcast.38), calls=%async_computation.2 | async-start | bytes 1835008 | tf_op jit(solution)/shard_map/all_to_all | solution.py:155
  74.8 4.3 %collective-permute-start.8 = (bf16[64,3584]{1,0:T(8,128)(2,1)}, bf16[64,3584]{1,0:T(8,128)(2,1)S(1)}, u32[]{:S(2)}, u32[]{:S(2)}) collective-permute-start(bf16[64,3584]{1,0:T(8,128)(2,1)} %copy-done.4), channel_id=1, source_target_pairs={{24,0},{25,1},{26,2},{27,3},{28,4},{29,5},{30,6},{31,7},{32,8},{33... | collective-permute-start | bytes 1376264 | tf_op jit(solution)/shard_map/ppermute | solution.py:152
  79.0 4.9 %collective-permute-start.7 = (bf16[72,3584]{1,0:T(8,128)(2,1)}, bf16[72,3584]{1,0:T(8,128)(2,1)S(1)}, u32[]{:S(2)}, u32[]{:S(2)}) collective-permute-start(bf16[72,3584]{1,0:T(8,128)(2,1)} %copy-done.1), channel_id=1, source_target_pairs={{16,0},{17,1},{18,2},{19,3},{20,4},{21,5},{22,6},{23,7},{24,8},{25... | collective-permute-start | bytes 1548296 | tf_op jit(solution)/shard_map/ppermute | solution.py:152
  83.9 6.2 %fusion.4 = bf16[128,1024]{1,0:T(8,128)(2,1)} fusion(bf16[128,3584]{1,0:T(8,128)(2,1)S(1)} %bitcast.36, bf16[1,1024,3584]{2,1,0:T(8,128)(2,1)} %param.14), kind=kOutput, calls=%fused_computation.4 | convolution fusion | flops 939655168 | bytes 8519680 | tf_op jit(solution)/shard_map/dot_general | solution.py:159
  90.1 0.0 all-to-all-done.2
  90.1 4.8 %all-to-all-start.1 = ((bf16[8,16,1024]{2,1,0:T(8,128)(2,1)}), bf16[8,16,1024]{2,1,0:T(8,128)(2,1)S(1)}, u32[]{:S(2)}, u32[]{:S(2)}) async-start(bf16[8,16,1024]{2,1,0:T(8,128)(2,1)} %bitcast.9), calls=%async_computation.1 | async-start | bytes 524288 | tf_op jit(solution)/shard_map/all_to_all | solution.py:155
  94.9 6.2 %fusion.7 = bf16[128,1024]{1,0:T(8,128)(2,1)} fusion(bf16[128,3584]{1,0:T(8,128)(2,1)S(1)} %bitcast.37, bf16[1,1024,3584]{2,1,0:T(8,128)(2,1)} %param.14), kind=kOutput, calls=%fused_computation.5 | convolution fusion | flops 939655168 | bytes 8519680 | tf_op jit(solution)/shard_map/dot_general | solution.py:159
  101.1 0.0 all-to-all-done.1
  101.1 0.0 copy-start
  101.1 4.8 %all-to-all-start.3 = ((bf16[8,16,1024]{2,1,0:T(8,128)(2,1)}), bf16[8,16,1024]{2,1,0:T(8,128)(2,1)S(1)}, u32[]{:S(2)}, u32[]{:S(2)}) async-start(bf16[8,16,1024]{2,1,0:T(8,128)(2,1)} %bitcast.14), calls=%async_computation.3 | async-start | bytes 524288 | tf_op jit(solution)/shard_map/all_to_all | solution.py:155
  106.0 3.3 %collective-permute-start.1 = (bf16[64,1024]{1,0:T(8,128)(2,1)S(1)}, bf16[64,1024]{1,0:T(8,128)(2,1)S(1)}, u32[]{:S(2)}, u32[]{:S(2)}) collective-permute-start(bf16[64,1024]{1,0:T(8,128)(2,1)S(1)} %slice_bitcast_fusion.2), channel_id=1, source_target_pairs={{0,120},{1,121},{2,122},{3,123},{4,124},{5,125},{6,126},{7,127},{8... | collective-permute-start | bytes 393224 | tf_op jit(solution)/shard_map/ppermute | solution.py:145
  109.3 2.7 %all-to-all-done.3 = bf16[8,16,1024]{2,1,0:T(8,128)(2,1)S(1)} async-done(((bf16[8,16,1024]{2,1,0:T(8,128)(2,1)}), bf16[8,16,1024]{2,1,0:T(8,128)(2,1)S(1)}, u32[]{:S(2)}, u32[]{:S(2)}) %all-to-all-start.3) | async-done | bytes 262176 | tf_op jit(solution)/shard_map/all_to_all | solution.py:155
  112.0 3.4 %collective-permute-start.5 = (bf16[64,1024]{1,0:T(8,128)(2,1)S(1)}, bf16[64,1024]{1,0:T(8,128)(2,1)S(1)}, u32[]{:S(2)}, u32[]{:S(2)}) collective-permute-start(bf16[64,1024]{1,0:T(8,128)(2,1)S(1)} %get-tuple-element.20), channel_id=1, source_target_pairs={{0,16},{1,17},{2,18},{3,19},{4,20},{5,21},{6,22},{7,23},{8,24},{9,... | collective-permute-start | bytes 393224 | tf_op jit(solution)/shard_map/ppermute | solution.py:148
  115.5 1.9 %collective-permute-start.6 = (bf16[64,1024]{1,0:T(8,128)(2,1)S(1)}, bf16[64,1024]{1,0:T(8,128)(2,1)S(1)}, u32[]{:S(2)}, u32[]{:S(2)}) collective-permute-start(bf16[64,1024]{1,0:T(8,128)(2,1)S(1)} %get-tuple-element.19), channel_id=1, source_target_pairs={{0,8},{1,9},{2,10},{3,11},{4,12},{5,13},{6,14},{7,15},{8,16},{9,17... | collective-permute-start | bytes 393224 | tf_op jit(solution)/shard_map/ppermute | solution.py:148
  117.4 18.4 %collective-permute-done.1.r1_ref = bf16[64,1024]{1,0:T(8,128)(2,1)S(1)} collective-permute-done((bf16[64,1024]{1,0:T(8,128)(2,1)S(1)}, bf16[64,1024]{1,0:T(8,128)(2,1)S(1)}, u32[]{:S(2)}, u32[]{:S(2)}) %collective-permute-start.1) | collective-permute-done | bytes 131104 | tf_op jit(solution)/shard_map/ppermute | solution.py:145
  135.9 0.0 copy-start.6
  135.9 0.0 collective-permute-done.5.r2_ref
  135.9 0.0 copy-start.7
  135.9 0.0 collective-permute-done.6.r3_ref
  135.9 0.0 copy-start.8
  135.9 0.0 copy-done
  135.9 0.6 copy-done.6
  136.5 0.0 copy-done.7
  136.6 0.1 copy-done.8
  136.6 2.6 %shard_map.105 = (bf16[128,1024]{1,0:T(8,128)(2,1)}, f32[32,128]{1,0:T(8,128)}, bf16[32,128]{1,0:T(8,128)(2,1)}) custom-call(s32[8,128]{1,0:T(8,128)} %get-tuple-element.11.meta_ref, s32[1,128]{1,0:T(1,128)} %chosen_ref.3, f32[32,128]{1,0:T(8,128)} %bitcast.46, bf16[128,1024]{1,0:T(8,128)(2,1)} %bitcast.44, bf16[128,1024]{1,0:T(8,128)(2,1)} %bitcast.39, ...), custom_call_target="tpu_custom_call" | custom-call | tf_op jit(solution)/shard_map/pallas_call | solution.py:193
  139.2 3.6 %collective-permute-start.9 = (bf16[32,128]{1,0:T(8,128)(2,1)}, bf16[32,128]{1,0:T(8,128)(2,1)S(1)}, u32[]{:S(2)}, u32[]{:S(2)}) collective-permute-start(bf16[32,128]{1,0:T(8,128)(2,1)} %get-tuple-element.18), channel_id=1, source_target_pairs={{32,0},{33,1},{34,2},{35,3},{36,4},{37,5},{38,6},{39,7},{40,8},{41... | collective-permute-start | bytes 24584 | tf_op jit(solution)/shard_map/ppermute | solution.py:152
  142.8 0.0 collective-permute-done.8.late_ref
  142.8 0.0 copy-start.5
  142.8 0.0 collective-permute-done.7.early_ref
  142.9 0.0 copy-start.3
  142.9 6.0 %collective-permute-done.9.score_ref = bf16[32,128]{1,0:T(8,128)(2,1)S(1)} collective-permute-done((bf16[32,128]{1,0:T(8,128)(2,1)}, bf16[32,128]{1,0:T(8,128)(2,1)S(1)}, u32[]{:S(2)}, u32[]{:S(2)}) %collective-permute-start.9) | collective-permute-done | bytes 8224 | tf_op jit(solution)/shard_map/ppermute | solution.py:152
  148.8 0.0 copy-done.5
  148.8 0.0 copy-done.3
  148.8 0.0 copy-start.9
  148.8 0.6 copy-done.9
  149.4 3.2 %shard_map.106 = bf16[128,3584]{1,0:T(8,128)(2,1)} custom-call(bf16[72,3584]{1,0:T(8,128)(2,1)} %copy-done.3, bf16[64,3584]{1,0:T(8,128)(2,1)} %copy-done.5, bf16[32,128]{1,0:T(8,128)(2,1)} %copy-done.9, bf16[32,3584]{1,0:T(8,128)(2,1)} %router_ref.1), custom_call_target="tpu_custom_call" | custom-call | tf_op jit(solution)/shard_map/pallas_call | solution.py:200
  (2 shorter events, 0.0 us)
Async XLA Ops:
  3.8 28.9 %collective-permute-start = (bf16[64,3584]{1,0:T(8,128)(2,1)}, bf16[64,3584]{1,0:T(8,128)(2,1)S(1)}, u32[]{:S(2)}, u32[]{:S(2)}) collective-permute-start(bf16[64,3584]{1,0:T(8,128)(2,1)} %get-tuple-element.13), channel_id=1, source_target_pairs={{0,8},{1,9},{2,10},{3,11},{4,12},{5,13},{6,14},{7,15},{8,16},{9,17... | collective-permute-start | bytes 1376264 | tf_op jit(solution)/shard_map/ppermute | solution.py:145
  8.0 31.5 %collective-permute-start.2 = (bf16[72,3584]{1,0:T(8,128)(2,1)}, bf16[72,3584]{1,0:T(8,128)(2,1)S(1)}, u32[]{:S(2)}, u32[]{:S(2)}) collective-permute-start(bf16[72,3584]{1,0:T(8,128)(2,1)} %get-tuple-element.14), channel_id=1, source_target_pairs={{0,1016},{1,1017},{2,1018},{3,1019},{4,1020},{5,1021},{6,1022},{7,... | collective-permute-start | bytes 1548296 | tf_op jit(solution)/shard_map/ppermute | solution.py:148
  34.7 35.3 %all-to-all-start = ((bf16[8,16,3584]{2,1,0:T(8,128)(2,1)}), bf16[8,16,3584]{2,1,0:T(8,128)(2,1)S(1)}, u32[]{:S(2)}, u32[]{:S(2)}) async-start(bf16[8,16,3584]{2,1,0:T(8,128)(2,1)} %pad_maximum_fusion), calls=%async_computation | async-start | bytes 1835008 | tf_op jit(solution)/shard_map/all_to_all | solution.py:155
  39.5 25.7 %copy-start.2 = (bf16[72,3584]{1,0:T(8,128)(2,1)}, bf16[72,3584]{1,0:T(8,128)(2,1)S(1)}, u32[]{:S(2)}) copy-start(bf16[72,3584]{1,0:T(8,128)(2,1)S(1)} %collective-permute-done.2.early1_ref) | copy-start | bytes 1548292
  39.5 25.6 %collective-permute-start.4 = (bf16[72,3584]{1,0:T(8,128)(2,1)S(1)}, bf16[72,3584]{1,0:T(8,128)(2,1)S(1)}, u32[]{:S(2)}, u32[]{:S(2)}) collective-permute-start(bf16[72,3584]{1,0:T(8,128)(2,1)S(1)} %collective-permute-done.2.early1_ref), channel_id=1, source_target_pairs={{0,1016},{1,1017},{2,1018},{3,1019},{4,1020},{5,1021},{6,1022},{7,... | collective-permute-start | bytes 1548296 | tf_op jit(solution)/shard_map/ppermute | solution.py:148
  44.0 21.2 %collective-permute-start.3 = (bf16[64,3584]{1,0:T(8,128)(2,1)}, bf16[64,3584]{1,0:T(8,128)(2,1)S(1)}, u32[]{:S(2)}, u32[]{:S(2)}) collective-permute-start(bf16[64,3584]{1,0:T(8,128)(2,1)} %get-tuple-element.15), channel_id=1, source_target_pairs={{0,1016},{1,1017},{2,1018},{3,1019},{4,1020},{5,1021},{6,1022},{7,... | collective-permute-start | bytes 1376264 | tf_op jit(solution)/shard_map/ppermute | solution.py:148
  65.2 0.8 copy-start.4
  66.0 0.8 copy-start.1
  70.0 20.2 %all-to-all-start.2 = ((bf16[8,16,3584]{2,1,0:T(8,128)(2,1)}), bf16[8,16,3584]{2,1,0:T(8,128)(2,1)S(1)}, u32[]{:S(2)}, u32[]{:S(2)}) async-start(bf16[8,16,3584]{2,1,0:T(8,128)(2,1)} %bitcast.38), calls=%async_computation.2 | async-start | bytes 1835008 | tf_op jit(solution)/shard_map/all_to_all | solution.py:155
  74.8 68.1 %collective-permute-start.8 = (bf16[64,3584]{1,0:T(8,128)(2,1)}, bf16[64,3584]{1,0:T(8,128)(2,1)S(1)}, u32[]{:S(2)}, u32[]{:S(2)}) collective-permute-start(bf16[64,3584]{1,0:T(8,128)(2,1)} %copy-done.4), channel_id=1, source_target_pairs={{24,0},{25,1},{26,2},{27,3},{28,4},{29,5},{30,6},{31,7},{32,8},{33... | collective-permute-start | bytes 1376264 | tf_op jit(solution)/shard_map/ppermute | solution.py:152
  79.0 63.8 %collective-permute-start.7 = (bf16[72,3584]{1,0:T(8,128)(2,1)}, bf16[72,3584]{1,0:T(8,128)(2,1)S(1)}, u32[]{:S(2)}, u32[]{:S(2)}) collective-permute-start(bf16[72,3584]{1,0:T(8,128)(2,1)} %copy-done.1), channel_id=1, source_target_pairs={{16,0},{17,1},{18,2},{19,3},{20,4},{21,5},{22,6},{23,7},{24,8},{25... | collective-permute-start | bytes 1548296 | tf_op jit(solution)/shard_map/ppermute | solution.py:152
  90.1 11.0 %all-to-all-start.1 = ((bf16[8,16,1024]{2,1,0:T(8,128)(2,1)}), bf16[8,16,1024]{2,1,0:T(8,128)(2,1)S(1)}, u32[]{:S(2)}, u32[]{:S(2)}) async-start(bf16[8,16,1024]{2,1,0:T(8,128)(2,1)} %bitcast.9), calls=%async_computation.1 | async-start | bytes 524288 | tf_op jit(solution)/shard_map/all_to_all | solution.py:155
  101.1 34.7 %copy-start = (bf16[8,16,1024]{2,1,0:T(8,128)(2,1)}, bf16[8,16,1024]{2,1,0:T(8,128)(2,1)S(1)}, u32[]{:S(2)}) copy-start(bf16[8,16,1024]{2,1,0:T(8,128)(2,1)S(1)} %all-to-all-done.1) | copy-start | bytes 786436
  101.1 10.9 %all-to-all-start.3 = ((bf16[8,16,1024]{2,1,0:T(8,128)(2,1)}), bf16[8,16,1024]{2,1,0:T(8,128)(2,1)S(1)}, u32[]{:S(2)}, u32[]{:S(2)}) async-start(bf16[8,16,1024]{2,1,0:T(8,128)(2,1)} %bitcast.14), calls=%async_computation.3 | async-start | bytes 524288 | tf_op jit(solution)/shard_map/all_to_all | solution.py:155
  106.0 29.9 %collective-permute-start.1 = (bf16[64,1024]{1,0:T(8,128)(2,1)S(1)}, bf16[64,1024]{1,0:T(8,128)(2,1)S(1)}, u32[]{:S(2)}, u32[]{:S(2)}) collective-permute-start(bf16[64,1024]{1,0:T(8,128)(2,1)S(1)} %slice_bitcast_fusion.2), channel_id=1, source_target_pairs={{0,120},{1,121},{2,122},{3,123},{4,124},{5,125},{6,126},{7,127},{8... | collective-permute-start | bytes 393224 | tf_op jit(solution)/shard_map/ppermute | solution.py:145
  112.0 23.8 %collective-permute-start.5 = (bf16[64,1024]{1,0:T(8,128)(2,1)S(1)}, bf16[64,1024]{1,0:T(8,128)(2,1)S(1)}, u32[]{:S(2)}, u32[]{:S(2)}) collective-permute-start(bf16[64,1024]{1,0:T(8,128)(2,1)S(1)} %get-tuple-element.20), channel_id=1, source_target_pairs={{0,16},{1,17},{2,18},{3,19},{4,20},{5,21},{6,22},{7,23},{8,24},{9,... | collective-permute-start | bytes 393224 | tf_op jit(solution)/shard_map/ppermute | solution.py:148
  115.5 20.4 %collective-permute-start.6 = (bf16[64,1024]{1,0:T(8,128)(2,1)S(1)}, bf16[64,1024]{1,0:T(8,128)(2,1)S(1)}, u32[]{:S(2)}, u32[]{:S(2)}) collective-permute-start(bf16[64,1024]{1,0:T(8,128)(2,1)S(1)} %get-tuple-element.19), channel_id=1, source_target_pairs={{0,8},{1,9},{2,10},{3,11},{4,12},{5,13},{6,14},{7,15},{8,16},{9,17... | collective-permute-start | bytes 393224 | tf_op jit(solution)/shard_map/ppermute | solution.py:148
  135.9 0.7 copy-start.6
  135.9 0.7 copy-start.7
  135.9 0.7 copy-start.8
  139.2 9.7 %collective-permute-start.9 = (bf16[32,128]{1,0:T(8,128)(2,1)}, bf16[32,128]{1,0:T(8,128)(2,1)S(1)}, u32[]{:S(2)}, u32[]{:S(2)}) collective-permute-start(bf16[32,128]{1,0:T(8,128)(2,1)} %get-tuple-element.18), channel_id=1, source_target_pairs={{32,0},{33,1},{34,2},{35,3},{36,4},{37,5},{38,6},{39,7},{40,8},{41... | collective-permute-start | bytes 24584 | tf_op jit(solution)/shard_map/ppermute | solution.py:152
  142.8 6.0 %copy-start.5 = (bf16[64,3584]{1,0:T(8,128)(2,1)}, bf16[64,3584]{1,0:T(8,128)(2,1)S(1)}, u32[]{:S(2)}) copy-start(bf16[64,3584]{1,0:T(8,128)(2,1)S(1)} %collective-permute-done.8.late_ref) | copy-start | bytes 1376260
  142.9 6.0 %copy-start.3 = (bf16[72,3584]{1,0:T(8,128)(2,1)}, bf16[72,3584]{1,0:T(8,128)(2,1)S(1)}, u32[]{:S(2)}) copy-start(bf16[72,3584]{1,0:T(8,128)(2,1)S(1)} %collective-permute-done.7.early_ref) | copy-start | bytes 1548292
  148.8 0.6 copy-start.9

commit v3 on v2

--- a/solution.py
+++ b/solution.py
@@ -23,11 +23,11 @@
     return jnp.broadcast_to(row, (count, row.shape[1])).T[:, :1]
 
 
-def prep_kernel(chosen_ref, places_ref, counts_ref, tok_ref, near_ref, up_ref, early_ref, late_ref, meta_ref):
+def prep_kernel(chosen_ref, places_ref, counts_ref, tok_ref, first_ref, early_ref, late_ref, meta_ref):
     tokens, width = tok_ref.shape
     half = late_ref.shape[0]
     experts = counts_ref.shape[0]
-    rows = near_ref.shape[0]
+    rows = first_ref.shape[0]
     own = lax.axis_index(expert_axes)
     own_z = lax.axis_index("zl")
     chosen = chosen_ref[...]
@@ -41,8 +41,8 @@
     offset = (lax.shift_right_logical(chosen, 3) - own_z) & 3
     dest = chosen & 7
 
-    def slot_of(k, pitch, base):
-        return jnp.where(live & (offset == k), dest * pitch + base + places, -1)
+    def slot_of(k):
+        return jnp.where(live & (offset == k), dest * slots + places, -1)
 
     order = lax.broadcasted_iota(jnp.int32, (1, tokens), 1)
     key = (jnp.where(live & (offset == 2), 0, tokens) + order).astype(jnp.float32)
@@ -50,8 +50,8 @@
     rank = jnp.sum((key_rows.T < key_rows).astype(jnp.float32), axis=0, keepdims=True)
     perm = as_pick(lax.broadcasted_iota(jnp.int32, (tokens, tokens), 0) == rank.astype(jnp.int32))
     row_id = lax.broadcasted_iota(jnp.int32, (8, tokens), 0)
-    one_down = slot_of(3, 2 * slots, 0).astype(jnp.float32)
-    two_down = slot_of(2, 2 * slots, slots).astype(jnp.float32)
+    one_down = slot_of(3).astype(jnp.float32)
+    two_down = slot_of(2).astype(jnp.float32)
     pair = jnp.where(row_id == 0, one_down, jnp.where(row_id == 1, two_down, 0.0)).astype(jnp.bfloat16)
     moved = lax.dot_general(pair, perm, NT, preferred_element_type=jnp.float32)
 
@@ -62,28 +62,45 @@
     table = jnp.where(row_id < 2, moved, jnp.where(row_id == 2, rank, 0.0)).astype(jnp.bfloat16)
     early_ref[half:, :tokens] = table
     late_ref[...] = ordered[half:]
-    slot_id = lax.broadcasted_iota(jnp.int32, (rows, tokens), 0)
-    up_ref[...] = jnp.dot(as_pick(slot_id == slot_of(1, slots, 0)), tok, preferred_element_type=jnp.float32).astype(jnp.bfloat16)
-    near_ref[...] = jnp.dot(as_pick(slot_id == slot_of(0, slots, 0)), tok, preferred_element_type=jnp.float32).astype(jnp.bfloat16)
-    back = jnp.where(row_id == 0, slot_of(0, 2 * slots, 0), -1)
+    target = jnp.where(live & (offset < 2), (2 * dest + offset) * slots + places, -1)
+    pick = as_pick(lax.broadcasted_iota(jnp.int32, (rows, tokens), 0) == target)
+    first_ref[...] = jnp.dot(pick, tok, preferred_element_type=jnp.float32).astype(jnp.bfloat16)
+    back = jnp.where(row_id == 0, slot_of(0), -1)
     for k in (1, 2, 3):
-        back = jnp.where(row_id == k, slot_of(k, slots, 0), back)
+        back = jnp.where(row_id == k, slot_of(k), back)
     meta_ref[...] = back
 
 
-def pack_kernel(early1_ref, late1_ref, early2_ref, out_ref):
-    rows = out_ref.shape[0]
-    half, _ = late1_ref.shape
+def pack_one_kernel(early_ref, late_ref, out_ref):
+    half = late_ref.shape[0]
     tokens = 2 * half
-    row = lax.broadcasted_iota(jnp.int32, (rows, tokens), 0)
-    one = early1_ref[half:, :tokens].astype(jnp.float32)[0:1, :].astype(jnp.int32)
-    two = early2_ref[half:, :tokens].astype(jnp.float32)[1:2, :].astype(jnp.int32)
-    pick_one = as_pick(row == one)
-    pick_two = as_pick(row == two)
-    out = jnp.dot(pick_one[:, :half], early1_ref[:half], preferred_element_type=jnp.float32)
-    out = out + jnp.dot(pick_one[:, half:], late1_ref[...], preferred_element_type=jnp.float32)
-    out = out + jnp.dot(pick_two[:, :half], early2_ref[:half], preferred_element_type=jnp.float32)
+    target = early_ref[half:, :tokens].astype(jnp.float32)[0:1, :].astype(jnp.int32)
+    pick = as_pick(lax.broadcasted_iota(jnp.int32, (out_ref.shape[0], tokens), 0) == target)
+    out = jnp.dot(pick[:, :half], early_ref[:half], preferred_element_type=jnp.float32)
+    out = out + jnp.dot(pick[:, half:], late_ref[...], preferred_element_type=jnp.float32)
     out_ref[...] = out.astype(jnp.bfloat16)
+
+
+def pack_two_kernel(early_ref, out_ref):
+    half = early_ref.shape[0] - 8
+    target = early_ref[half:, :2 * half].astype(jnp.float32)[1:2, :].astype(jnp.int32)
+    pick = as_pick(lax.broadcasted_iota(jnp.int32, (out_ref.shape[0], 2 * half), 0) == target)
+    out_ref[...] = jnp.dot(pick[:, :half], early_ref[:half], preferred_element_type=jnp.float32).astype(jnp.bfloat16)
+
+
+def serve_kernel(r0_ref, r1_ref, r2_ref, r3_ref, weight_ref, out_ref, held_ref):
+    rows = r0_ref.shape[0]
+    step = weight_ref.shape[0]
+
+    @pl.when(pl.program_id(0) == 0)
+    def _():
+        for k, ref in enumerate((r0_ref, r1_ref, r2_ref, r3_ref)):
+            held_ref[k * rows:(k + 1) * rows] = ref[...]
+
+    found = lax.dot_general(weight_ref[...], held_ref[...], NT, preferred_element_type=jnp.float32).T
+    for k in range(4):
+        part = found[k * rows:(k + 1) * rows].reshape(rows // slots, slots, step)
+        out_ref[:, k] = part.astype(jnp.bfloat16)
 
 
 def back_kernel(meta_ref, chosen_ref, scores_ref, hidden_ref, r0_ref, r1_ref, r2_ref, r3_ref, act_ref, score_ref, score_bf_ref):
@@ -154,48 +171,57 @@
     def exchange(value):
         return lax.all_to_all(value, group, split_axis=0, concat_axis=0, tiled=True)
 
-    def serve(value):
-        flat = value.reshape(nxc * 2 * slots, width)
-        out = lax.dot_general(flat, weight, NT, preferred_element_type=jnp.float32).astype(jnp.bfloat16)
-        return out.reshape(nxc, 2 * slots, hidden_width)
-
-    def cut(value, k):
-        return value[:, k * slots:(k + 1) * slots].reshape(rows, hidden_width)
-
-    near, up, early, late, meta = pl.pallas_call(
+    def spread(value):
+        return exchange(value.reshape(nxc, slots, width)).reshape(rows, width)
+
+    def serve(*values):
+        step = hidden_width // 2
+        return pl.pallas_call(
+            serve_kernel,
+            grid=(hidden_width // step,),
+            out_shape=sds((nxc, 4, slots, hidden_width)),
+            in_specs=[pl.BlockSpec((rows, width), lambda j: (0, 0))] * 4 + [pl.BlockSpec((step, width), lambda j: (j, 0))],
+            out_specs=pl.BlockSpec((nxc, 4, slots, step), lambda j: (0, 0, 0, j)),
+            scratch_shapes=[pltpu.VMEM((4 * rows, width), jnp.bfloat16)],
+        )(*values, weight)
+
+    def part(value, k):
+        return value[:, k].reshape(rows, value.shape[3])
+
+    first, early, late, meta = pl.pallas_call(
         prep_kernel,
-        out_shape=(sds((rows, width)), sds((rows, width)), sds((half + 8, width)), sds((half, width)), sds((8, tokens), jnp.int32)),
+        out_shape=(sds((2 * rows, width)), sds((half + 8, width)), sds((half, width)), sds((8, tokens), jnp.int32)),
         in_specs=whole(4),
-        out_specs=tuple(whole(5)),
+        out_specs=tuple(whole(4)),
     )(expert_ids, slot_ids, counts[0], tok)
     early1 = along_path(early, -1)
-    up_got = along_z(up, 1)
+    first = exchange(first.reshape(nxc, 2, slots, width))
     late1 = along_path(late, -1)
     early2 = along_path(early1, -1)
-    first = jnp.concatenate([near.reshape(nxc, slots, width), up_got.reshape(nxc, slots, width)], axis=1)
-    first = exchange(first)
+    near, up = part(first, 0), part(first, 1)
+    up = along_z(up, 1)
+    one = pl.pallas_call(
+        pack_one_kernel, out_shape=sds((rows, width)), in_specs=whole(2), out_specs=whole(1)[0]
+    )(early1, late1)
+    one = spread(one)
     late4 = to_end(late1, 3)
-    second = pl.pallas_call(
-        pack_kernel, out_shape=sds((2 * rows, width)), in_specs=whole(3), out_specs=whole(1)[0]
-    )(early1, late1, early2)
-    second = exchange(second.reshape(nxc, 2 * slots, width))
+    two = pl.pallas_call(
+        pack_two_kernel, out_shape=sds((rows, width)), in_specs=whole(1), out_specs=whole(1)[0]
+    )(early2)
+    two = spread(two)
     early4 = to_end(early2, 2)
-    first_back = serve(first)
-    first_got = exchange(first_back)
-    second_back = serve(second)
-    second_got = exchange(second_back)
-    r1 = cut(first_got, 1)
+    served = serve(near, up, one, two)
+    served = exchange(served)
+    r0, r1, r3, r2 = (part(served, k) for k in range(4))
+    r2 = along_path(r2, 2)
     r1 = along_z(r1, -1)
-    r3 = cut(second_got, 0)
-    r2 = cut(second_got, 1)
-    r2 = along_path(r2, 2)
     r3 = along_path(r3, 1)
     act, score, score_bf = pl.pallas_call(
         back_kernel,
         out_shape=(sds((tokens, hidden_width)), sds((scores.shape[2], tokens), jnp.float32), sds((scores.shape[2], tokens))),
         in_specs=whole(8),
         out_specs=tuple(whole(3)),
-    )(meta, expert_ids, scores[0].T, hidden_act[0], first_got.reshape(2 * rows, hidden_width), r1, r2, r3)
+    )(meta, expert_ids, scores[0].T, hidden_act[0], r0, r1, r2, r3)
     late_score = to_end(score_bf, nzl)
     upstream = pl.pallas_call(
         up_kernel, out_shape=sds((tokens, width)), in_specs=whole(4), out_specs=whole(1)[0]

time: 154 us -> 169 us (1.097)
  the two profiles are of different devices: /device:TPU:50 before, /device:TPU:10 now
where the time goes in v3:
time: 169 us; the launch traced here: 168 us
  starting transfers between devices  72.3 us (43%)
  waiting for transfers between devices  70.4 us (42%)
  Pallas kernels  19.1 us (11%)
  local copies, waits for them, and re-layouts  5.15 us (3%)
    ppermute x2, waiting for transfers between devices, along_z(): return lax.ppermute(value, axes, lanes(pairs))  41.4 us
    ppermute x5, starting transfers between devices, along_path(): lax.ppermute(value, axes, lanes([(a, (a + distance) % places) for a in ra...  33.3 us
    all_to_all x4, starting transfers between devices, exchange(): return lax.all_to_all(value, group, split_axis=0, concat_axis=0, tiled=True)  19.3 us
    ppermute x5, waiting for transfers between devices, along_path(): lax.ppermute(value, axes, lanes([(a, (a + distance) % places) for a in ra...  17.4 us
    ppermute x3, starting transfers between devices, to_end(): return lax.ppermute(value, axes, lanes(pairs))  12.7 us
    ppermute x2, starting transfers between devices, along_z(): return lax.ppermute(value, axes, lanes(pairs))  7.04 us
    ppermute x3, waiting for transfers between devices, to_end(): return lax.ppermute(value, axes, lanes(pairs))  6.07 us
    pallas_call x1, Pallas kernels, serve(): pl.pallas_call(serve_kernel, grid=(hidden_width // step,), out_shape=sds(...  5.83 us
  transfers between devices with their start and end apart: 14, of which 8 were waited for; matrix products, arithmetic and copies ran while one was open for 1% of the time, Pallas kernels for 4%

profile of v3, /device:TPU:10, one launch (start us, length us, event | category | flops | bytes accessed | tf_op | source)
XLA Modules:
  0.0 167.8 jit_solution(2171100545698393420)
XLA Ops:
  0.6 3.1 %shard_map.103 = (bf16[128,3584]{1,0:T(8,128)(2,1)}, bf16[72,3584]{1,0:T(8,128)(2,1)}, bf16[64,3584]{1,0:T(8,128)(2,1)}, s32[8,128]{1,0:T(8,128)}) custom-call(s32[1,128]{1,0:T(1,128)} %chosen_ref.3, s32[1,128]{1,0:T(1,128)} %places_ref.1, s32[32,32]{1,0:T(8,128)} %bitcast.38, bf16[128,3584]{1,0:T(8,128)(2,1)} %bitcast.35), custom_call_target="tpu_custom_call" | custom-call | tf_op jit(solution)/shard_map/pallas_call | solution.py:191
  3.7 4.8 %all-to-all-start = ((bf16[8,2,8,3584]{3,2,1,0:T(8,128)(2,1)}), bf16[8,2,8,3584]{3,2,1,0:T(8,128)(2,1)S(1)}, u32[]{:S(2)}, u32[]{:S(2)}) async-start(bf16[8,2,8,3584]{3,2,1,0:T(8,128)(2,1)} %bitcast.34), calls=%async_computation | async-start | bytes 1835008 | tf_op jit(solution)/shard_map/all_to_all | solution.py:172
  8.6 18.1 %collective-permute-start.1 = (bf16[72,3584]{1,0:T(8,128)(2,1)}, bf16[72,3584]{1,0:T(8,128)(2,1)S(1)}, u32[]{:S(2)}, u32[]{:S(2)}) collective-permute-start(bf16[72,3584]{1,0:T(8,128)(2,1)} %get-tuple-element.12), channel_id=1, source_target_pairs={{0,1016},{1,1017},{2,1018},{3,1019},{4,1020},{5,1021},{6,1022},{7,... | collective-permute-start | bytes 1548296 | tf_op jit(solution)/shard_map/ppermute | solution.py:165
  26.7 2.5 %collective-permute-start.2 = (bf16[64,3584]{1,0:T(8,128)(2,1)}, bf16[64,3584]{1,0:T(8,128)(2,1)S(1)}, u32[]{:S(2)}, u32[]{:S(2)}) collective-permute-start(bf16[64,3584]{1,0:T(8,128)(2,1)} %get-tuple-element.13), channel_id=1, source_target_pairs={{0,1016},{1,1017},{2,1018},{3,1019},{4,1020},{5,1021},{6,1022},{7,... | collective-permute-start | bytes 1376264 | tf_op jit(solution)/shard_map/ppermute | solution.py:165
  29.1 10.0 %collective-permute-done.1.early_ref = bf16[72,3584]{1,0:T(8,128)(2,1)S(1)} collective-permute-done((bf16[72,3584]{1,0:T(8,128)(2,1)}, bf16[72,3584]{1,0:T(8,128)(2,1)S(1)}, u32[]{:S(2)}, u32[]{:S(2)}) %collective-permute-start.1) | collective-permute-done | bytes 516128 | tf_op jit(solution)/shard_map/ppermute | solution.py:165
  39.1 0.0 copy-start.4
  39.1 6.4 %collective-permute-start.3 = (bf16[72,3584]{1,0:T(8,128)(2,1)S(1)}, bf16[72,3584]{1,0:T(8,128)(2,1)S(1)}, u32[]{:S(2)}, u32[]{:S(2)}) collective-permute-start(bf16[72,3584]{1,0:T(8,128)(2,1)S(1)} %collective-permute-done.1.early_ref), channel_id=1, source_target_pairs={{0,1016},{1,1017},{2,1018},{3,1019},{4,1020},{5,1021},{6,1022},{7,... | collective-permute-start | bytes 1548296 | tf_op jit(solution)/shard_map/ppermute | solution.py:165
  45.5 3.4 %collective-permute-done.2.late_ref = bf16[64,3584]{1,0:T(8,128)(2,1)S(1)} collective-permute-done((bf16[64,3584]{1,0:T(8,128)(2,1)}, bf16[64,3584]{1,0:T(8,128)(2,1)S(1)}, u32[]{:S(2)}, u32[]{:S(2)}) %collective-permute-start.2) | collective-permute-done | bytes 458784 | tf_op jit(solution)/shard_map/ppermute | solution.py:165
  48.9 0.0 copy-done.4
  48.9 0.0 copy-start.6
  48.9 0.8 copy-done.6
  49.7 2.4 %shard_map.104 = bf16[64,3584]{1,0:T(8,128)(2,1)} custom-call(bf16[72,3584]{1,0:T(8,128)(2,1)} %copy-done.4, bf16[64,3584]{1,0:T(8,128)(2,1)} %copy-done.6), custom_call_target="tpu_custom_call" | custom-call | tf_op jit(solution)/shard_map/pallas_call | solution.py:203
  52.1 0.0 all-to-all-done
  52.1 4.8 %all-to-all-start.1 = ((bf16[8,8,3584]{2,1,0:T(8,128)(2,1)}), bf16[8,8,3584]{2,1,0:T(8,128)(2,1)S(1)}, u32[]{:S(2)}, u32[]{:S(2)}) async-start(bf16[8,8,3584]{2,1,0:T(8,128)(2,1)} %bitcast.30), calls=%async_computation.1 | async-start | bytes 917504 | tf_op jit(solution)/shard_map/all_to_all | solution.py:172
  56.9 0.0 copy-start.7
  56.9 0.8 slice_bitcast_fusion
  57.8 1.9 %collective-permute-start = (bf16[64,3584]{1,0:T(8,128)(2,1)S(1)}, bf16[64,3584]{1,0:T(8,128)(2,1)}, u32[]{:S(2)}, u32[]{:S(2)}) collective-permute-start(bf16[64,3584]{1,0:T(8,128)(2,1)S(1)} %get-tuple-element.17), channel_id=1, source_target_pairs={{0,8},{1,9},{2,10},{3,11},{4,12},{5,13},{6,14},{7,15},{8,16},{9,17... | collective-permute-start | bytes 1376264 | tf_op jit(solution)/shard_map/ppermute | solution.py:162
  59.7 0.0 collective-permute-done.3.early_ref
  59.7 0.0 copy-start.2
  59.7 0.8 copy-done.2
  60.5 2.1 %shard_map.105 = bf16[64,3584]{1,0:T(8,128)(2,1)} custom-call(bf16[72,3584]{1,0:T(8,128)(2,1)} %copy-done.2), custom_call_target="tpu_custom_call" | custom-call | tf_op jit(solution)/shard_map/pallas_call | solution.py:208
  62.6 0.0 copy-start.3
  62.6 2.5 %all-to-all-done.1 = bf16[8,8,3584]{2,1,0:T(8,128)(2,1)S(1)} async-done(((bf16[8,8,3584]{2,1,0:T(8,128)(2,1)}), bf16[8,8,3584]{2,1,0:T(8,128)(2,1)S(1)}, u32[]{:S(2)}, u32[]{:S(2)}) %all-to-all-start.1) | async-done | bytes 458784 | tf_op jit(solution)/shard_map/all_to_all | solution.py:172
  65.1 0.0 copy-start
  65.1 4.8 %all-to-all-start.2 = ((bf16[8,8,3584]{2,1,0:T(8,128)(2,1)}), bf16[8,8,3584]{2,1,0:T(8,128)(2,1)S(1)}, u32[]{:S(2)}, u32[]{:S(2)}) async-start(bf16[8,8,3584]{2,1,0:T(8,128)(2,1)} %bitcast.31), calls=%async_computation.2 | async-start | bytes 917504 | tf_op jit(solution)/shard_map/all_to_all | solution.py:172
  69.9 5.2 %collective-permute-done.r1_ref = bf16[64,3584]{1,0:T(8,128)(2,1)} collective-permute-done((bf16[64,3584]{1,0:T(8,128)(2,1)S(1)}, bf16[64,3584]{1,0:T(8,128)(2,1)}, u32[]{:S(2)}, u32[]{:S(2)}) %collective-permute-start) | collective-permute-done | bytes 458784 | tf_op jit(solution)/shard_map/ppermute | solution.py:162
  75.2 3.0 %all-to-all-done.2 = bf16[8,8,3584]{2,1,0:T(8,128)(2,1)S(1)} async-done(((bf16[8,8,3584]{2,1,0:T(8,128)(2,1)}), bf16[8,8,3584]{2,1,0:T(8,128)(2,1)S(1)}, u32[]{:S(2)}, u32[]{:S(2)}) %all-to-all-start.2) | async-done | bytes 458784 | tf_op jit(solution)/shard_map/all_to_all | solution.py:172
  78.1 0.0 copy-start.1
  78.1 0.0 copy-done
  78.1 0.8 copy-done.1
  78.9 5.8 %shard_map.106 = bf16[8,4,8,1024]{3,2,1,0:T(8,128)(2,1)} custom-call(bf16[64,3584]{1,0:T(8,128)(2,1)} %get-tuple-element.18.r0_ref, bf16[64,3584]{1,0:T(8,128)(2,1)} %collective-permute-done.r1_ref, bf16[64,3584]{1,0:T(8,128)(2,1)} %bitcast.32, bf16[64,3584]{1,0:T(8,128)(2,1)} %bitcast.33, bf16[1024,3584]{1,0:T(8,128)(2,1)} %bitcast.29), custom_call_target="tpu_custom_call" | custom-call | tf_op jit(solution)/shard_map/pallas_call | solution.py:179
  84.7 4.8 %all-to-all-start.3 = ((bf16[8,4,8,1024]{3,2,1,0:T(8,128)(2,1)}), bf16[8,4,8,1024]{3,2,1,0:T(8,128)(2,1)S(1)}, u32[]{:S(2)}, u32[]{:S(2)}) async-start(bf16[8,4,8,1024]{3,2,1,0:T(8,128)(2,1)} %shard_map.106), calls=%async_computation.3 | async-start | bytes 1048576 | tf_op jit(solution)/shard_map/all_to_all | solution.py:172
  89.6 0.0 copy-done.3
  89.6 5.4 %collective-permute-start.7 = (bf16[72,3584]{1,0:T(8,128)(2,1)S(1)}, bf16[72,3584]{1,0:T(8,128)(2,1)S(1)}, u32[]{:S(2)}, u32[]{:S(2)}) collective-permute-start(bf16[72,3584]{1,0:T(8,128)(2,1)S(1)} %copy-done.3), channel_id=1, source_target_pairs={{16,0},{17,1},{18,2},{19,3},{20,4},{21,5},{22,6},{23,7},{24,8},{25... | collective-permute-start | bytes 1548296 | tf_op jit(solution)/shard_map/ppermute | solution.py:169
  95.0 0.0 copy-done.7
  95.0 3.7 %collective-permute-start.8 = (bf16[64,3584]{1,0:T(8,128)(2,1)S(1)}, bf16[64,3584]{1,0:T(8,128)(2,1)S(1)}, u32[]{:S(2)}, u32[]{:S(2)}) collective-permute-start(bf16[64,3584]{1,0:T(8,128)(2,1)S(1)} %copy-done.7), channel_id=1, source_target_pairs={{24,0},{25,1},{26,2},{27,3},{28,4},{29,5},{30,6},{31,7},{32,8},{33... | collective-permute-start | bytes 1376264 | tf_op jit(solution)/shard_map/ppermute | solution.py:169
  98.7 0.0 all-to-all-done.3
  98.7 0.7 slice_bitcast_fusion.2
  99.4 2.5 %collective-permute-start.6 = (bf16[64,1024]{1,0:T(8,128)(2,1)S(1)}, bf16[64,1024]{1,0:T(8,128)(2,1)S(1)}, u32[]{:S(2)}, u32[]{:S(2)}) collective-permute-start(bf16[64,1024]{1,0:T(8,128)(2,1)S(1)} %get-tuple-element.19), channel_id=1, source_target_pairs={{0,8},{1,9},{2,10},{3,11},{4,12},{5,13},{6,14},{7,15},{8,16},{9,17... | collective-permute-start | bytes 393224 | tf_op jit(solution)/shard_map/ppermute | solution.py:165
  102.0 3.8 %collective-permute-start.5 = (bf16[64,1024]{1,0:T(8,128)(2,1)S(1)}, bf16[64,1024]{1,0:T(8,128)(2,1)S(1)}, u32[]{:S(2)}, u32[]{:S(2)}) collective-permute-start(bf16[64,1024]{1,0:T(8,128)(2,1)S(1)} %get-tuple-element.20), channel_id=1, source_target_pairs={{0,16},{1,17},{2,18},{3,19},{4,20},{5,21},{6,22},{7,23},{8,24},{9,... | collective-permute-start | bytes 393224 | tf_op jit(solution)/shard_map/ppermute | solution.py:165
  105.8 5.1 %collective-permute-start.4 = (bf16[64,1024]{1,0:T(8,128)(2,1)S(1)}, bf16[64,1024]{1,0:T(8,128)(2,1)S(1)}, u32[]{:S(2)}, u32[]{:S(2)}) collective-permute-start(bf16[64,1024]{1,0:T(8,128)(2,1)S(1)} %get-tuple-element.21), channel_id=1, source_target_pairs={{0,120},{1,121},{2,122},{3,123},{4,124},{5,125},{6,126},{7,127},{8... | collective-permute-start | bytes 393224 | tf_op jit(solution)/shard_map/ppermute | solution.py:162
  111.0 0.0 collective-permute-done.6.r3_ref
  111.0 0.0 copy-start.9
  111.0 4.0 %collective-permute-done.5.r2_ref = bf16[64,1024]{1,0:T(8,128)(2,1)S(1)} collective-permute-done((bf16[64,1024]{1,0:T(8,128)(2,1)S(1)}, bf16[64,1024]{1,0:T(8,128)(2,1)S(1)}, u32[]{:S(2)}, u32[]{:S(2)}) %collective-permute-start.5) | collective-permute-done | bytes 131104 | tf_op jit(solution)/shard_map/ppermute | solution.py:165
  115.0 0.0 copy-start.10
  115.0 36.2 %collective-permute-done.4.r1_ref = bf16[64,1024]{1,0:T(8,128)(2,1)S(1)} collective-permute-done((bf16[64,1024]{1,0:T(8,128)(2,1)S(1)}, bf16[64,1024]{1,0:T(8,128)(2,1)S(1)}, u32[]{:S(2)}, u32[]{:S(2)}) %collective-permute-start.4) | collective-permute-done | bytes 131104 | tf_op jit(solution)/shard_map/ppermute | solution.py:162
  151.2 0.0 copy-start.11
  151.2 0.0 copy-done.9
  151.2 0.0 copy-done.10
  151.2 0.6 copy-done.11
  151.8 2.5 %shard_map.107 = (bf16[128,1024]{1,0:T(8,128)(2,1)}, f32[32,128]{1,0:T(8,128)}, bf16[32,128]{1,0:T(8,128)(2,1)}) custom-call(s32[8,128]{1,0:T(8,128)} %get-tuple-element.10.meta_ref, s32[1,128]{1,0:T(1,128)} %chosen_ref.3, f32[32,128]{1,0:T(8,128)} %bitcast.39, bf16[128,1024]{1,0:T(8,128)(2,1)} %bitcast.37, bf16[64,1024]{1,0:T(8,128)(2,1)} %get-tuple-element.22.r0_ref, ...), custom_call_target="tpu_custom_call" | custom-call | tf_op jit(solution)/shard_map/pallas_call | solution.py:219
  154.4 3.5 %collective-permute-start.9 = (bf16[32,128]{1,0:T(8,128)(2,1)}, bf16[32,128]{1,0:T(8,128)(2,1)S(1)}, u32[]{:S(2)}, u32[]{:S(2)}) collective-permute-start(bf16[32,128]{1,0:T(8,128)(2,1)} %get-tuple-element.16), channel_id=1, source_target_pairs={{32,0},{33,1},{34,2},{35,3},{36,4},{37,5},{38,6},{39,7},{40,8},{41... | collective-permute-start | bytes 24584 | tf_op jit(solution)/shard_map/ppermute | solution.py:169
  157.9 0.0 collective-permute-done.8.late_ref
  157.9 0.0 copy-start.8
  157.9 0.0 collective-permute-done.7.early_ref
  157.9 0.0 copy-start.5
  157.9 6.1 %collective-permute-done.9.score_ref = bf16[32,128]{1,0:T(8,128)(2,1)S(1)} collective-permute-done((bf16[32,128]{1,0:T(8,128)(2,1)}, bf16[32,128]{1,0:T(8,128)(2,1)S(1)}, u32[]{:S(2)}, u32[]{:S(2)}) %collective-permute-start.9) | collective-permute-done | bytes 8224 | tf_op jit(solution)/shard_map/ppermute | solution.py:169
  164.0 0.0 copy-done.8
  164.0 0.0 copy-done.5
  164.0 0.0 copy-start.12
  164.0 0.6 copy-done.12
  164.6 3.2 %shard_map.108 = bf16[128,3584]{1,0:T(8,128)(2,1)} custom-call(bf16[72,3584]{1,0:T(8,128)(2,1)} %copy-done.5, bf16[64,3584]{1,0:T(8,128)(2,1)} %copy-done.8, bf16[32,128]{1,0:T(8,128)(2,1)} %copy-done.12, bf16[32,3584]{1,0:T(8,128)(2,1)} %router_ref.1), custom_call_target="tpu_custom_call" | custom-call | tf_op jit(solution)/shard_map/pallas_call | solution.py:226
Async XLA Ops:
  3.7 48.4 %all-to-all-start = ((bf16[8,2,8,3584]{3,2,1,0:T(8,128)(2,1)}), bf16[8,2,8,3584]{3,2,1,0:T(8,128)(2,1)S(1)}, u32[]{:S(2)}, u32[]{:S(2)}) async-start(bf16[8,2,8,3584]{3,2,1,0:T(8,128)(2,1)} %bitcast.34), calls=%async_computation | async-start | bytes 1835008 | tf_op jit(solution)/shard_map/all_to_all | solution.py:172
  8.6 30.5 %collective-permute-start.1 = (bf16[72,3584]{1,0:T(8,128)(2,1)}, bf16[72,3584]{1,0:T(8,128)(2,1)S(1)}, u32[]{:S(2)}, u32[]{:S(2)}) collective-permute-start(bf16[72,3584]{1,0:T(8,128)(2,1)} %get-tuple-element.12), channel_id=1, source_target_pairs={{0,1016},{1,1017},{2,1018},{3,1019},{4,1020},{5,1021},{6,1022},{7,... | collective-permute-start | bytes 1548296 | tf_op jit(solution)/shard_map/ppermute | solution.py:165
  26.7 22.3 %collective-permute-start.2 = (bf16[64,3584]{1,0:T(8,128)(2,1)}, bf16[64,3584]{1,0:T(8,128)(2,1)S(1)}, u32[]{:S(2)}, u32[]{:S(2)}) collective-permute-start(bf16[64,3584]{1,0:T(8,128)(2,1)} %get-tuple-element.13), channel_id=1, source_target_pairs={{0,1016},{1,1017},{2,1018},{3,1019},{4,1020},{5,1021},{6,1022},{7,... | collective-permute-start | bytes 1376264 | tf_op jit(solution)/shard_map/ppermute | solution.py:165
  39.1 9.8 %copy-start.4 = (bf16[72,3584]{1,0:T(8,128)(2,1)}, bf16[72,3584]{1,0:T(8,128)(2,1)S(1)}, u32[]{:S(2)}) copy-start(bf16[72,3584]{1,0:T(8,128)(2,1)S(1)} %collective-permute-done.1.early_ref) | copy-start | bytes 1548292
  39.1 20.6 %collective-permute-start.3 = (bf16[72,3584]{1,0:T(8,128)(2,1)S(1)}, bf16[72,3584]{1,0:T(8,128)(2,1)S(1)}, u32[]{:S(2)}, u32[]{:S(2)}) collective-permute-start(bf16[72,3584]{1,0:T(8,128)(2,1)S(1)} %collective-permute-done.1.early_ref), channel_id=1, source_target_pairs={{0,1016},{1,1017},{2,1018},{3,1019},{4,1020},{5,1021},{6,1022},{7,... | collective-permute-start | bytes 1548296 | tf_op jit(solution)/shard_map/ppermute | solution.py:165
  48.9 0.8 copy-start.6
  52.1 13.0 %all-to-all-start.1 = ((bf16[8,8,3584]{2,1,0:T(8,128)(2,1)}), bf16[8,8,3584]{2,1,0:T(8,128)(2,1)S(1)}, u32[]{:S(2)}, u32[]{:S(2)}) async-start(bf16[8,8,3584]{2,1,0:T(8,128)(2,1)} %bitcast.30), calls=%async_computation.1 | async-start | bytes 917504 | tf_op jit(solution)/shard_map/all_to_all | solution.py:172
  56.9 38.1 %copy-start.7 = (bf16[64,3584]{1,0:T(8,128)(2,1)S(1)}, bf16[64,3584]{1,0:T(8,128)(2,1)}, u32[]{:S(2)}) copy-start(bf16[64,3584]{1,0:T(8,128)(2,1)} %copy-done.6) | copy-start | bytes 1376260
  57.8 17.4 %collective-permute-start = (bf16[64,3584]{1,0:T(8,128)(2,1)S(1)}, bf16[64,3584]{1,0:T(8,128)(2,1)}, u32[]{:S(2)}, u32[]{:S(2)}) collective-permute-start(bf16[64,3584]{1,0:T(8,128)(2,1)S(1)} %get-tuple-element.17), channel_id=1, source_target_pairs={{0,8},{1,9},{2,10},{3,11},{4,12},{5,13},{6,14},{7,15},{8,16},{9,17... | collective-permute-start | bytes 1376264 | tf_op jit(solution)/shard_map/ppermute | solution.py:162
  59.7 0.8 copy-start.2
  62.6 27.0 %copy-start.3 = (bf16[72,3584]{1,0:T(8,128)(2,1)S(1)}, bf16[72,3584]{1,0:T(8,128)(2,1)}, u32[]{:S(2)}) copy-start(bf16[72,3584]{1,0:T(8,128)(2,1)} %copy-done.2) | copy-start | bytes 1548292
  65.1 13.0 %copy-start = (bf16[8,8,3584]{2,1,0:T(8,128)(2,1)}, bf16[8,8,3584]{2,1,0:T(8,128)(2,1)S(1)}, u32[]{:S(2)}) copy-start(bf16[8,8,3584]{2,1,0:T(8,128)(2,1)S(1)} %all-to-all-done.1) | copy-start | bytes 1376260
  65.1 13.0 %all-to-all-start.2 = ((bf16[8,8,3584]{2,1,0:T(8,128)(2,1)}), bf16[8,8,3584]{2,1,0:T(8,128)(2,1)S(1)}, u32[]{:S(2)}, u32[]{:S(2)}) async-start(bf16[8,8,3584]{2,1,0:T(8,128)(2,1)} %bitcast.31), calls=%async_computation.2 | async-start | bytes 917504 | tf_op jit(solution)/shard_map/all_to_all | solution.py:172
  78.1 0.8 copy-start.1
  84.7 14.0 %all-to-all-start.3 = ((bf16[8,4,8,1024]{3,2,1,0:T(8,128)(2,1)}), bf16[8,4,8,1024]{3,2,1,0:T(8,128)(2,1)S(1)}, u32[]{:S(2)}, u32[]{:S(2)}) async-start(bf16[8,4,8,1024]{3,2,1,0:T(8,128)(2,1)} %shard_map.106), calls=%async_computation.3 | async-start | bytes 1048576 | tf_op jit(solution)/shard_map/all_to_all | solution.py:172
  89.6 68.4 %collective-permute-start.7 = (bf16[72,3584]{1,0:T(8,128)(2,1)S(1)}, bf16[72,3584]{1,0:T(8,128)(2,1)S(1)}, u32[]{:S(2)}, u32[]{:S(2)}) collective-permute-start(bf16[72,3584]{1,0:T(8,128)(2,1)S(1)} %copy-done.3), channel_id=1, source_target_pairs={{16,0},{17,1},{18,2},{19,3},{20,4},{21,5},{22,6},{23,7},{24,8},{25... | collective-permute-start | bytes 1548296 | tf_op jit(solution)/shard_map/ppermute | solution.py:169
  95.0 62.9 %collective-permute-start.8 = (bf16[64,3584]{1,0:T(8,128)(2,1)S(1)}, bf16[64,3584]{1,0:T(8,128)(2,1)S(1)}, u32[]{:S(2)}, u32[]{:S(2)}) collective-permute-start(bf16[64,3584]{1,0:T(8,128)(2,1)S(1)} %copy-done.7), channel_id=1, source_target_pairs={{24,0},{25,1},{26,2},{27,3},{28,4},{29,5},{30,6},{31,7},{32,8},{33... | collective-permute-start | bytes 1376264 | tf_op jit(solution)/shard_map/ppermute | solution.py:169
  99.4 11.5 %collective-permute-start.6 = (bf16[64,1024]{1,0:T(8,128)(2,1)S(1)}, bf16[64,1024]{1,0:T(8,128)(2,1)S(1)}, u32[]{:S(2)}, u32[]{:S(2)}) collective-permute-start(bf16[64,1024]{1,0:T(8,128)(2,1)S(1)} %get-tuple-element.19), channel_id=1, source_target_pairs={{0,8},{1,9},{2,10},{3,11},{4,12},{5,13},{6,14},{7,15},{8,16},{9,17... | collective-permute-start | bytes 393224 | tf_op jit(solution)/shard_map/ppermute | solution.py:165
  102.0 13.0 %collective-permute-start.5 = (bf16[64,1024]{1,0:T(8,128)(2,1)S(1)}, bf16[64,1024]{1,0:T(8,128)(2,1)S(1)}, u32[]{:S(2)}, u32[]{:S(2)}) collective-permute-start(bf16[64,1024]{1,0:T(8,128)(2,1)S(1)} %get-tuple-element.20), channel_id=1, source_target_pairs={{0,16},{1,17},{2,18},{3,19},{4,20},{5,21},{6,22},{7,23},{8,24},{9,... | collective-permute-start | bytes 393224 | tf_op jit(solution)/shard_map/ppermute | solution.py:165
  105.8 45.3 %collective-permute-start.4 = (bf16[64,1024]{1,0:T(8,128)(2,1)S(1)}, bf16[64,1024]{1,0:T(8,128)(2,1)S(1)}, u32[]{:S(2)}, u32[]{:S(2)}) collective-permute-start(bf16[64,1024]{1,0:T(8,128)(2,1)S(1)} %get-tuple-element.21), channel_id=1, source_target_pairs={{0,120},{1,121},{2,122},{3,123},{4,124},{5,125},{6,126},{7,127},{8... | collective-permute-start | bytes 393224 | tf_op jit(solution)/shard_map/ppermute | solution.py:162
  111.0 40.2 %copy-start.9 = (bf16[64,1024]{1,0:T(8,128)(2,1)}, bf16[64,1024]{1,0:T(8,128)(2,1)S(1)}, u32[]{:S(2)}) copy-start(bf16[64,1024]{1,0:T(8,128)(2,1)S(1)} %collective-permute-done.6.r3_ref) | copy-start | bytes 393220
  115.0 36.2 %copy-start.10 = (bf16[64,1024]{1,0:T(8,128)(2,1)}, bf16[64,1024]{1,0:T(8,128)(2,1)S(1)}, u32[]{:S(2)}) copy-start(bf16[64,1024]{1,0:T(8,128)(2,1)S(1)} %collective-permute-done.5.r2_ref) | copy-start | bytes 393220
  151.2 0.6 copy-start.11
  154.4 9.7 %collective-permute-start.9 = (bf16[32,128]{1,0:T(8,128)(2,1)}, bf16[32,128]{1,0:T(8,128)(2,1)S(1)}, u32[]{:S(2)}, u32[]{:S(2)}) collective-permute-start(bf16[32,128]{1,0:T(8,128)(2,1)} %get-tuple-element.16), channel_id=1, source_target_pairs={{32,0},{33,1},{34,2},{35,3},{36,4},{37,5},{38,6},{39,7},{40,8},{41... | collective-permute-start | bytes 24584 | tf_op jit(solution)/shard_map/ppermute | solution.py:169
  157.9 6.1 %copy-start.8 = (bf16[64,3584]{1,0:T(8,128)(2,1)}, bf16[64,3584]{1,0:T(8,128)(2,1)S(1)}, u32[]{:S(2)}) copy-start(bf16[64,3584]{1,0:T(8,128)(2,1)S(1)} %collective-permute-done.8.late_ref) | copy-start | bytes 1376260
  157.9 6.1 %copy-start.5 = (bf16[72,3584]{1,0:T(8,128)(2,1)}, bf16[72,3584]{1,0:T(8,128)(2,1)S(1)}, u32[]{:S(2)}) copy-start(bf16[72,3584]{1,0:T(8,128)(2,1)S(1)} %collective-permute-done.7.early_ref) | copy-start | bytes 1548292
  164.0 0.6 copy-start.12

commit v4 on v3

--- a/solution.py
+++ b/solution.py
@@ -151,7 +151,6 @@
     hidden_width = hidden_act.shape[2]
     half = tokens // 2
     rows = nxc * slots
-    places = ny * nz
     weight = down_weight[0]
 
     def lanes(pairs):
@@ -161,11 +160,13 @@
         pairs = [(y * nz + z, y * nz + (z + distance) % nz) for y in range(ny) for z in range(nz)]
         return lax.ppermute(value, axes, lanes(pairs))
 
-    def along_path(value, distance):
-        return lax.ppermute(value, axes, lanes([(a, (a + distance) % places) for a in range(places)]))
-
     def to_end(value, left):
-        pairs = [(a, (a - left) % places) for a in range(places) if (a + nzl - left) % places >= nzl]
+        pairs = []
+        for y in range(ny):
+            for z in range(nz):
+                to = y * nz + (z + nzl - left) % nz - nzl
+                if to >= 0:
+                    pairs.append((y * nz + z, to))
         return lax.ppermute(value, axes, lanes(pairs))
 
     def exchange(value):
@@ -194,10 +195,10 @@
         in_specs=whole(4),
         out_specs=tuple(whole(4)),
     )(expert_ids, slot_ids, counts[0], tok)
-    early1 = along_path(early, -1)
+    early1 = along_z(early, -1)
     first = exchange(first.reshape(nxc, 2, slots, width))
-    late1 = along_path(late, -1)
-    early2 = along_path(early1, -1)
+    late1 = along_z(late, -1)
+    early2 = along_z(early1, -1)
     near, up = part(first, 0), part(first, 1)
     up = along_z(up, 1)
     one = pl.pallas_call(
@@ -213,9 +214,9 @@
     served = serve(near, up, one, two)
     served = exchange(served)
     r0, r1, r3, r2 = (part(served, k) for k in range(4))
-    r2 = along_path(r2, 2)
+    r2 = along_z(r2, 2)
     r1 = along_z(r1, -1)
-    r3 = along_path(r3, 1)
+    r3 = along_z(r3, 1)
     act, score, score_bf = pl.pallas_call(
         back_kernel,
         out_shape=(sds((tokens, hidden_width)), sds((scores.shape[2], tokens), jnp.float32), sds((scores.shape[2], tokens))),

time: 169 us -> 169 us (level)
  waiting for transfers between devices: 70.4 us -> 75.3 us
  starting transfers between devices: 72.3 us -> 67.5 us
    ppermute x5 -> x0, starting transfers between devices: 33.3 us -> none  [along_path(): lax.ppermute(value, axes, lanes([(a, (a + distance) % places) for a in ra...]
    ppermute x2 -> x7, starting transfers between devices: 7.04 us -> 37.2 us  [along_z(): return lax.ppermute(value, axes, lanes(pairs))]
    ppermute x2 -> x7, waiting for transfers between devices: 41.4 us -> 61.2 us  [along_z(): return lax.ppermute(value, axes, lanes(pairs))]
    ppermute x5 -> x0, waiting for transfers between devices: 17.4 us -> none  [along_path(): lax.ppermute(value, axes, lanes([(a, (a + distance) % places) for a in ra...]
    ppermute x3, starting transfers between devices: 12.7 us -> 10.9 us  [to_end(): return lax.ppermute(value, axes, lanes(pairs))]
  transfers between devices with their start and end apart: 14 -> 14, of which waited for: 8 -> 9; matrix products, arithmetic and copies ran while one was open for 1% -> 1% of each run, Pallas kernels for 4% -> 4%
where the time goes in v4:
time: 169 us; the launch traced here: 168 us
  waiting for transfers between devices  75.3 us (45%)
  starting transfers between devices  67.5 us (40%)
  Pallas kernels  19.1 us (11%)
  local copies, waits for them, and re-layouts  5.15 us (3%)
    ppermute x7, waiting for transfers between devices, along_z(): return lax.ppermute(value, axes, lanes(pairs))  61.2 us
    ppermute x7, starting transfers between devices, along_z(): return lax.ppermute(value, axes, lanes(pairs))  37.2 us
    all_to_all x4, starting transfers between devices, exchange(): return lax.all_to_all(value, group, split_axis=0, concat_axis=0, tiled=True)  19.3 us
    ppermute x3, starting transfers between devices, to_end(): return lax.ppermute(value, axes, lanes(pairs))  10.9 us
    ppermute x3, waiting for transfers between devices, to_end(): return lax.ppermute(value, axes, lanes(pairs))  7.7 us
    all_to_all x4, waiting for transfers between devices, exchange(): return lax.all_to_all(value, group, split_axis=0, concat_axis=0, tiled=True)  6.49 us
    pallas_call x1, Pallas kernels, serve(): pl.pallas_call(serve_kernel, grid=(hidden_width // step,), out_shape=sds(...  5.83 us
    unnamed x26, local copies, waits for them, and re-layouts  3.61 us
  transfers between devices with their start and end apart: 14, of which 9 were waited for; matrix products, arithmetic and copies ran while one was open for 1% of the time, Pallas kernels for 4%

profile of v4, /device:TPU:10, one launch (start us, length us, event | category | flops | bytes accessed | tf_op | source)
XLA Modules:
  0.0 167.9 jit_solution(2522405297761175271)
XLA Ops:
  0.6 3.1 %shard_map.103 = (bf16[128,3584]{1,0:T(8,128)(2,1)}, bf16[72,3584]{1,0:T(8,128)(2,1)}, bf16[64,3584]{1,0:T(8,128)(2,1)}, s32[8,128]{1,0:T(8,128)}) custom-call(s32[1,128]{1,0:T(1,128)} %chosen_ref.3, s32[1,128]{1,0:T(1,128)} %places_ref.1, s32[32,32]{1,0:T(8,128)} %bitcast.38, bf16[128,3584]{1,0:T(8,128)(2,1)} %bitcast.35), custom_call_target="tpu_custom_call" | custom-call | tf_op jit(solution)/shard_map/pallas_call | solution.py:192
  3.7 4.8 %all-to-all-start = ((bf16[8,2,8,3584]{3,2,1,0:T(8,128)(2,1)}), bf16[8,2,8,3584]{3,2,1,0:T(8,128)(2,1)S(1)}, u32[]{:S(2)}, u32[]{:S(2)}) async-start(bf16[8,2,8,3584]{3,2,1,0:T(8,128)(2,1)} %bitcast.34), calls=%async_computation | async-start | bytes 1835008 | tf_op jit(solution)/shard_map/all_to_all | solution.py:173
  8.6 18.2 %collective-permute-start.1 = (bf16[72,3584]{1,0:T(8,128)(2,1)}, bf16[72,3584]{1,0:T(8,128)(2,1)S(1)}, u32[]{:S(2)}, u32[]{:S(2)}) collective-permute-start(bf16[72,3584]{1,0:T(8,128)(2,1)} %get-tuple-element.12), channel_id=1, source_target_pairs={{0,120},{1,121},{2,122},{3,123},{4,124},{5,125},{6,126},{7,127},{8... | collective-permute-start | bytes 1548296 | tf_op jit(solution)/shard_map/ppermute | solution.py:161
  26.8 2.5 %collective-permute-start.2 = (bf16[64,3584]{1,0:T(8,128)(2,1)}, bf16[64,3584]{1,0:T(8,128)(2,1)S(1)}, u32[]{:S(2)}, u32[]{:S(2)}) collective-permute-start(bf16[64,3584]{1,0:T(8,128)(2,1)} %get-tuple-element.13), channel_id=1, source_target_pairs={{0,120},{1,121},{2,122},{3,123},{4,124},{5,125},{6,126},{7,127},{8... | collective-permute-start | bytes 1376264 | tf_op jit(solution)/shard_map/ppermute | solution.py:161
  29.2 10.0 %collective-permute-done.1.early_ref = bf16[72,3584]{1,0:T(8,128)(2,1)S(1)} collective-permute-done((bf16[72,3584]{1,0:T(8,128)(2,1)}, bf16[72,3584]{1,0:T(8,128)(2,1)S(1)}, u32[]{:S(2)}, u32[]{:S(2)}) %collective-permute-start.1) | collective-permute-done | bytes 516128 | tf_op jit(solution)/shard_map/ppermute | solution.py:161
  39.2 0.0 copy-start.4
  39.2 5.5 %collective-permute-start.3 = (bf16[72,3584]{1,0:T(8,128)(2,1)S(1)}, bf16[72,3584]{1,0:T(8,128)(2,1)S(1)}, u32[]{:S(2)}, u32[]{:S(2)}) collective-permute-start(bf16[72,3584]{1,0:T(8,128)(2,1)S(1)} %collective-permute-done.1.early_ref), channel_id=1, source_target_pairs={{0,120},{1,121},{2,122},{3,123},{4,124},{5,125},{6,126},{7,127},{8... | collective-permute-start | bytes 1548296 | tf_op jit(solution)/shard_map/ppermute | solution.py:161
  44.7 4.3 %collective-permute-done.2.late_ref = bf16[64,3584]{1,0:T(8,128)(2,1)S(1)} collective-permute-done((bf16[64,3584]{1,0:T(8,128)(2,1)}, bf16[64,3584]{1,0:T(8,128)(2,1)S(1)}, u32[]{:S(2)}, u32[]{:S(2)}) %collective-permute-start.2) | collective-permute-done | bytes 458784 | tf_op jit(solution)/shard_map/ppermute | solution.py:161
  49.0 0.0 copy-done.4
  49.0 0.0 copy-start.6
  49.0 0.8 copy-done.6
  49.8 2.4 %shard_map.104 = bf16[64,3584]{1,0:T(8,128)(2,1)} custom-call(bf16[72,3584]{1,0:T(8,128)(2,1)} %copy-done.4, bf16[64,3584]{1,0:T(8,128)(2,1)} %copy-done.6), custom_call_target="tpu_custom_call" | custom-call | tf_op jit(solution)/shard_map/pallas_call | solution.py:204
  52.2 0.0 all-to-all-done
  52.2 4.8 %all-to-all-start.1 = ((bf16[8,8,3584]{2,1,0:T(8,128)(2,1)}), bf16[8,8,3584]{2,1,0:T(8,128)(2,1)S(1)}, u32[]{:S(2)}, u32[]{:S(2)}) async-start(bf16[8,8,3584]{2,1,0:T(8,128)(2,1)} %bitcast.30), calls=%async_computation.1 | async-start | bytes 917504 | tf_op jit(solution)/shard_map/all_to_all | solution.py:173
  57.0 0.0 copy-start.7
  57.0 0.8 slice_bitcast_fusion
  57.9 1.9 %collective-permute-start = (bf16[64,3584]{1,0:T(8,128)(2,1)S(1)}, bf16[64,3584]{1,0:T(8,128)(2,1)}, u32[]{:S(2)}, u32[]{:S(2)}) collective-permute-start(bf16[64,3584]{1,0:T(8,128)(2,1)S(1)} %get-tuple-element.17), channel_id=1, source_target_pairs={{0,8},{1,9},{2,10},{3,11},{4,12},{5,13},{6,14},{7,15},{8,16},{9,17... | collective-permute-start | bytes 1376264 | tf_op jit(solution)/shard_map/ppermute | solution.py:161
  59.8 0.0 collective-permute-done.3.early_ref
  59.8 0.0 copy-start.2
  59.8 0.8 copy-done.2
  60.6 2.1 %shard_map.105 = bf16[64,3584]{1,0:T(8,128)(2,1)} custom-call(bf16[72,3584]{1,0:T(8,128)(2,1)} %copy-done.2), custom_call_target="tpu_custom_call" | custom-call | tf_op jit(solution)/shard_map/pallas_call | solution.py:209
  62.7 0.0 copy-start.3
  62.7 2.5 %all-to-all-done.1 = bf16[8,8,3584]{2,1,0:T(8,128)(2,1)S(1)} async-done(((bf16[8,8,3584]{2,1,0:T(8,128)(2,1)}), bf16[8,8,3584]{2,1,0:T(8,128)(2,1)S(1)}, u32[]{:S(2)}, u32[]{:S(2)}) %all-to-all-start.1) | async-done | bytes 458784 | tf_op jit(solution)/shard_map/all_to_all | solution.py:173
  65.2 0.0 copy-start
  65.2 4.8 %all-to-all-start.2 = ((bf16[8,8,3584]{2,1,0:T(8,128)(2,1)}), bf16[8,8,3584]{2,1,0:T(8,128)(2,1)S(1)}, u32[]{:S(2)}, u32[]{:S(2)}) async-start(bf16[8,8,3584]{2,1,0:T(8,128)(2,1)} %bitcast.31), calls=%async_computation.2 | async-start | bytes 917504 | tf_op jit(solution)/shard_map/all_to_all | solution.py:173
  70.0 4.2 %collective-permute-done.r1_ref = bf16[64,3584]{1,0:T(8,128)(2,1)} collective-permute-done((bf16[64,3584]{1,0:T(8,128)(2,1)S(1)}, bf16[64,3584]{1,0:T(8,128)(2,1)}, u32[]{:S(2)}, u32[]{:S(2)}) %collective-permute-start) | collective-permute-done | bytes 458784 | tf_op jit(solution)/shard_map/ppermute | solution.py:161
  74.3 4.0 %all-to-all-done.2 = bf16[8,8,3584]{2,1,0:T(8,128)(2,1)S(1)} async-done(((bf16[8,8,3584]{2,1,0:T(8,128)(2,1)}), bf16[8,8,3584]{2,1,0:T(8,128)(2,1)S(1)}, u32[]{:S(2)}, u32[]{:S(2)}) %all-to-all-start.2) | async-done | bytes 458784 | tf_op jit(solution)/shard_map/all_to_all | solution.py:173
  78.2 0.0 copy-start.1
  78.2 0.0 copy-done
  78.2 0.8 copy-done.1
  79.0 5.8 %shard_map.106 = bf16[8,4,8,1024]{3,2,1,0:T(8,128)(2,1)} custom-call(bf16[64,3584]{1,0:T(8,128)(2,1)} %get-tuple-element.18.r0_ref, bf16[64,3584]{1,0:T(8,128)(2,1)} %collective-permute-done.r1_ref, bf16[64,3584]{1,0:T(8,128)(2,1)} %bitcast.32, bf16[64,3584]{1,0:T(8,128)(2,1)} %bitcast.33, bf16[1024,3584]{1,0:T(8,128)(2,1)} %bitcast.29), custom_call_target="tpu_custom_call" | custom-call | tf_op jit(solution)/shard_map/pallas_call | solution.py:180
  84.8 4.9 %all-to-all-start.3 = ((bf16[8,4,8,1024]{3,2,1,0:T(8,128)(2,1)}), bf16[8,4,8,1024]{3,2,1,0:T(8,128)(2,1)S(1)}, u32[]{:S(2)}, u32[]{:S(2)}) async-start(bf16[8,4,8,1024]{3,2,1,0:T(8,128)(2,1)} %shard_map.106), calls=%async_computation.3 | async-start | bytes 1048576 | tf_op jit(solution)/shard_map/all_to_all | solution.py:173
  89.7 0.0 copy-done.3
  89.7 4.4 %collective-permute-start.7 = (bf16[72,3584]{1,0:T(8,128)(2,1)S(1)}, bf16[72,3584]{1,0:T(8,128)(2,1)S(1)}, u32[]{:S(2)}, u32[]{:S(2)}) collective-permute-start(bf16[72,3584]{1,0:T(8,128)(2,1)S(1)} %copy-done.3), channel_id=1, source_target_pairs={{16,0},{17,1},{18,2},{19,3},{20,4},{21,5},{22,6},{23,7},{24,8},{25... | collective-permute-start | bytes 1548296 | tf_op jit(solution)/shard_map/ppermute | solution.py:170
  94.1 0.0 copy-done.7
  94.1 4.6 %collective-permute-start.8 = (bf16[64,3584]{1,0:T(8,128)(2,1)S(1)}, bf16[64,3584]{1,0:T(8,128)(2,1)S(1)}, u32[]{:S(2)}, u32[]{:S(2)}) collective-permute-start(bf16[64,3584]{1,0:T(8,128)(2,1)S(1)} %copy-done.7), channel_id=1, source_target_pairs={{24,0},{25,1},{26,2},{27,3},{28,4},{29,5},{30,6},{31,7},{32,8},{33... | collective-permute-start | bytes 1376264 | tf_op jit(solution)/shard_map/ppermute | solution.py:170
  98.7 0.0 all-to-all-done.3
  98.7 0.7 slice_bitcast_fusion.2
  99.4 1.9 %collective-permute-start.6 = (bf16[64,1024]{1,0:T(8,128)(2,1)S(1)}, bf16[64,1024]{1,0:T(8,128)(2,1)S(1)}, u32[]{:S(2)}, u32[]{:S(2)}) collective-permute-start(bf16[64,1024]{1,0:T(8,128)(2,1)S(1)} %get-tuple-element.19), channel_id=1, source_target_pairs={{0,8},{1,9},{2,10},{3,11},{4,12},{5,13},{6,14},{7,15},{8,16},{9,17... | collective-permute-start | bytes 393224 | tf_op jit(solution)/shard_map/ppermute | solution.py:161
  101.3 3.6 %collective-permute-start.5 = (bf16[64,1024]{1,0:T(8,128)(2,1)S(1)}, bf16[64,1024]{1,0:T(8,128)(2,1)S(1)}, u32[]{:S(2)}, u32[]{:S(2)}) collective-permute-start(bf16[64,1024]{1,0:T(8,128)(2,1)S(1)} %get-tuple-element.20), channel_id=1, source_target_pairs={{0,16},{1,17},{2,18},{3,19},{4,20},{5,21},{6,22},{7,23},{8,24},{9,... | collective-permute-start | bytes 393224 | tf_op jit(solution)/shard_map/ppermute | solution.py:161
  104.9 3.7 %collective-permute-start.4 = (bf16[64,1024]{1,0:T(8,128)(2,1)S(1)}, bf16[64,1024]{1,0:T(8,128)(2,1)S(1)}, u32[]{:S(2)}, u32[]{:S(2)}) collective-permute-start(bf16[64,1024]{1,0:T(8,128)(2,1)S(1)} %get-tuple-element.21), channel_id=1, source_target_pairs={{0,120},{1,121},{2,122},{3,123},{4,124},{5,125},{6,126},{7,127},{8... | collective-permute-start | bytes 393224 | tf_op jit(solution)/shard_map/ppermute | solution.py:161
  108.6 0.7 collective-permute-done.6.r3_ref
  109.3 0.0 copy-start.9
  109.3 5.4 %collective-permute-done.5.r2_ref = bf16[64,1024]{1,0:T(8,128)(2,1)S(1)} collective-permute-done((bf16[64,1024]{1,0:T(8,128)(2,1)S(1)}, bf16[64,1024]{1,0:T(8,128)(2,1)S(1)}, u32[]{:S(2)}, u32[]{:S(2)}) %collective-permute-start.5) | collective-permute-done | bytes 131104 | tf_op jit(solution)/shard_map/ppermute | solution.py:161
  114.8 0.0 copy-start.10
  114.8 36.5 %collective-permute-done.4.r1_ref = bf16[64,1024]{1,0:T(8,128)(2,1)S(1)} collective-permute-done((bf16[64,1024]{1,0:T(8,128)(2,1)S(1)}, bf16[64,1024]{1,0:T(8,128)(2,1)S(1)}, u32[]{:S(2)}, u32[]{:S(2)}) %collective-permute-start.4) | collective-permute-done | bytes 131104 | tf_op jit(solution)/shard_map/ppermute | solution.py:161
  151.3 0.0 copy-start.11
  151.3 0.0 copy-done.9
  151.3 0.0 copy-done.10
  151.3 0.6 copy-done.11
  151.9 2.5 %shard_map.107 = (bf16[128,1024]{1,0:T(8,128)(2,1)}, f32[32,128]{1,0:T(8,128)}, bf16[32,128]{1,0:T(8,128)(2,1)}) custom-call(s32[8,128]{1,0:T(8,128)} %get-tuple-element.10.meta_ref, s32[1,128]{1,0:T(1,128)} %chosen_ref.3, f32[32,128]{1,0:T(8,128)} %bitcast.39, bf16[128,1024]{1,0:T(8,128)(2,1)} %bitcast.37, bf16[64,1024]{1,0:T(8,128)(2,1)} %get-tuple-element.22.r0_ref, ...), custom_call_target="tpu_custom_call" | custom-call | tf_op jit(solution)/shard_map/pallas_call | solution.py:220
  154.4 1.9 %collective-permute-start.9 = (bf16[32,128]{1,0:T(8,128)(2,1)}, bf16[32,128]{1,0:T(8,128)(2,1)S(1)}, u32[]{:S(2)}, u32[]{:S(2)}) collective-permute-start(bf16[32,128]{1,0:T(8,128)(2,1)} %get-tuple-element.16), channel_id=1, source_target_pairs={{32,0},{33,1},{34,2},{35,3},{36,4},{37,5},{38,6},{39,7},{40,8},{41... | collective-permute-start | bytes 24584 | tf_op jit(solution)/shard_map/ppermute | solution.py:170
  156.4 0.0 collective-permute-done.8.late_ref
  156.4 0.0 copy-start.8
  156.4 0.0 collective-permute-done.7.early_ref
  156.4 0.0 copy-start.5
  156.4 7.7 %collective-permute-done.9.score_ref = bf16[32,128]{1,0:T(8,128)(2,1)S(1)} collective-permute-done((bf16[32,128]{1,0:T(8,128)(2,1)}, bf16[32,128]{1,0:T(8,128)(2,1)S(1)}, u32[]{:S(2)}, u32[]{:S(2)}) %collective-permute-start.9) | collective-permute-done | bytes 8224 | tf_op jit(solution)/shard_map/ppermute | solution.py:170
  164.1 0.0 copy-done.8
  164.1 0.0 copy-done.5
  164.1 0.0 copy-start.12
  164.1 0.6 copy-done.12
  164.7 3.2 %shard_map.108 = bf16[128,3584]{1,0:T(8,128)(2,1)} custom-call(bf16[72,3584]{1,0:T(8,128)(2,1)} %copy-done.5, bf16[64,3584]{1,0:T(8,128)(2,1)} %copy-done.8, bf16[32,128]{1,0:T(8,128)(2,1)} %copy-done.12, bf16[32,3584]{1,0:T(8,128)(2,1)} %router_ref.1), custom_call_target="tpu_custom_call" | custom-call | tf_op jit(solution)/shard_map/pallas_call | solution.py:227
Async XLA Ops:
  3.7 48.5 %all-to-all-start = ((bf16[8,2,8,3584]{3,2,1,0:T(8,128)(2,1)}), bf16[8,2,8,3584]{3,2,1,0:T(8,128)(2,1)S(1)}, u32[]{:S(2)}, u32[]{:S(2)}) async-start(bf16[8,2,8,3584]{3,2,1,0:T(8,128)(2,1)} %bitcast.34), calls=%async_computation | async-start | bytes 1835008 | tf_op jit(solution)/shard_map/all_to_all | solution.py:173
  8.6 30.6 %collective-permute-start.1 = (bf16[72,3584]{1,0:T(8,128)(2,1)}, bf16[72,3584]{1,0:T(8,128)(2,1)S(1)}, u32[]{:S(2)}, u32[]{:S(2)}) collective-permute-start(bf16[72,3584]{1,0:T(8,128)(2,1)} %get-tuple-element.12), channel_id=1, source_target_pairs={{0,120},{1,121},{2,122},{3,123},{4,124},{5,125},{6,126},{7,127},{8... | collective-permute-start | bytes 1548296 | tf_op jit(solution)/shard_map/ppermute | solution.py:161
  26.8 22.3 %collective-permute-start.2 = (bf16[64,3584]{1,0:T(8,128)(2,1)}, bf16[64,3584]{1,0:T(8,128)(2,1)S(1)}, u32[]{:S(2)}, u32[]{:S(2)}) collective-permute-start(bf16[64,3584]{1,0:T(8,128)(2,1)} %get-tuple-element.13), channel_id=1, source_target_pairs={{0,120},{1,121},{2,122},{3,123},{4,124},{5,125},{6,126},{7,127},{8... | collective-permute-start | bytes 1376264 | tf_op jit(solution)/shard_map/ppermute | solution.py:161
  39.2 9.8 %copy-start.4 = (bf16[72,3584]{1,0:T(8,128)(2,1)}, bf16[72,3584]{1,0:T(8,128)(2,1)S(1)}, u32[]{:S(2)}) copy-start(bf16[72,3584]{1,0:T(8,128)(2,1)S(1)} %collective-permute-done.1.early_ref) | copy-start | bytes 1548292
  39.2 20.6 %collective-permute-start.3 = (bf16[72,3584]{1,0:T(8,128)(2,1)S(1)}, bf16[72,3584]{1,0:T(8,128)(2,1)S(1)}, u32[]{:S(2)}, u32[]{:S(2)}) collective-permute-start(bf16[72,3584]{1,0:T(8,128)(2,1)S(1)} %collective-permute-done.1.early_ref), channel_id=1, source_target_pairs={{0,120},{1,121},{2,122},{3,123},{4,124},{5,125},{6,126},{7,127},{8... | collective-permute-start | bytes 1548296 | tf_op jit(solution)/shard_map/ppermute | solution.py:161
  49.0 0.8 copy-start.6
  52.2 13.0 %all-to-all-start.1 = ((bf16[8,8,3584]{2,1,0:T(8,128)(2,1)}), bf16[8,8,3584]{2,1,0:T(8,128)(2,1)S(1)}, u32[]{:S(2)}, u32[]{:S(2)}) async-start(bf16[8,8,3584]{2,1,0:T(8,128)(2,1)} %bitcast.30), calls=%async_computation.1 | async-start | bytes 917504 | tf_op jit(solution)/shard_map/all_to_all | solution.py:173
  57.0 37.1 %copy-start.7 = (bf16[64,3584]{1,0:T(8,128)(2,1)S(1)}, bf16[64,3584]{1,0:T(8,128)(2,1)}, u32[]{:S(2)}) copy-start(bf16[64,3584]{1,0:T(8,128)(2,1)} %copy-done.6) | copy-start | bytes 1376260
  57.9 16.4 %collective-permute-start = (bf16[64,3584]{1,0:T(8,128)(2,1)S(1)}, bf16[64,3584]{1,0:T(8,128)(2,1)}, u32[]{:S(2)}, u32[]{:S(2)}) collective-permute-start(bf16[64,3584]{1,0:T(8,128)(2,1)S(1)} %get-tuple-element.17), channel_id=1, source_target_pairs={{0,8},{1,9},{2,10},{3,11},{4,12},{5,13},{6,14},{7,15},{8,16},{9,17... | collective-permute-start | bytes 1376264 | tf_op jit(solution)/shard_map/ppermute | solution.py:161
  59.8 0.8 copy-start.2
  62.7 27.0 %copy-start.3 = (bf16[72,3584]{1,0:T(8,128)(2,1)S(1)}, bf16[72,3584]{1,0:T(8,128)(2,1)}, u32[]{:S(2)}) copy-start(bf16[72,3584]{1,0:T(8,128)(2,1)} %copy-done.2) | copy-start | bytes 1548292
  65.2 13.0 %copy-start = (bf16[8,8,3584]{2,1,0:T(8,128)(2,1)}, bf16[8,8,3584]{2,1,0:T(8,128)(2,1)S(1)}, u32[]{:S(2)}) copy-start(bf16[8,8,3584]{2,1,0:T(8,128)(2,1)S(1)} %all-to-all-done.1) | copy-start | bytes 1376260
  65.2 13.0 %all-to-all-start.2 = ((bf16[8,8,3584]{2,1,0:T(8,128)(2,1)}), bf16[8,8,3584]{2,1,0:T(8,128)(2,1)S(1)}, u32[]{:S(2)}, u32[]{:S(2)}) async-start(bf16[8,8,3584]{2,1,0:T(8,128)(2,1)} %bitcast.31), calls=%async_computation.2 | async-start | bytes 917504 | tf_op jit(solution)/shard_map/all_to_all | solution.py:173
  78.2 0.8 copy-start.1
  84.8 13.9 %all-to-all-start.3 = ((bf16[8,4,8,1024]{3,2,1,0:T(8,128)(2,1)}), bf16[8,4,8,1024]{3,2,1,0:T(8,128)(2,1)S(1)}, u32[]{:S(2)}, u32[]{:S(2)}) async-start(bf16[8,4,8,1024]{3,2,1,0:T(8,128)(2,1)} %shard_map.106), calls=%async_computation.3 | async-start | bytes 1048576 | tf_op jit(solution)/shard_map/all_to_all | solution.py:173
  89.7 66.7 %collective-permute-start.7 = (bf16[72,3584]{1,0:T(8,128)(2,1)S(1)}, bf16[72,3584]{1,0:T(8,128)(2,1)S(1)}, u32[]{:S(2)}, u32[]{:S(2)}) collective-permute-start(bf16[72,3584]{1,0:T(8,128)(2,1)S(1)} %copy-done.3), channel_id=1, source_target_pairs={{16,0},{17,1},{18,2},{19,3},{20,4},{21,5},{22,6},{23,7},{24,8},{25... | collective-permute-start | bytes 1548296 | tf_op jit(solution)/shard_map/ppermute | solution.py:170
  94.1 62.3 %collective-permute-start.8 = (bf16[64,3584]{1,0:T(8,128)(2,1)S(1)}, bf16[64,3584]{1,0:T(8,128)(2,1)S(1)}, u32[]{:S(2)}, u32[]{:S(2)}) collective-permute-start(bf16[64,3584]{1,0:T(8,128)(2,1)S(1)} %copy-done.7), channel_id=1, source_target_pairs={{24,0},{25,1},{26,2},{27,3},{28,4},{29,5},{30,6},{31,7},{32,8},{33... | collective-permute-start | bytes 1376264 | tf_op jit(solution)/shard_map/ppermute | solution.py:170
  99.4 9.9 %collective-permute-start.6 = (bf16[64,1024]{1,0:T(8,128)(2,1)S(1)}, bf16[64,1024]{1,0:T(8,128)(2,1)S(1)}, u32[]{:S(2)}, u32[]{:S(2)}) collective-permute-start(bf16[64,1024]{1,0:T(8,128)(2,1)S(1)} %get-tuple-element.19), channel_id=1, source_target_pairs={{0,8},{1,9},{2,10},{3,11},{4,12},{5,13},{6,14},{7,15},{8,16},{9,17... | collective-permute-start | bytes 393224 | tf_op jit(solution)/shard_map/ppermute | solution.py:161
  101.3 13.4 %collective-permute-start.5 = (bf16[64,1024]{1,0:T(8,128)(2,1)S(1)}, bf16[64,1024]{1,0:T(8,128)(2,1)S(1)}, u32[]{:S(2)}, u32[]{:S(2)}) collective-permute-start(bf16[64,1024]{1,0:T(8,128)(2,1)S(1)} %get-tuple-element.20), channel_id=1, source_target_pairs={{0,16},{1,17},{2,18},{3,19},{4,20},{5,21},{6,22},{7,23},{8,24},{9,... | collective-permute-start | bytes 393224 | tf_op jit(solution)/shard_map/ppermute | solution.py:161
  104.9 46.3 %collective-permute-start.4 = (bf16[64,1024]{1,0:T(8,128)(2,1)S(1)}, bf16[64,1024]{1,0:T(8,128)(2,1)S(1)}, u32[]{:S(2)}, u32[]{:S(2)}) collective-permute-start(bf16[64,1024]{1,0:T(8,128)(2,1)S(1)} %get-tuple-element.21), channel_id=1, source_target_pairs={{0,120},{1,121},{2,122},{3,123},{4,124},{5,125},{6,126},{7,127},{8... | collective-permute-start | bytes 393224 | tf_op jit(solution)/shard_map/ppermute | solution.py:161
  109.3 41.9 %copy-start.9 = (bf16[64,1024]{1,0:T(8,128)(2,1)}, bf16[64,1024]{1,0:T(8,128)(2,1)S(1)}, u32[]{:S(2)}) copy-start(bf16[64,1024]{1,0:T(8,128)(2,1)S(1)} %collective-permute-done.6.r3_ref) | copy-start | bytes 393220
  114.8 36.5 %copy-start.10 = (bf16[64,1024]{1,0:T(8,128)(2,1)}, bf16[64,1024]{1,0:T(8,128)(2,1)S(1)}, u32[]{:S(2)}) copy-start(bf16[64,1024]{1,0:T(8,128)(2,1)S(1)} %collective-permute-done.5.r2_ref) | copy-start | bytes 393220
  151.3 0.6 copy-start.11
  154.4 9.7 %collective-permute-start.9 = (bf16[32,128]{1,0:T(8,128)(2,1)}, bf16[32,128]{1,0:T(8,128)(2,1)S(1)}, u32[]{:S(2)}, u32[]{:S(2)}) collective-permute-start(bf16[32,128]{1,0:T(8,128)(2,1)} %get-tuple-element.16), channel_id=1, source_target_pairs={{32,0},{33,1},{34,2},{35,3},{36,4},{37,5},{38,6},{39,7},{40,8},{41... | collective-permute-start | bytes 24584 | tf_op jit(solution)/shard_map/ppermute | solution.py:170
  156.4 7.7 %copy-start.8 = (bf16[64,3584]{1,0:T(8,128)(2,1)}, bf16[64,3584]{1,0:T(8,128)(2,1)S(1)}, u32[]{:S(2)}) copy-start(bf16[64,3584]{1,0:T(8,128)(2,1)S(1)} %collective-permute-done.8.late_ref) | copy-start | bytes 1376260
  156.4 7.7 %copy-start.5 = (bf16[72,3584]{1,0:T(8,128)(2,1)}, bf16[72,3584]{1,0:T(8,128)(2,1)S(1)}, u32[]{:S(2)}) copy-start(bf16[72,3584]{1,0:T(8,128)(2,1)S(1)} %collective-permute-done.7.early_ref) | copy-start | bytes 1548292
  164.1 0.6 copy-start.12

commit v5 on v4

--- a/solution.py
+++ b/solution.py
@@ -8,6 +8,7 @@
 
 route_scale = 2.5
 slots = 8
+bf16 = jnp.bfloat16
 axes = ("y", "zh", "zl", "x", "c")
 group = ("x", "c")
 expert_axes = ("zl", "x", "c")
@@ -88,19 +89,22 @@
     out_ref[...] = jnp.dot(pick[:, :half], early_ref[:half], preferred_element_type=jnp.float32).astype(jnp.bfloat16)
 
 
-def serve_kernel(r0_ref, r1_ref, r2_ref, r3_ref, weight_ref, out_ref, held_ref):
+def serve_kernel(r0_ref, r1_ref, r2_ref, r3_ref, weight_ref, out_ref, held_ref, fetched_ref, sems):
     rows = r0_ref.shape[0]
-    step = weight_ref.shape[0]
-
-    @pl.when(pl.program_id(0) == 0)
-    def _():
-        for k, ref in enumerate((r0_ref, r1_ref, r2_ref, r3_ref)):
-            held_ref[k * rows:(k + 1) * rows] = ref[...]
-
-    found = lax.dot_general(weight_ref[...], held_ref[...], NT, preferred_element_type=jnp.float32).T
-    for k in range(4):
-        part = found[k * rows:(k + 1) * rows].reshape(rows // slots, slots, step)
-        out_ref[:, k] = part.astype(jnp.bfloat16)
+    count = sems.shape[0]
+    step = weight_ref.shape[0] // count
+    blocks = [pl.ds(j * step, step) for j in range(count)]
+    fetches = [pltpu.make_async_copy(weight_ref.at[blocks[j]], fetched_ref.at[blocks[j]], sems.at[j]) for j in range(count)]
+    for fetch in fetches:
+        fetch.start()
+    for k, ref in enumerate((r0_ref, r1_ref, r2_ref, r3_ref)):
+        held_ref[k * rows:(k + 1) * rows] = ref[...]
+    for fetch, block in zip(fetches, blocks):
+        fetch.wait()
+        found = lax.dot_general(fetched_ref[block, :], held_ref[...], NT, preferred_element_type=jnp.float32).T
+        for k in range(4):
+            part = found[k * rows:(k + 1) * rows].reshape(rows // slots, slots, step)
+            out_ref[:, k, :, block] = part.astype(jnp.bfloat16)
 
 
 def back_kernel(meta_ref, chosen_ref, scores_ref, hidden_ref, r0_ref, r1_ref, r2_ref, r3_ref, act_ref, score_ref, score_bf_ref):
@@ -136,12 +140,17 @@
     out_ref[...] = out.astype(jnp.bfloat16)
 
 
-def whole(count):
-    return [pl.BlockSpec(memory_space=pltpu.VMEM)] * count
-
-
-def sds(shape, dtype=jnp.bfloat16):
-    return jax.ShapeDtypeStruct(shape, dtype)
+def call(kernel, outs, *operands, scratch=()):
+    space = {"held": pltpu.VMEM, "near": pltpu.HBM, "far": pltpu.HBM}
+    values = [pltpu.with_memory_space_constraint(x, space[how]) for how, x in operands]
+    return pl.pallas_call(
+        kernel,
+        out_shape=tuple(space[how](shape, dtype) for how, shape, dtype in outs),
+        in_specs=[pl.BlockSpec(memory_space=pltpu.HBM if how == "far" else pltpu.VMEM) for how, _ in operands],
+        out_specs=tuple(pl.BlockSpec(memory_space=pltpu.VMEM) for _ in outs),
+        scratch_shapes=scratch,
+        compiler_params=pltpu.CompilerParams(vmem_limit_bytes=24 * 1024 * 1024),
+    )(*values)
 
 
 def on_device(dims, grad_out, hidden_act, scores, expert_ids, slot_ids, counts, down_weight, router):
@@ -176,39 +185,40 @@
         return exchange(value.reshape(nxc, slots, width)).reshape(rows, width)
 
     def serve(*values):
-        step = hidden_width // 2
-        return pl.pallas_call(
-            serve_kernel,
-            grid=(hidden_width // step,),
-            out_shape=sds((nxc, 4, slots, hidden_width)),
-            in_specs=[pl.BlockSpec((rows, width), lambda j: (0, 0))] * 4 + [pl.BlockSpec((step, width), lambda j: (j, 0))],
-            out_specs=pl.BlockSpec((nxc, 4, slots, step), lambda j: (0, 0, 0, j)),
-            scratch_shapes=[pltpu.VMEM((4 * rows, width), jnp.bfloat16)],
-        )(*values, weight)
+        scratch = [
+            pltpu.VMEM((4 * rows, width), bf16),
+            pltpu.VMEM((hidden_width, width), bf16),
+            pltpu.SemaphoreType.DMA((4,)),
+        ]
+        outs = [("held", (nxc, 4, slots, hidden_width), bf16)]
+        return call(serve_kernel, outs, *held(*values), ("far", weight), scratch=scratch)[0]
+
+    def held(*values):
+        return [("held", v) for v in values]
+
+    def near_by(*values):
+        return [("near", v) for v in values]
 
     def part(value, k):
         return value[:, k].reshape(rows, value.shape[3])
 
-    first, early, late, meta = pl.pallas_call(
-        prep_kernel,
-        out_shape=(sds((2 * rows, width)), sds((half + 8, width)), sds((half, width)), sds((8, tokens), jnp.int32)),
-        in_specs=whole(4),
-        out_specs=tuple(whole(4)),
-    )(expert_ids, slot_ids, counts[0], tok)
+    outs = [
+        ("held", (2 * rows, width), bf16),
+        ("held", (half + 8, width), bf16),
+        ("held", (half, width), bf16),
+        ("near", (8, tokens), jnp.int32),
+    ]
+    first, early, late, meta = call(prep_kernel, outs, *near_by(expert_ids, slot_ids, counts[0], tok))
     early1 = along_z(early, -1)
     first = exchange(first.reshape(nxc, 2, slots, width))
     late1 = along_z(late, -1)
     early2 = along_z(early1, -1)
     near, up = part(first, 0), part(first, 1)
     up = along_z(up, 1)
-    one = pl.pallas_call(
-        pack_one_kernel, out_shape=sds((rows, width)), in_specs=whole(2), out_specs=whole(1)[0]
-    )(early1, late1)
+    one = call(pack_one_kernel, [("held", (rows, width), bf16)], *held(early1, late1))[0]
     one = spread(one)
     late4 = to_end(late1, 3)
-    two = pl.pallas_call(
-        pack_two_kernel, out_shape=sds((rows, width)), in_specs=whole(1), out_specs=whole(1)[0]
-    )(early2)
+    two = call(pack_two_kernel, [("held", (rows, width), bf16)], *held(early2))[0]
     two = spread(two)
     early4 = to_end(early2, 2)
     served = serve(near, up, one, two)
@@ -217,16 +227,16 @@
     r2 = along_z(r2, 2)
     r1 = along_z(r1, -1)
     r3 = along_z(r3, 1)
-    act, score, score_bf = pl.pallas_call(
-        back_kernel,
-        out_shape=(sds((tokens, hidden_width)), sds((scores.shape[2], tokens), jnp.float32), sds((scores.shape[2], tokens))),
-        in_specs=whole(8),
-        out_specs=tuple(whole(3)),
-    )(meta, expert_ids, scores[0].T, hidden_act[0], r0, r1, r2, r3)
+    experts = scores.shape[2]
+    outs = [
+        ("near", (tokens, hidden_width), bf16),
+        ("near", (experts, tokens), jnp.float32),
+        ("held", (experts, tokens), bf16),
+    ]
+    ins = near_by(meta, expert_ids, scores[0].T, hidden_act[0]) + held(r0, r1, r2, r3)
+    act, score, score_bf = call(back_kernel, outs, *ins)
     late_score = to_end(score_bf, nzl)
-    upstream = pl.pallas_call(
-        up_kernel, out_shape=sds((tokens, width)), in_specs=whole(4), out_specs=whole(1)[0]
-    )(early4, late4, late_score, router)
+    upstream = call(up_kernel, [("near", (tokens, width), bf16)], *held(early4, late4, late_score, router))[0]
     return act[None], score.T[None], upstream[None]
 
 

time: 169 us -> 164 us (0.970)
  local copies, waits for them, and re-layouts: 5.15 us -> 2.02 us
  Pallas kernels: 19.1 us -> 16.7 us
    unnamed x26 -> x2, local copies, waits for them, and re-layouts: 3.61 us -> 0.01 us
    pallas_call x6, Pallas kernels: 19.1 us -> 16.7 us  [call(): pl.pallas_call(kernel, out_shape=tuple((space[how](shape, dtype) for how,...]
    ppermute x7, waiting for transfers between devices: 61.2 us -> 62.9 us  [along_z(): return lax.ppermute(value, axes, lanes(pairs))]
  transfers between devices with their start and end apart: 14 -> 14, of which waited for: 9 -> 10; matrix products, arithmetic and copies ran while one was open for 1% -> 1% of each run, Pallas kernels for 4% -> 3%
where the time goes in v5:
time: 164 us; the launch traced here: 163 us
  waiting for transfers between devices  75.9 us (46%)
  starting transfers between devices  67.8 us (41%)
  Pallas kernels  16.7 us (10%)
  local copies, waits for them, and re-layouts  2.02 us (1%)
    ppermute x7, waiting for transfers between devices, along_z(): return lax.ppermute(value, axes, lanes(pairs))  62.9 us
    ppermute x7, starting transfers between devices, along_z(): return lax.ppermute(value, axes, lanes(pairs))  37.5 us
    all_to_all x4, starting transfers between devices, exchange(): return lax.all_to_all(value, group, split_axis=0, concat_axis=0, tiled=True)  19.3 us
    pallas_call x6, Pallas kernels, call(): pl.pallas_call(kernel, out_shape=tuple((space[how](shape, dtype) for how,...  16.7 us
    ppermute x3, starting transfers between devices, to_end(): return lax.ppermute(value, axes, lanes(pairs))  11 us
    ppermute x3, waiting for transfers between devices, to_end(): return lax.ppermute(value, axes, lanes(pairs))  7.51 us
    all_to_all x4, waiting for transfers between devices, exchange(): return lax.all_to_all(value, group, split_axis=0, concat_axis=0, tiled=True)  5.46 us
  transfers between devices with their start and end apart: 14, of which 10 were waited for; matrix products, arithmetic and copies ran while one was open for 1% of the time, Pallas kernels for 3%

profile of v5, /device:TPU:10, one launch (start us, length us, event | category | flops | bytes accessed | tf_op | source)
XLA Modules:
  0.0 163.2 jit_solution(7849715741066253812)
XLA Ops:
  0.6 3.0 %shard_map.103 = (bf16[128,3584]{1,0:T(8,128)(2,1)}, bf16[72,3584]{1,0:T(8,128)(2,1)S(1)}, bf16[64,3584]{1,0:T(8,128)(2,1)S(1)}, s32[8,128]{1,0:T(8,128)}) custom-call(s32[1,128]{1,0:T(1,128)} %chosen_ref.3, s32[1,128]{1,0:T(1,128)} %places_ref.1, s32[32,32]{1,0:T(8,128)} %bitcast.35, bf16[128,3584]{1,0:T(8,128)(2,1)} %bitcast.32), custom_call_target="tpu_custom_call" | custom-call | tf_op jit(solution)/shard_map/pallas_call | solution.py:146
  3.7 4.8 %all-to-all-start = ((bf16[8,2,8,3584]{3,2,1,0:T(8,128)(2,1)}), bf16[8,2,8,3584]{3,2,1,0:T(8,128)(2,1)}, u32[]{:S(2)}, u32[]{:S(2)}) async-start(bf16[8,2,8,3584]{3,2,1,0:T(8,128)(2,1)} %bitcast.5), calls=%async_computation | async-start | bytes 1835008 | tf_op jit(solution)/shard_map/all_to_all | solution.py:182
  8.5 18.2 %collective-permute-start.1 = (bf16[72,3584]{1,0:T(8,128)(2,1)S(1)}, bf16[72,3584]{1,0:T(8,128)(2,1)S(1)}, u32[]{:S(2)}, u32[]{:S(2)}) collective-permute-start(bf16[72,3584]{1,0:T(8,128)(2,1)S(1)} %get-tuple-element.12), channel_id=1, source_target_pairs={{0,120},{1,121},{2,122},{3,123},{4,124},{5,125},{6,126},{7,127},{8... | collective-permute-start | bytes 1548296 | tf_op jit(solution)/shard_map/ppermute | solution.py:170
  26.7 2.5 %collective-permute-start.2 = (bf16[64,3584]{1,0:T(8,128)(2,1)S(1)}, bf16[64,3584]{1,0:T(8,128)(2,1)S(1)}, u32[]{:S(2)}, u32[]{:S(2)}) collective-permute-start(bf16[64,3584]{1,0:T(8,128)(2,1)S(1)} %get-tuple-element.13), channel_id=1, source_target_pairs={{0,120},{1,121},{2,122},{3,123},{4,124},{5,125},{6,126},{7,127},{8... | collective-permute-start | bytes 1376264 | tf_op jit(solution)/shard_map/ppermute | solution.py:170
  29.2 9.6 %collective-permute-done.1.early_ref = bf16[72,3584]{1,0:T(8,128)(2,1)S(1)} collective-permute-done((bf16[72,3584]{1,0:T(8,128)(2,1)S(1)}, bf16[72,3584]{1,0:T(8,128)(2,1)S(1)}, u32[]{:S(2)}, u32[]{:S(2)}) %collective-permute-start.1) | collective-permute-done | bytes 516128 | tf_op jit(solution)/shard_map/ppermute | solution.py:170
  38.8 5.6 %collective-permute-start.3 = (bf16[72,3584]{1,0:T(8,128)(2,1)S(1)}, bf16[72,3584]{1,0:T(8,128)(2,1)S(1)}, u32[]{:S(2)}, u32[]{:S(2)}) collective-permute-start(bf16[72,3584]{1,0:T(8,128)(2,1)S(1)} %collective-permute-done.1.early_ref), channel_id=1, source_target_pairs={{0,120},{1,121},{2,122},{3,123},{4,124},{5,125},{6,126},{7,127},{8... | collective-permute-start | bytes 1548296 | tf_op jit(solution)/shard_map/ppermute | solution.py:170
  44.4 4.2 %collective-permute-done.2.late_ref = bf16[64,3584]{1,0:T(8,128)(2,1)S(1)} collective-permute-done((bf16[64,3584]{1,0:T(8,128)(2,1)S(1)}, bf16[64,3584]{1,0:T(8,128)(2,1)S(1)}, u32[]{:S(2)}, u32[]{:S(2)}) %collective-permute-start.2) | collective-permute-done | bytes 458784 | tf_op jit(solution)/shard_map/ppermute | solution.py:170
  48.7 1.2 shard_map.104
  49.9 0.0 all-to-all-done
  49.9 4.8 %all-to-all-start.1 = ((bf16[8,8,3584]{2,1,0:T(8,128)(2,1)}), bf16[8,8,3584]{2,1,0:T(8,128)(2,1)S(1)}, u32[]{:S(2)}, u32[]{:S(2)}) async-start(bf16[8,8,3584]{2,1,0:T(8,128)(2,1)} %bitcast.8), calls=%async_computation.1 | async-start | bytes 917504 | tf_op jit(solution)/shard_map/all_to_all | solution.py:182
  54.7 2.0 %slice_bitcast_fusion = (bf16[64,3584]{1,0:T(8,128)(2,1)}, bf16[64,3584]{1,0:T(8,128)(2,1)S(1)}) fusion(bf16[8,2,8,3584]{3,2,1,0:T(8,128)(2,1)} %all-to-all-done), kind=kLoop, calls=%fused_computation | loop fusion | bytes 1835008 | tf_op jit(solution)/shard_map/reshape;squeeze | solution.py:203
  56.7 0.0 copy-start
  56.7 2.0 %collective-permute-start = (bf16[64,3584]{1,0:T(8,128)(2,1)}, bf16[64,3584]{1,0:T(8,128)(2,1)S(1)}, u32[]{:S(2)}, u32[]{:S(2)}) collective-permute-start(bf16[64,3584]{1,0:T(8,128)(2,1)} %get-tuple-element.17), channel_id=1, source_target_pairs={{0,8},{1,9},{2,10},{3,11},{4,12},{5,13},{6,14},{7,15},{8,16},{9,17... | collective-permute-start | bytes 1376264 | tf_op jit(solution)/shard_map/ppermute | solution.py:170
  58.7 0.1 collective-permute-done.3.early_ref
  58.9 1.0 shard_map.105
  59.9 3.0 %all-to-all-done.1 = bf16[8,8,3584]{2,1,0:T(8,128)(2,1)S(1)} async-done(((bf16[8,8,3584]{2,1,0:T(8,128)(2,1)}), bf16[8,8,3584]{2,1,0:T(8,128)(2,1)S(1)}, u32[]{:S(2)}, u32[]{:S(2)}) %all-to-all-start.1) | async-done | bytes 458784 | tf_op jit(solution)/shard_map/all_to_all | solution.py:182
  62.9 4.8 %all-to-all-start.2 = ((bf16[8,8,3584]{2,1,0:T(8,128)(2,1)}), bf16[8,8,3584]{2,1,0:T(8,128)(2,1)S(1)}, u32[]{:S(2)}, u32[]{:S(2)}) async-start(bf16[8,8,3584]{2,1,0:T(8,128)(2,1)} %bitcast.10), calls=%async_computation.2 | async-start | bytes 917504 | tf_op jit(solution)/shard_map/all_to_all | solution.py:182
  67.7 5.7 %collective-permute-done.r1_ref = bf16[64,3584]{1,0:T(8,128)(2,1)S(1)} collective-permute-done((bf16[64,3584]{1,0:T(8,128)(2,1)}, bf16[64,3584]{1,0:T(8,128)(2,1)S(1)}, u32[]{:S(2)}, u32[]{:S(2)}) %collective-permute-start) | collective-permute-done | bytes 458784 | tf_op jit(solution)/shard_map/ppermute | solution.py:170
  73.4 2.5 %all-to-all-done.2 = bf16[8,8,3584]{2,1,0:T(8,128)(2,1)S(1)} async-done(((bf16[8,8,3584]{2,1,0:T(8,128)(2,1)}), bf16[8,8,3584]{2,1,0:T(8,128)(2,1)S(1)}, u32[]{:S(2)}, u32[]{:S(2)}) %all-to-all-start.2) | async-done | bytes 458784 | tf_op jit(solution)/shard_map/all_to_all | solution.py:182
  75.9 7.1 %shard_map.106 = bf16[8,4,8,1024]{3,2,1,0:T(8,128)(2,1)} custom-call(bf16[64,3584]{1,0:T(8,128)(2,1)S(1)} %get-tuple-element.18.r0_ref, bf16[64,3584]{1,0:T(8,128)(2,1)S(1)} %collective-permute-done.r1_ref, bf16[64,3584]{1,0:T(8,128)(2,1)S(1)} %bitcast.29, bf16[64,3584]{1,0:T(8,128)(2,1)S(1)} %bitcast.30, bf16[1024,3584]{1,0:T(8,128)(2,1)} %bitcast.31), custom_call_target="tpu_custom_call" | custom-call | tf_op jit(solution)/shard_map/pallas_call | solution.py:146
  83.0 4.9 %all-to-all-start.3 = ((bf16[8,4,8,1024]{3,2,1,0:T(8,128)(2,1)}), bf16[8,4,8,1024]{3,2,1,0:T(8,128)(2,1)S(1)}, u32[]{:S(2)}, u32[]{:S(2)}) async-start(bf16[8,4,8,1024]{3,2,1,0:T(8,128)(2,1)} %shard_map.106), calls=%async_computation.3 | async-start | bytes 1048576 | tf_op jit(solution)/shard_map/all_to_all | solution.py:182
  87.9 4.3 %collective-permute-start.7 = (bf16[72,3584]{1,0:T(8,128)(2,1)S(1)}, bf16[72,3584]{1,0:T(8,128)(2,1)S(1)}, u32[]{:S(2)}, u32[]{:S(2)}) collective-permute-start(bf16[72,3584]{1,0:T(8,128)(2,1)S(1)} %collective-permute-done.3.early_ref), channel_id=1, source_target_pairs={{16,0},{17,1},{18,2},{19,3},{20,4},{21,5},{22,6},{23,7},{24,8},{25... | collective-permute-start | bytes 1548296 | tf_op jit(solution)/shard_map/ppermute | solution.py:179
  92.1 4.9 %collective-permute-start.8 = (bf16[64,3584]{1,0:T(8,128)(2,1)S(1)}, bf16[64,3584]{1,0:T(8,128)(2,1)S(1)}, u32[]{:S(2)}, u32[]{:S(2)}) collective-permute-start(bf16[64,3584]{1,0:T(8,128)(2,1)S(1)} %collective-permute-done.2.late_ref), channel_id=1, source_target_pairs={{24,0},{25,1},{26,2},{27,3},{28,4},{29,5},{30,6},{31,7},{32,8},{33... | collective-permute-start | bytes 1376264 | tf_op jit(solution)/shard_map/ppermute | solution.py:179
  97.0 0.0 all-to-all-done.3
  97.1 1.9 %collective-permute-start.6 = (bf16[64,1024]{1,0:T(8,128)(2,1)S(1)}, bf16[64,1024]{1,0:T(8,128)(2,1)S(1)}, u32[]{:S(2)}, u32[]{:S(2)}) collective-permute-start(bf16[64,1024]{1,0:T(8,128)(2,1)S(1)} %get-tuple-element.19), channel_id=1, source_target_pairs={{0,8},{1,9},{2,10},{3,11},{4,12},{5,13},{6,14},{7,15},{8,16},{9,17... | collective-permute-start | bytes 393224 | tf_op jit(solution)/shard_map/ppermute | solution.py:170
  99.0 3.3 %collective-permute-start.5 = (bf16[64,1024]{1,0:T(8,128)(2,1)S(1)}, bf16[64,1024]{1,0:T(8,128)(2,1)S(1)}, u32[]{:S(2)}, u32[]{:S(2)}) collective-permute-start(bf16[64,1024]{1,0:T(8,128)(2,1)S(1)} %get-tuple-element.20), channel_id=1, source_target_pairs={{0,16},{1,17},{2,18},{3,19},{4,20},{5,21},{6,22},{7,23},{8,24},{9,... | collective-permute-start | bytes 393224 | tf_op jit(solution)/shard_map/ppermute | solution.py:170
  102.3 3.9 %collective-permute-start.4 = (bf16[64,1024]{1,0:T(8,128)(2,1)S(1)}, bf16[64,1024]{1,0:T(8,128)(2,1)S(1)}, u32[]{:S(2)}, u32[]{:S(2)}) collective-permute-start(bf16[64,1024]{1,0:T(8,128)(2,1)S(1)} %get-tuple-element.21), channel_id=1, source_target_pairs={{0,120},{1,121},{2,122},{3,123},{4,124},{5,125},{6,126},{7,127},{8... | collective-permute-start | bytes 393224 | tf_op jit(solution)/shard_map/ppermute | solution.py:170
  106.3 0.7 collective-permute-done.6.r3_ref
  107.0 5.4 %collective-permute-done.5.r2_ref = bf16[64,1024]{1,0:T(8,128)(2,1)S(1)} collective-permute-done((bf16[64,1024]{1,0:T(8,128)(2,1)S(1)}, bf16[64,1024]{1,0:T(8,128)(2,1)S(1)}, u32[]{:S(2)}, u32[]{:S(2)}) %collective-permute-start.5) | collective-permute-done | bytes 131104 | tf_op jit(solution)/shard_map/ppermute | solution.py:170
  112.4 37.0 %collective-permute-done.4.r1_ref = bf16[64,1024]{1,0:T(8,128)(2,1)S(1)} collective-permute-done((bf16[64,1024]{1,0:T(8,128)(2,1)S(1)}, bf16[64,1024]{1,0:T(8,128)(2,1)S(1)}, u32[]{:S(2)}, u32[]{:S(2)}) %collective-permute-start.4) | collective-permute-done | bytes 131104 | tf_op jit(solution)/shard_map/ppermute | solution.py:170
  149.5 2.3 %shard_map.107 = (bf16[128,1024]{1,0:T(8,128)(2,1)}, f32[32,128]{1,0:T(8,128)}, bf16[32,128]{1,0:T(8,128)(2,1)S(1)}) custom-call(s32[8,128]{1,0:T(8,128)} %get-tuple-element.10.meta_ref, s32[1,128]{1,0:T(1,128)} %chosen_ref.3, f32[32,128]{1,0:T(8,128)} %bitcast.36, bf16[128,1024]{1,0:T(8,128)(2,1)} %bitcast.34, ...), custom_call_target="tpu_custom_call" | custom-call | tf_op jit(solution)/shard_map/pallas_call | solution.py:146
  151.8 1.9 %collective-permute-start.9 = (bf16[32,128]{1,0:T(8,128)(2,1)S(1)}, bf16[32,128]{1,0:T(8,128)(2,1)S(1)}, u32[]{:S(2)}, u32[]{:S(2)}) collective-permute-start(bf16[32,128]{1,0:T(8,128)(2,1)S(1)} %get-tuple-element.16), channel_id=1, source_target_pairs={{32,0},{33,1},{34,2},{35,3},{36,4},{37,5},{38,6},{39,7},{40,8},{41... | collective-permute-start | bytes 24584 | tf_op jit(solution)/shard_map/ppermute | solution.py:179
  153.7 0.0 collective-permute-done.8.late_ref
  153.7 0.0 collective-permute-done.7.early_ref
  153.7 7.5 %collective-permute-done.9.score_ref = bf16[32,128]{1,0:T(8,128)(2,1)S(1)} collective-permute-done((bf16[32,128]{1,0:T(8,128)(2,1)S(1)}, bf16[32,128]{1,0:T(8,128)(2,1)S(1)}, u32[]{:S(2)}, u32[]{:S(2)}) %collective-permute-start.9) | collective-permute-done | bytes 8224 | tf_op jit(solution)/shard_map/ppermute | solution.py:179
  161.2 0.0 copy-done
  161.2 2.0 %shard_map.108 = bf16[128,3584]{1,0:T(8,128)(2,1)} custom-call(bf16[72,3584]{1,0:T(8,128)(2,1)S(1)} %collective-permute-done.7.early_ref, bf16[64,3584]{1,0:T(8,128)(2,1)S(1)} %collective-permute-done.8.late_ref, bf16[32,128]{1,0:T(8,128)(2,1)S(1)} %collective-permute-done.9.score_ref, bf16[32,3584]{1,0:T(8,128)(2,1)S(1)} %copy-done), custom_call_target="tpu_custom_call" | custom-call | tf_op jit(solution)/shard_map/pallas_call | solution.py:146
  (1 shorter events, 0.0 us)
Async XLA Ops:
  3.7 46.2 %all-to-all-start = ((bf16[8,2,8,3584]{3,2,1,0:T(8,128)(2,1)}), bf16[8,2,8,3584]{3,2,1,0:T(8,128)(2,1)}, u32[]{:S(2)}, u32[]{:S(2)}) async-start(bf16[8,2,8,3584]{3,2,1,0:T(8,128)(2,1)} %bitcast.5), calls=%async_computation | async-start | bytes 1835008 | tf_op jit(solution)/shard_map/all_to_all | solution.py:182
  8.5 30.3 %collective-permute-start.1 = (bf16[72,3584]{1,0:T(8,128)(2,1)S(1)}, bf16[72,3584]{1,0:T(8,128)(2,1)S(1)}, u32[]{:S(2)}, u32[]{:S(2)}) collective-permute-start(bf16[72,3584]{1,0:T(8,128)(2,1)S(1)} %get-tuple-element.12), channel_id=1, source_target_pairs={{0,120},{1,121},{2,122},{3,123},{4,124},{5,125},{6,126},{7,127},{8... | collective-permute-start | bytes 1548296 | tf_op jit(solution)/shard_map/ppermute | solution.py:170
  26.7 21.9 %collective-permute-start.2 = (bf16[64,3584]{1,0:T(8,128)(2,1)S(1)}, bf16[64,3584]{1,0:T(8,128)(2,1)S(1)}, u32[]{:S(2)}, u32[]{:S(2)}) collective-permute-start(bf16[64,3584]{1,0:T(8,128)(2,1)S(1)} %get-tuple-element.13), channel_id=1, source_target_pairs={{0,120},{1,121},{2,122},{3,123},{4,124},{5,125},{6,126},{7,127},{8... | collective-permute-start | bytes 1376264 | tf_op jit(solution)/shard_map/ppermute | solution.py:170
  38.8 20.0 %collective-permute-start.3 = (bf16[72,3584]{1,0:T(8,128)(2,1)S(1)}, bf16[72,3584]{1,0:T(8,128)(2,1)S(1)}, u32[]{:S(2)}, u32[]{:S(2)}) collective-permute-start(bf16[72,3584]{1,0:T(8,128)(2,1)S(1)} %collective-permute-done.1.early_ref), channel_id=1, source_target_pairs={{0,120},{1,121},{2,122},{3,123},{4,124},{5,125},{6,126},{7,127},{8... | collective-permute-start | bytes 1548296 | tf_op jit(solution)/shard_map/ppermute | solution.py:170
  49.9 13.0 %all-to-all-start.1 = ((bf16[8,8,3584]{2,1,0:T(8,128)(2,1)}), bf16[8,8,3584]{2,1,0:T(8,128)(2,1)S(1)}, u32[]{:S(2)}, u32[]{:S(2)}) async-start(bf16[8,8,3584]{2,1,0:T(8,128)(2,1)} %bitcast.8), calls=%async_computation.1 | async-start | bytes 917504 | tf_op jit(solution)/shard_map/all_to_all | solution.py:182
  56.7 104.5 %copy-start = (bf16[32,3584]{1,0:T(8,128)(2,1)S(1)}, bf16[32,3584]{1,0:T(8,128)(2,1)}, u32[]{:S(2)}) copy-start(bf16[32,3584]{1,0:T(8,128)(2,1)} %router_ref.1) | copy-start | bytes 688132
  56.7 16.7 %collective-permute-start = (bf16[64,3584]{1,0:T(8,128)(2,1)}, bf16[64,3584]{1,0:T(8,128)(2,1)S(1)}, u32[]{:S(2)}, u32[]{:S(2)}) collective-permute-start(bf16[64,3584]{1,0:T(8,128)(2,1)} %get-tuple-element.17), channel_id=1, source_target_pairs={{0,8},{1,9},{2,10},{3,11},{4,12},{5,13},{6,14},{7,15},{8,16},{9,17... | collective-permute-start | bytes 1376264 | tf_op jit(solution)/shard_map/ppermute | solution.py:170
  62.9 13.0 %all-to-all-start.2 = ((bf16[8,8,3584]{2,1,0:T(8,128)(2,1)}), bf16[8,8,3584]{2,1,0:T(8,128)(2,1)S(1)}, u32[]{:S(2)}, u32[]{:S(2)}) async-start(bf16[8,8,3584]{2,1,0:T(8,128)(2,1)} %bitcast.10), calls=%async_computation.2 | async-start | bytes 917504 | tf_op jit(solution)/shard_map/all_to_all | solution.py:182
  83.0 14.0 %all-to-all-start.3 = ((bf16[8,4,8,1024]{3,2,1,0:T(8,128)(2,1)}), bf16[8,4,8,1024]{3,2,1,0:T(8,128)(2,1)S(1)}, u32[]{:S(2)}, u32[]{:S(2)}) async-start(bf16[8,4,8,1024]{3,2,1,0:T(8,128)(2,1)} %shard_map.106), calls=%async_computation.3 | async-start | bytes 1048576 | tf_op jit(solution)/shard_map/all_to_all | solution.py:182
  87.9 65.8 %collective-permute-start.7 = (bf16[72,3584]{1,0:T(8,128)(2,1)S(1)}, bf16[72,3584]{1,0:T(8,128)(2,1)S(1)}, u32[]{:S(2)}, u32[]{:S(2)}) collective-permute-start(bf16[72,3584]{1,0:T(8,128)(2,1)S(1)} %collective-permute-done.3.early_ref), channel_id=1, source_target_pairs={{16,0},{17,1},{18,2},{19,3},{20,4},{21,5},{22,6},{23,7},{24,8},{25... | collective-permute-start | bytes 1548296 | tf_op jit(solution)/shard_map/ppermute | solution.py:179
  92.1 61.6 %collective-permute-start.8 = (bf16[64,3584]{1,0:T(8,128)(2,1)S(1)}, bf16[64,3584]{1,0:T(8,128)(2,1)S(1)}, u32[]{:S(2)}, u32[]{:S(2)}) collective-permute-start(bf16[64,3584]{1,0:T(8,128)(2,1)S(1)} %collective-permute-done.2.late_ref), channel_id=1, source_target_pairs={{24,0},{25,1},{26,2},{27,3},{28,4},{29,5},{30,6},{31,7},{32,8},{33... | collective-permute-start | bytes 1376264 | tf_op jit(solution)/shard_map/ppermute | solution.py:179
  97.1 9.9 %collective-permute-start.6 = (bf16[64,1024]{1,0:T(8,128)(2,1)S(1)}, bf16[64,1024]{1,0:T(8,128)(2,1)S(1)}, u32[]{:S(2)}, u32[]{:S(2)}) collective-permute-start(bf16[64,1024]{1,0:T(8,128)(2,1)S(1)} %get-tuple-element.19), channel_id=1, source_target_pairs={{0,8},{1,9},{2,10},{3,11},{4,12},{5,13},{6,14},{7,15},{8,16},{9,17... | collective-permute-start | bytes 393224 | tf_op jit(solution)/shard_map/ppermute | solution.py:170
  99.0 13.4 %collective-permute-start.5 = (bf16[64,1024]{1,0:T(8,128)(2,1)S(1)}, bf16[64,1024]{1,0:T(8,128)(2,1)S(1)}, u32[]{:S(2)}, u32[]{:S(2)}) collective-permute-start(bf16[64,1024]{1,0:T(8,128)(2,1)S(1)} %get-tuple-element.20), channel_id=1, source_target_pairs={{0,16},{1,17},{2,18},{3,19},{4,20},{5,21},{6,22},{7,23},{8,24},{9,... | collective-permute-start | bytes 393224 | tf_op jit(solution)/shard_map/ppermute | solution.py:170
  102.3 47.1 %collective-permute-start.4 = (bf16[64,1024]{1,0:T(8,128)(2,1)S(1)}, bf16[64,1024]{1,0:T(8,128)(2,1)S(1)}, u32[]{:S(2)}, u32[]{:S(2)}) collective-permute-start(bf16[64,1024]{1,0:T(8,128)(2,1)S(1)} %get-tuple-element.21), channel_id=1, source_target_pairs={{0,120},{1,121},{2,122},{3,123},{4,124},{5,125},{6,126},{7,127},{8... | collective-permute-start | bytes 393224 | tf_op jit(solution)/shard_map/ppermute | solution.py:170
  151.8 9.4 %collective-permute-start.9 = (bf16[32,128]{1,0:T(8,128)(2,1)S(1)}, bf16[32,128]{1,0:T(8,128)(2,1)S(1)}, u32[]{:S(2)}, u32[]{:S(2)}) collective-permute-start(bf16[32,128]{1,0:T(8,128)(2,1)S(1)} %get-tuple-element.16), channel_id=1, source_target_pairs={{32,0},{33,1},{34,2},{35,3},{36,4},{37,5},{38,6},{39,7},{40,8},{41... | collective-permute-start | bytes 24584 | tf_op jit(solution)/shard_map/ppermute | solution.py:179

commit v6 on v5

--- a/solution.py
+++ b/solution.py
@@ -24,9 +24,10 @@
     return jnp.broadcast_to(row, (count, row.shape[1])).T[:, :1]
 
 
-def prep_kernel(chosen_ref, places_ref, counts_ref, tok_ref, first_ref, early_ref, late_ref, meta_ref):
+def prep_kernel(chosen_ref, places_ref, counts_ref, tok_ref, first_ref, early_ref, late_ref, rest_ref, meta_ref):
     tokens, width = tok_ref.shape
-    half = late_ref.shape[0]
+    half = early_ref.shape[0] - 8
+    last = tokens - rest_ref.shape[0]
     experts = counts_ref.shape[0]
     rows = first_ref.shape[0]
     own = lax.axis_index(expert_axes)
@@ -46,7 +47,7 @@
         return jnp.where(live & (offset == k), dest * slots + places, -1)
 
     order = lax.broadcasted_iota(jnp.int32, (1, tokens), 1)
-    key = (jnp.where(live & (offset == 2), 0, tokens) + order).astype(jnp.float32)
+    key = (jnp.where(live & (offset >= 2), jnp.where(offset == 2, 0, tokens), 2 * tokens) + order).astype(jnp.float32)
     key_rows = jnp.broadcast_to(key, (tokens, tokens))
     rank = jnp.sum((key_rows.T < key_rows).astype(jnp.float32), axis=0, keepdims=True)
     perm = as_pick(lax.broadcasted_iota(jnp.int32, (tokens, tokens), 0) == rank.astype(jnp.int32))
@@ -62,7 +63,8 @@
     early_ref[half:] = jnp.zeros((8, width), jnp.bfloat16)
     table = jnp.where(row_id < 2, moved, jnp.where(row_id == 2, rank, 0.0)).astype(jnp.bfloat16)
     early_ref[half:, :tokens] = table
-    late_ref[...] = ordered[half:]
+    late_ref[...] = ordered[half:last]
+    rest_ref[...] = ordered[last:]
     target = jnp.where(live & (offset < 2), (2 * dest + offset) * slots + places, -1)
     pick = as_pick(lax.broadcasted_iota(jnp.int32, (rows, tokens), 0) == target)
     first_ref[...] = jnp.dot(pick, tok, preferred_element_type=jnp.float32).astype(jnp.bfloat16)
@@ -73,12 +75,12 @@
 
 
 def pack_one_kernel(early_ref, late_ref, out_ref):
-    half = late_ref.shape[0]
-    tokens = 2 * half
-    target = early_ref[half:, :tokens].astype(jnp.float32)[0:1, :].astype(jnp.int32)
-    pick = as_pick(lax.broadcasted_iota(jnp.int32, (out_ref.shape[0], tokens), 0) == target)
+    half = early_ref.shape[0] - 8
+    count = half + late_ref.shape[0]
+    target = early_ref[half:, :2 * half].astype(jnp.float32)[0:1, :].astype(jnp.int32)
+    pick = as_pick(lax.broadcasted_iota(jnp.int32, (out_ref.shape[0], 2 * half), 0) == target)
     out = jnp.dot(pick[:, :half], early_ref[:half], preferred_element_type=jnp.float32)
-    out = out + jnp.dot(pick[:, half:], late_ref[...], preferred_element_type=jnp.float32)
+    out = out + jnp.dot(pick[:, half:count], late_ref[...], preferred_element_type=jnp.float32)
     out_ref[...] = out.astype(jnp.bfloat16)
 
 
@@ -89,22 +91,43 @@
     out_ref[...] = jnp.dot(pick[:, :half], early_ref[:half], preferred_element_type=jnp.float32).astype(jnp.bfloat16)
 
 
-def serve_kernel(r0_ref, r1_ref, r2_ref, r3_ref, weight_ref, out_ref, held_ref, fetched_ref, sems):
-    rows = r0_ref.shape[0]
+def serve_part(weight, held, rows):
+    found = lax.dot_general(weight, held, NT, preferred_element_type=jnp.float32).T
+    parts = []
+    for k in range(found.shape[0] // rows):
+        part = found[k * rows:(k + 1) * rows].reshape(rows // slots, slots, weight.shape[0])
+        parts.append(part.astype(jnp.bfloat16))
+    return parts
+
+
+def fetch_blocks(weight_ref, fetched_ref, sems):
     count = sems.shape[0]
     step = weight_ref.shape[0] // count
     blocks = [pl.ds(j * step, step) for j in range(count)]
     fetches = [pltpu.make_async_copy(weight_ref.at[blocks[j]], fetched_ref.at[blocks[j]], sems.at[j]) for j in range(count)]
     for fetch in fetches:
         fetch.start()
-    for k, ref in enumerate((r0_ref, r1_ref, r2_ref, r3_ref)):
+    return list(zip(fetches, blocks))
+
+
+def serve_three_kernel(r0_ref, r1_ref, r2_ref, weight_ref, out_ref, fetched_ref, held_ref, sems):
+    rows = r0_ref.shape[0]
+    fetches = fetch_blocks(weight_ref, fetched_ref, sems)
+    for k, ref in enumerate((r0_ref, r1_ref, r2_ref)):
         held_ref[k * rows:(k + 1) * rows] = ref[...]
-    for fetch, block in zip(fetches, blocks):
+    for fetch, block in fetches:
         fetch.wait()
-        found = lax.dot_general(fetched_ref[block, :], held_ref[...], NT, preferred_element_type=jnp.float32).T
-        for k in range(4):
-            part = found[k * rows:(k + 1) * rows].reshape(rows // slots, slots, step)
-            out_ref[:, k, :, block] = part.astype(jnp.bfloat16)
+        for k, part in enumerate(serve_part(fetched_ref[block, :], held_ref[...], rows)):
+            out_ref[:, k, :, block] = part
+
+
+def serve_last_kernel(three_ref, r3_ref, weight_ref, out_ref, fetched_ref, sems):
+    rows = r3_ref.shape[0]
+    fetches = fetch_blocks(weight_ref, fetched_ref, sems)
+    out_ref[:, :3] = three_ref[...]
+    for fetch, block in fetches:
+        fetch.wait()
+        out_ref[:, 3, :, block] = serve_part(fetched_ref[block, :], r3_ref[...], rows)[0]
 
 
 def back_kernel(meta_ref, chosen_ref, scores_ref, hidden_ref, r0_ref, r1_ref, r2_ref, r3_ref, act_ref, score_ref, score_bf_ref):
@@ -128,14 +151,16 @@
     score_bf_ref[...] = score.astype(jnp.bfloat16)
 
 
-def up_kernel(early_ref, late_ref, score_ref, router_ref, out_ref):
-    half = late_ref.shape[0]
-    tokens = 2 * half
+def up_kernel(early_ref, late_ref, rest_ref, score_ref, router_ref, out_ref):
+    half = early_ref.shape[0] - 8
+    tokens = out_ref.shape[0]
+    last = tokens - rest_ref.shape[0]
     rank = column(early_ref[half:, :tokens].astype(jnp.float32)[2:3, :], tokens).astype(jnp.int32)
     pick = as_pick(lax.broadcasted_iota(jnp.int32, (tokens, tokens), 1) == rank)
     scores = score_ref[...].astype(jnp.float32).T.astype(jnp.bfloat16)
     out = jnp.dot(pick[:, :half], early_ref[:half], preferred_element_type=jnp.float32)
-    out = out + jnp.dot(pick[:, half:], late_ref[...], preferred_element_type=jnp.float32)
+    out = out + jnp.dot(pick[:, half:last], late_ref[...], preferred_element_type=jnp.float32)
+    out = out + jnp.dot(pick[:, last:], rest_ref[...], preferred_element_type=jnp.float32)
     out = out + jnp.dot(scores, router_ref[...], preferred_element_type=jnp.float32)
     out_ref[...] = out.astype(jnp.bfloat16)
 
@@ -160,6 +185,7 @@
     hidden_width = hidden_act.shape[2]
     half = tokens // 2
     rows = nxc * slots
+    spare = tokens - 14 * nxc
     weight = down_weight[0]
 
     def lanes(pairs):
@@ -184,14 +210,15 @@
     def spread(value):
         return exchange(value.reshape(nxc, slots, width)).reshape(rows, width)
 
-    def serve(*values):
-        scratch = [
-            pltpu.VMEM((4 * rows, width), bf16),
-            pltpu.VMEM((hidden_width, width), bf16),
-            pltpu.SemaphoreType.DMA((4,)),
-        ]
+    def serve_three(*values):
+        scratch = [pltpu.VMEM((hidden_width, width), bf16), pltpu.VMEM((3 * rows, width), bf16), pltpu.SemaphoreType.DMA((2,))]
+        outs = [("held", (nxc, 3, slots, hidden_width), bf16)]
+        return call(serve_three_kernel, outs, *held(*values), ("far", weight), scratch=scratch)[0]
+
+    def serve_last(*values):
+        scratch = [pltpu.VMEM((hidden_width, width), bf16), pltpu.SemaphoreType.DMA((4,))]
         outs = [("held", (nxc, 4, slots, hidden_width), bf16)]
-        return call(serve_kernel, outs, *held(*values), ("far", weight), scratch=scratch)[0]
+        return call(serve_last_kernel, outs, *held(*values), ("far", weight), scratch=scratch)[0]
 
     def held(*values):
         return [("held", v) for v in values]
@@ -205,24 +232,29 @@
     outs = [
         ("held", (2 * rows, width), bf16),
         ("held", (half + 8, width), bf16),
-        ("held", (half, width), bf16),
+        ("held", (tokens - half - spare, width), bf16),
+        ("held", (spare, width), bf16),
         ("near", (8, tokens), jnp.int32),
     ]
-    first, early, late, meta = call(prep_kernel, outs, *near_by(expert_ids, slot_ids, counts[0], tok))
+    first, early, late, rest, meta = call(prep_kernel, outs, *near_by(expert_ids, slot_ids, counts[0], tok))
     early1 = along_z(early, -1)
     first = exchange(first.reshape(nxc, 2, slots, width))
     late1 = along_z(late, -1)
+    rest = along_z(rest, nzl)
     early2 = along_z(early1, -1)
     near, up = part(first, 0), part(first, 1)
     up = along_z(up, 1)
     one = call(pack_one_kernel, [("held", (rows, width), bf16)], *held(early1, late1))[0]
     one = spread(one)
     late4 = to_end(late1, 3)
+    rest = along_z(rest, nzl)
     two = call(pack_two_kernel, [("held", (rows, width), bf16)], *held(early2))[0]
     two = spread(two)
     early4 = to_end(early2, 2)
-    served = serve(near, up, one, two)
+    three = serve_three(near, up, one)
+    served = serve_last(three, two)
     served = exchange(served)
+    rest4 = to_end(rest, nz - nzl)
     r0, r1, r3, r2 = (part(served, k) for k in range(4))
     r2 = along_z(r2, 2)
     r1 = along_z(r1, -1)
@@ -236,7 +268,7 @@
     ins = near_by(meta, expert_ids, scores[0].T, hidden_act[0]) + held(r0, r1, r2, r3)
     act, score, score_bf = call(back_kernel, outs, *ins)
     late_score = to_end(score_bf, nzl)
-    upstream = call(up_kernel, [("near", (tokens, width), bf16)], *held(early4, late4, late_score, router))[0]
+    upstream = call(up_kernel, [("near", (tokens, width), bf16)], *held(early4, late4, rest4, late_score, router))[0]
     return act[None], score.T[None], upstream[None]
 
 

time: 164 us -> 159 us (0.970)
  the two profiles are of different devices: /device:TPU:10 before, /device:TPU:50 now
where the time goes in v6:
time: 159 us; the launch traced here: 158 us
  starting transfers between devices  80.4 us (51%)
  waiting for transfers between devices  51.7 us (33%)
  Pallas kernels  23.1 us (15%)
  local copies, waits for them, and re-layouts  2.03 us (1%)
    ppermute x9, waiting for transfers between devices, along_z(): return lax.ppermute(value, axes, lanes(pairs))  47.3 us
    ppermute x9, starting transfers between devices, along_z(): return lax.ppermute(value, axes, lanes(pairs))  45 us
    pallas_call x7, Pallas kernels, call(): pl.pallas_call(kernel, out_shape=tuple((space[how](shape, dtype) for how,...  23.1 us
    all_to_all x4, starting transfers between devices, exchange(): return lax.all_to_all(value, group, split_axis=0, concat_axis=0, tiled=True)  19.3 us
    ppermute x4, starting transfers between devices, to_end(): return lax.ppermute(value, axes, lanes(pairs))  16.1 us
  transfers between devices with their start and end apart: 17, of which 10 were waited for; matrix products, arithmetic and copies ran while one was open for 1% of the time, Pallas kernels for 7%

profile of v6, /device:TPU:50, one launch (start us, length us, event | category | flops | bytes accessed | tf_op | source)
XLA Modules:
  0.0 158.1 jit_solution(12578387781067031959)
XLA Ops:
  0.6 3.0 %shard_map.103 = (bf16[128,3584]{1,0:T(8,128)(2,1)}, bf16[72,3584]{1,0:T(8,128)(2,1)S(1)}, bf16[48,3584]{1,0:T(8,128)(2,1)S(1)}, bf16[16,3584]{1,0:T(8,128)(2,1)S(1)}, s32[8,128]{1,0:T(8,128)}) custom-call(s32[1,128]{1,0:T(1,128)} %chosen_ref.3, s32[1,128]{1,0:T(1,128)} %places_ref.1, s32[32,32]{1,0:T(8,128)} %bitcast.36, bf16[128,3584]{1,0:T(8,128)(2,1)} %bitcast.33), custom_call_target="tpu_custom_call" | custom-call | tf_op jit(solution)/shard_map/pallas_call | solution.py:171
  3.7 4.8 %all-to-all-start = ((bf16[8,2,8,3584]{3,2,1,0:T(8,128)(2,1)}), bf16[8,2,8,3584]{3,2,1,0:T(8,128)(2,1)}, u32[]{:S(2)}, u32[]{:S(2)}) async-start(bf16[8,2,8,3584]{3,2,1,0:T(8,128)(2,1)} %bitcast.5), calls=%async_computation | async-start | bytes 1835008 | tf_op jit(solution)/shard_map/all_to_all | solution.py:208
  8.5 18.2 %collective-permute-start.1 = (bf16[72,3584]{1,0:T(8,128)(2,1)S(1)}, bf16[72,3584]{1,0:T(8,128)(2,1)S(1)}, u32[]{:S(2)}, u32[]{:S(2)}) collective-permute-start(bf16[72,3584]{1,0:T(8,128)(2,1)S(1)} %get-tuple-element.13), channel_id=1, source_target_pairs={{0,120},{1,121},{2,122},{3,123},{4,124},{5,125},{6,126},{7,127},{8... | collective-permute-start | bytes 1548296 | tf_op jit(solution)/shard_map/ppermute | solution.py:196
  26.7 2.5 %collective-permute-start.2 = (bf16[48,3584]{1,0:T(8,128)(2,1)S(1)}, bf16[48,3584]{1,0:T(8,128)(2,1)S(1)}, u32[]{:S(2)}, u32[]{:S(2)}) collective-permute-start(bf16[48,3584]{1,0:T(8,128)(2,1)S(1)} %get-tuple-element.14), channel_id=1, source_target_pairs={{0,120},{1,121},{2,122},{3,123},{4,124},{5,125},{6,126},{7,127},{8... | collective-permute-start | bytes 1032200 | tf_op jit(solution)/shard_map/ppermute | solution.py:196
  29.2 9.6 %collective-permute-done.1.early_ref = bf16[72,3584]{1,0:T(8,128)(2,1)S(1)} collective-permute-done((bf16[72,3584]{1,0:T(8,128)(2,1)S(1)}, bf16[72,3584]{1,0:T(8,128)(2,1)S(1)}, u32[]{:S(2)}, u32[]{:S(2)}) %collective-permute-start.1) | collective-permute-done | bytes 516128 | tf_op jit(solution)/shard_map/ppermute | solution.py:196
  38.8 5.6 %collective-permute-start.3 = (bf16[72,3584]{1,0:T(8,128)(2,1)S(1)}, bf16[72,3584]{1,0:T(8,128)(2,1)S(1)}, u32[]{:S(2)}, u32[]{:S(2)}) collective-permute-start(bf16[72,3584]{1,0:T(8,128)(2,1)S(1)} %collective-permute-done.1.early_ref), channel_id=1, source_target_pairs={{0,120},{1,121},{2,122},{3,123},{4,124},{5,125},{6,126},{7,127},{8... | collective-permute-start | bytes 1548296 | tf_op jit(solution)/shard_map/ppermute | solution.py:196
  44.4 1.8 %collective-permute-done.2.late_ref = bf16[48,3584]{1,0:T(8,128)(2,1)S(1)} collective-permute-done((bf16[48,3584]{1,0:T(8,128)(2,1)S(1)}, bf16[48,3584]{1,0:T(8,128)(2,1)S(1)}, u32[]{:S(2)}, u32[]{:S(2)}) %collective-permute-start.2) | collective-permute-done | bytes 344096 | tf_op jit(solution)/shard_map/ppermute | solution.py:196
  46.2 1.2 shard_map.104
  47.4 0.0 all-to-all-done
  47.5 4.8 %all-to-all-start.1 = ((bf16[8,8,3584]{2,1,0:T(8,128)(2,1)}), bf16[8,8,3584]{2,1,0:T(8,128)(2,1)S(1)}, u32[]{:S(2)}, u32[]{:S(2)}) async-start(bf16[8,8,3584]{2,1,0:T(8,128)(2,1)} %bitcast.8), calls=%async_computation.1 | async-start | bytes 917504 | tf_op jit(solution)/shard_map/all_to_all | solution.py:208
  52.3 2.0 %slice_bitcast_fusion = (bf16[64,3584]{1,0:T(8,128)(2,1)}, bf16[64,3584]{1,0:T(8,128)(2,1)S(1)}) fusion(bf16[8,2,8,3584]{3,2,1,0:T(8,128)(2,1)} %all-to-all-done), kind=kLoop, calls=%fused_computation | loop fusion | bytes 1835008 | tf_op jit(solution)/shard_map/reshape;squeeze | solution.py:230
  54.2 1.9 %collective-permute-start = (bf16[64,3584]{1,0:T(8,128)(2,1)}, bf16[64,3584]{1,0:T(8,128)(2,1)S(1)}, u32[]{:S(2)}, u32[]{:S(2)}) collective-permute-start(bf16[64,3584]{1,0:T(8,128)(2,1)} %get-tuple-element.19), channel_id=1, source_target_pairs={{0,8},{1,9},{2,10},{3,11},{4,12},{5,13},{6,14},{7,15},{8,16},{9,17... | collective-permute-start | bytes 1376264 | tf_op jit(solution)/shard_map/ppermute | solution.py:196
  56.2 0.3 collective-permute-done.3.early_ref
  56.4 1.0 shard_map.106
  57.4 3.0 %all-to-all-done.1 = bf16[8,8,3584]{2,1,0:T(8,128)(2,1)S(1)} async-done(((bf16[8,8,3584]{2,1,0:T(8,128)(2,1)}), bf16[8,8,3584]{2,1,0:T(8,128)(2,1)S(1)}, u32[]{:S(2)}, u32[]{:S(2)}) %all-to-all-start.1) | async-done | bytes 458784 | tf_op jit(solution)/shard_map/all_to_all | solution.py:208
  60.4 4.8 %all-to-all-start.2 = ((bf16[8,8,3584]{2,1,0:T(8,128)(2,1)}), bf16[8,8,3584]{2,1,0:T(8,128)(2,1)S(1)}, u32[]{:S(2)}, u32[]{:S(2)}) async-start(bf16[8,8,3584]{2,1,0:T(8,128)(2,1)} %bitcast.11), calls=%async_computation.2 | async-start | bytes 917504 | tf_op jit(solution)/shard_map/all_to_all | solution.py:208
  65.3 5.6 %collective-permute-done.r1_ref = bf16[64,3584]{1,0:T(8,128)(2,1)S(1)} collective-permute-done((bf16[64,3584]{1,0:T(8,128)(2,1)}, bf16[64,3584]{1,0:T(8,128)(2,1)S(1)}, u32[]{:S(2)}, u32[]{:S(2)}) %collective-permute-start) | collective-permute-done | bytes 458784 | tf_op jit(solution)/shard_map/ppermute | solution.py:196
  70.8 6.3 %shard_map.105.three_ref = bf16[8,3,8,1024]{3,2,1,0:T(8,128)(2,1)S(1)} custom-call(bf16[64,3584]{1,0:T(8,128)(2,1)S(1)} %get-tuple-element.20.r0_ref, bf16[64,3584]{1,0:T(8,128)(2,1)S(1)} %collective-permute-done.r1_ref, bf16[64,3584]{1,0:T(8,128)(2,1)S(1)} %bitcast.29, bf16[1024,3584]{1,0:T(8,128)(2,1)} %bitcast.31), custom_call_target="tpu_custom_call" | custom-call | tf_op jit(solution)/shard_map/pallas_call | solution.py:171
  77.1 0.0 copy-start
  77.1 0.0 all-to-all-done.2
  77.2 6.9 %shard_map.107 = bf16[8,4,8,1024]{3,2,1,0:T(8,128)(2,1)} custom-call(bf16[8,3,8,1024]{3,2,1,0:T(8,128)(2,1)S(1)} %shard_map.105.three_ref, bf16[64,3584]{1,0:T(8,128)(2,1)S(1)} %bitcast.30, bf16[1024,3584]{1,0:T(8,128)(2,1)} %bitcast.32), custom_call_target="tpu_custom_call" | custom-call | tf_op jit(solution)/shard_map/pallas_call | solution.py:171
  84.0 4.8 %all-to-all-start.3 = ((bf16[8,4,8,1024]{3,2,1,0:T(8,128)(2,1)}), bf16[8,4,8,1024]{3,2,1,0:T(8,128)(2,1)S(1)}, u32[]{:S(2)}, u32[]{:S(2)}) async-start(bf16[8,4,8,1024]{3,2,1,0:T(8,128)(2,1)} %shard_map.107), calls=%async_computation.3 | async-start | bytes 1048576 | tf_op jit(solution)/shard_map/all_to_all | solution.py:208
  88.9 1.9 %collective-permute-start.9 = (bf16[16,3584]{1,0:T(8,128)(2,1)S(1)}, bf16[16,3584]{1,0:T(8,128)(2,1)S(1)}, u32[]{:S(2)}, u32[]{:S(2)}) collective-permute-start(bf16[16,3584]{1,0:T(8,128)(2,1)S(1)} %get-tuple-element.17), channel_id=1, source_target_pairs={{0,32},{1,33},{2,34},{3,35},{4,36},{5,37},{6,38},{7,39},{8,40},{9,... | collective-permute-start | bytes 344072 | tf_op jit(solution)/shard_map/ppermute | solution.py:196
  90.8 3.5 %collective-permute-start.7 = (bf16[72,3584]{1,0:T(8,128)(2,1)S(1)}, bf16[72,3584]{1,0:T(8,128)(2,1)S(1)}, u32[]{:S(2)}, u32[]{:S(2)}) collective-permute-start(bf16[72,3584]{1,0:T(8,128)(2,1)S(1)} %collective-permute-done.3.early_ref), channel_id=1, source_target_pairs={{16,0},{17,1},{18,2},{19,3},{20,4},{21,5},{22,6},{23,7},{24,8},{25... | collective-permute-start | bytes 1548296 | tf_op jit(solution)/shard_map/ppermute | solution.py:205
  94.3 13.0 %collective-permute-done.9 = bf16[16,3584]{1,0:T(8,128)(2,1)S(1)} collective-permute-done((bf16[16,3584]{1,0:T(8,128)(2,1)S(1)}, bf16[16,3584]{1,0:T(8,128)(2,1)S(1)}, u32[]{:S(2)}, u32[]{:S(2)}) %collective-permute-start.9) | collective-permute-done | bytes 114720 | tf_op jit(solution)/shard_map/ppermute | solution.py:196
  107.3 2.2 %collective-permute-start.10 = (bf16[16,3584]{1,0:T(8,128)(2,1)S(1)}, bf16[16,3584]{1,0:T(8,128)(2,1)S(1)}, u32[]{:S(2)}, u32[]{:S(2)}) collective-permute-start(bf16[16,3584]{1,0:T(8,128)(2,1)S(1)} %collective-permute-done.9), channel_id=1, source_target_pairs={{0,32},{1,33},{2,34},{3,35},{4,36},{5,37},{6,38},{7,39},{8,40},{9,... | collective-permute-start | bytes 344072 | tf_op jit(solution)/shard_map/ppermute | solution.py:196
  109.5 1.9 %collective-permute-start.8 = (bf16[48,3584]{1,0:T(8,128)(2,1)S(1)}, bf16[48,3584]{1,0:T(8,128)(2,1)S(1)}, u32[]{:S(2)}, u32[]{:S(2)}) collective-permute-start(bf16[48,3584]{1,0:T(8,128)(2,1)S(1)} %collective-permute-done.2.late_ref), channel_id=1, source_target_pairs={{24,0},{25,1},{26,2},{27,3},{28,4},{29,5},{30,6},{31,7},{32,8},{33... | collective-permute-start | bytes 1032200 | tf_op jit(solution)/shard_map/ppermute | solution.py:205
  111.5 0.0 all-to-all-done.3
  111.5 1.9 %collective-permute-start.6 = (bf16[64,1024]{1,0:T(8,128)(2,1)S(1)}, bf16[64,1024]{1,0:T(8,128)(2,1)S(1)}, u32[]{:S(2)}, u32[]{:S(2)}) collective-permute-start(bf16[64,1024]{1,0:T(8,128)(2,1)S(1)} %get-tuple-element.21), channel_id=1, source_target_pairs={{0,8},{1,9},{2,10},{3,11},{4,12},{5,13},{6,14},{7,15},{8,16},{9,17... | collective-permute-start | bytes 393224 | tf_op jit(solution)/shard_map/ppermute | solution.py:196
  113.4 6.3 %collective-permute-start.5 = (bf16[64,1024]{1,0:T(8,128)(2,1)S(1)}, bf16[64,1024]{1,0:T(8,128)(2,1)S(1)}, u32[]{:S(2)}, u32[]{:S(2)}) collective-permute-start(bf16[64,1024]{1,0:T(8,128)(2,1)S(1)} %get-tuple-element.22), channel_id=1, source_target_pairs={{0,16},{1,17},{2,18},{3,19},{4,20},{5,21},{6,22},{7,23},{8,24},{9,... | collective-permute-start | bytes 393224 | tf_op jit(solution)/shard_map/ppermute | solution.py:196
  119.7 0.0 collective-permute-done.10
  119.7 4.5 %collective-permute-start.4 = (bf16[64,1024]{1,0:T(8,128)(2,1)S(1)}, bf16[64,1024]{1,0:T(8,128)(2,1)S(1)}, u32[]{:S(2)}, u32[]{:S(2)}) collective-permute-start(bf16[64,1024]{1,0:T(8,128)(2,1)S(1)} %get-tuple-element.23), channel_id=1, source_target_pairs={{0,120},{1,121},{2,122},{3,123},{4,124},{5,125},{6,126},{7,127},{8... | collective-permute-start | bytes 393224 | tf_op jit(solution)/shard_map/ppermute | solution.py:196
  124.3 0.5 collective-permute-done.6.r3_ref
  124.7 2.7 %collective-permute-start.11 = (bf16[16,3584]{1,0:T(8,128)(2,1)S(1)}, bf16[16,3584]{1,0:T(8,128)(2,1)S(1)}, u32[]{:S(2)}, u32[]{:S(2)}) collective-permute-start(bf16[16,3584]{1,0:T(8,128)(2,1)S(1)} %collective-permute-done.10), channel_id=1, source_target_pairs={{0,32},{1,33},{2,34},{3,35},{4,36},{5,37},{6,38},{7,39},{8,40},{9,... | collective-permute-start | bytes 344072 | tf_op jit(solution)/shard_map/ppermute | solution.py:205
  127.4 8.5 %collective-permute-done.5.r2_ref = bf16[64,1024]{1,0:T(8,128)(2,1)S(1)} collective-permute-done((bf16[64,1024]{1,0:T(8,128)(2,1)S(1)}, bf16[64,1024]{1,0:T(8,128)(2,1)S(1)}, u32[]{:S(2)}, u32[]{:S(2)}) %collective-permute-start.5) | collective-permute-done | bytes 131104 | tf_op jit(solution)/shard_map/ppermute | solution.py:196
  136.0 8.0 %collective-permute-done.4.r1_ref = bf16[64,1024]{1,0:T(8,128)(2,1)S(1)} collective-permute-done((bf16[64,1024]{1,0:T(8,128)(2,1)S(1)}, bf16[64,1024]{1,0:T(8,128)(2,1)S(1)}, u32[]{:S(2)}, u32[]{:S(2)}) %collective-permute-start.4) | collective-permute-done | bytes 131104 | tf_op jit(solution)/shard_map/ppermute | solution.py:196
  144.0 2.3 %shard_map.108 = (bf16[128,1024]{1,0:T(8,128)(2,1)}, f32[32,128]{1,0:T(8,128)}, bf16[32,128]{1,0:T(8,128)(2,1)S(1)}) custom-call(s32[8,128]{1,0:T(8,128)} %get-tuple-element.11.meta_ref, s32[1,128]{1,0:T(1,128)} %chosen_ref.3, f32[32,128]{1,0:T(8,128)} %bitcast.37, bf16[128,1024]{1,0:T(8,128)(2,1)} %bitcast.35, ...), custom_call_target="tpu_custom_call" | custom-call | tf_op jit(solution)/shard_map/pallas_call | solution.py:171
  146.4 8.0 %collective-permute-start.12 = (bf16[32,128]{1,0:T(8,128)(2,1)S(1)}, bf16[32,128]{1,0:T(8,128)(2,1)S(1)}, u32[]{:S(2)}, u32[]{:S(2)}) collective-permute-start(bf16[32,128]{1,0:T(8,128)(2,1)S(1)} %get-tuple-element.18), channel_id=1, source_target_pairs={{32,0},{33,1},{34,2},{35,3},{36,4},{37,5},{38,6},{39,7},{40,8},{41... | collective-permute-start | bytes 24584 | tf_op jit(solution)/shard_map/ppermute | solution.py:205
  154.4 0.0 collective-permute-done.11.rest_ref
  154.4 0.0 collective-permute-done.8.late_ref
  154.4 0.0 collective-permute-done.7.early_ref
  154.4 1.4 collective-permute-done.12.score_ref
  155.8 0.0 copy-done
  155.8 2.2 %shard_map.109 = bf16[128,3584]{1,0:T(8,128)(2,1)} custom-call(bf16[72,3584]{1,0:T(8,128)(2,1)S(1)} %collective-permute-done.7.early_ref, bf16[48,3584]{1,0:T(8,128)(2,1)S(1)} %collective-permute-done.8.late_ref, bf16[16,3584]{1,0:T(8,128)(2,1)S(1)} %collective-permute-done.11.rest_ref, bf16[32,128]{1,0:T(8,128)(2,1)S(1)} %collective-permute-done.12.score_ref, ...), custom_call_target="tpu_custom_call" | custom-call | tf_op jit(solution)/shard_map/pallas_call | solution.py:171
  (1 shorter events, 0.0 us)
Async XLA Ops:
  3.7 43.8 %all-to-all-start = ((bf16[8,2,8,3584]{3,2,1,0:T(8,128)(2,1)}), bf16[8,2,8,3584]{3,2,1,0:T(8,128)(2,1)}, u32[]{:S(2)}, u32[]{:S(2)}) async-start(bf16[8,2,8,3584]{3,2,1,0:T(8,128)(2,1)} %bitcast.5), calls=%async_computation | async-start | bytes 1835008 | tf_op jit(solution)/shard_map/all_to_all | solution.py:208
  8.5 30.3 %collective-permute-start.1 = (bf16[72,3584]{1,0:T(8,128)(2,1)S(1)}, bf16[72,3584]{1,0:T(8,128)(2,1)S(1)}, u32[]{:S(2)}, u32[]{:S(2)}) collective-permute-start(bf16[72,3584]{1,0:T(8,128)(2,1)S(1)} %get-tuple-element.13), channel_id=1, source_target_pairs={{0,120},{1,121},{2,122},{3,123},{4,124},{5,125},{6,126},{7,127},{8... | collective-permute-start | bytes 1548296 | tf_op jit(solution)/shard_map/ppermute | solution.py:196
  26.7 19.5 %collective-permute-start.2 = (bf16[48,3584]{1,0:T(8,128)(2,1)S(1)}, bf16[48,3584]{1,0:T(8,128)(2,1)S(1)}, u32[]{:S(2)}, u32[]{:S(2)}) collective-permute-start(bf16[48,3584]{1,0:T(8,128)(2,1)S(1)} %get-tuple-element.14), channel_id=1, source_target_pairs={{0,120},{1,121},{2,122},{3,123},{4,124},{5,125},{6,126},{7,127},{8... | collective-permute-start | bytes 1032200 | tf_op jit(solution)/shard_map/ppermute | solution.py:196
  38.8 17.6 %collective-permute-start.3 = (bf16[72,3584]{1,0:T(8,128)(2,1)S(1)}, bf16[72,3584]{1,0:T(8,128)(2,1)S(1)}, u32[]{:S(2)}, u32[]{:S(2)}) collective-permute-start(bf16[72,3584]{1,0:T(8,128)(2,1)S(1)} %collective-permute-done.1.early_ref), channel_id=1, source_target_pairs={{0,120},{1,121},{2,122},{3,123},{4,124},{5,125},{6,126},{7,127},{8... | collective-permute-start | bytes 1548296 | tf_op jit(solution)/shard_map/ppermute | solution.py:196
  47.5 13.0 %all-to-all-start.1 = ((bf16[8,8,3584]{2,1,0:T(8,128)(2,1)}), bf16[8,8,3584]{2,1,0:T(8,128)(2,1)S(1)}, u32[]{:S(2)}, u32[]{:S(2)}) async-start(bf16[8,8,3584]{2,1,0:T(8,128)(2,1)} %bitcast.8), calls=%async_computation.1 | async-start | bytes 917504 | tf_op jit(solution)/shard_map/all_to_all | solution.py:208
  54.2 16.6 %collective-permute-start = (bf16[64,3584]{1,0:T(8,128)(2,1)}, bf16[64,3584]{1,0:T(8,128)(2,1)S(1)}, u32[]{:S(2)}, u32[]{:S(2)}) collective-permute-start(bf16[64,3584]{1,0:T(8,128)(2,1)} %get-tuple-element.19), channel_id=1, source_target_pairs={{0,8},{1,9},{2,10},{3,11},{4,12},{5,13},{6,14},{7,15},{8,16},{9,17... | collective-permute-start | bytes 1376264 | tf_op jit(solution)/shard_map/ppermute | solution.py:196
  60.4 16.7 %all-to-all-start.2 = ((bf16[8,8,3584]{2,1,0:T(8,128)(2,1)}), bf16[8,8,3584]{2,1,0:T(8,128)(2,1)S(1)}, u32[]{:S(2)}, u32[]{:S(2)}) async-start(bf16[8,8,3584]{2,1,0:T(8,128)(2,1)} %bitcast.11), calls=%async_computation.2 | async-start | bytes 917504 | tf_op jit(solution)/shard_map/all_to_all | solution.py:208
  77.1 78.7 %copy-start = (bf16[32,3584]{1,0:T(8,128)(2,1)S(1)}, bf16[32,3584]{1,0:T(8,128)(2,1)}, u32[]{:S(2)}) copy-start(bf16[32,3584]{1,0:T(8,128)(2,1)} %router_ref.1) | copy-start | bytes 688132
  84.0 27.4 %all-to-all-start.3 = ((bf16[8,4,8,1024]{3,2,1,0:T(8,128)(2,1)}), bf16[8,4,8,1024]{3,2,1,0:T(8,128)(2,1)S(1)}, u32[]{:S(2)}, u32[]{:S(2)}) async-start(bf16[8,4,8,1024]{3,2,1,0:T(8,128)(2,1)} %shard_map.107), calls=%async_computation.3 | async-start | bytes 1048576 | tf_op jit(solution)/shard_map/all_to_all | solution.py:208
  88.9 18.5 %collective-permute-start.9 = (bf16[16,3584]{1,0:T(8,128)(2,1)S(1)}, bf16[16,3584]{1,0:T(8,128)(2,1)S(1)}, u32[]{:S(2)}, u32[]{:S(2)}) collective-permute-start(bf16[16,3584]{1,0:T(8,128)(2,1)S(1)} %get-tuple-element.17), channel_id=1, source_target_pairs={{0,32},{1,33},{2,34},{3,35},{4,36},{5,37},{6,38},{7,39},{8,40},{9,... | collective-permute-start | bytes 344072 | tf_op jit(solution)/shard_map/ppermute | solution.py:196
  90.8 63.6 %collective-permute-start.7 = (bf16[72,3584]{1,0:T(8,128)(2,1)S(1)}, bf16[72,3584]{1,0:T(8,128)(2,1)S(1)}, u32[]{:S(2)}, u32[]{:S(2)}) collective-permute-start(bf16[72,3584]{1,0:T(8,128)(2,1)S(1)} %collective-permute-done.3.early_ref), channel_id=1, source_target_pairs={{16,0},{17,1},{18,2},{19,3},{20,4},{21,5},{22,6},{23,7},{24,8},{25... | collective-permute-start | bytes 1548296 | tf_op jit(solution)/shard_map/ppermute | solution.py:205
  107.3 12.4 %collective-permute-start.10 = (bf16[16,3584]{1,0:T(8,128)(2,1)S(1)}, bf16[16,3584]{1,0:T(8,128)(2,1)S(1)}, u32[]{:S(2)}, u32[]{:S(2)}) collective-permute-start(bf16[16,3584]{1,0:T(8,128)(2,1)S(1)} %collective-permute-done.9), channel_id=1, source_target_pairs={{0,32},{1,33},{2,34},{3,35},{4,36},{5,37},{6,38},{7,39},{8,40},{9,... | collective-permute-start | bytes 344072 | tf_op jit(solution)/shard_map/ppermute | solution.py:196
  109.5 44.8 %collective-permute-start.8 = (bf16[48,3584]{1,0:T(8,128)(2,1)S(1)}, bf16[48,3584]{1,0:T(8,128)(2,1)S(1)}, u32[]{:S(2)}, u32[]{:S(2)}) collective-permute-start(bf16[48,3584]{1,0:T(8,128)(2,1)S(1)} %collective-permute-done.2.late_ref), channel_id=1, source_target_pairs={{24,0},{25,1},{26,2},{27,3},{28,4},{29,5},{30,6},{31,7},{32,8},{33... | collective-permute-start | bytes 1032200 | tf_op jit(solution)/shard_map/ppermute | solution.py:205
  111.5 13.2 %collective-permute-start.6 = (bf16[64,1024]{1,0:T(8,128)(2,1)S(1)}, bf16[64,1024]{1,0:T(8,128)(2,1)S(1)}, u32[]{:S(2)}, u32[]{:S(2)}) collective-permute-start(bf16[64,1024]{1,0:T(8,128)(2,1)S(1)} %get-tuple-element.21), channel_id=1, source_target_pairs={{0,8},{1,9},{2,10},{3,11},{4,12},{5,13},{6,14},{7,15},{8,16},{9,17... | collective-permute-start | bytes 393224 | tf_op jit(solution)/shard_map/ppermute | solution.py:196
  113.4 22.5 %collective-permute-start.5 = (bf16[64,1024]{1,0:T(8,128)(2,1)S(1)}, bf16[64,1024]{1,0:T(8,128)(2,1)S(1)}, u32[]{:S(2)}, u32[]{:S(2)}) collective-permute-start(bf16[64,1024]{1,0:T(8,128)(2,1)S(1)} %get-tuple-element.22), channel_id=1, source_target_pairs={{0,16},{1,17},{2,18},{3,19},{4,20},{5,21},{6,22},{7,23},{8,24},{9,... | collective-permute-start | bytes 393224 | tf_op jit(solution)/shard_map/ppermute | solution.py:196
  119.7 24.3 %collective-permute-start.4 = (bf16[64,1024]{1,0:T(8,128)(2,1)S(1)}, bf16[64,1024]{1,0:T(8,128)(2,1)S(1)}, u32[]{:S(2)}, u32[]{:S(2)}) collective-permute-start(bf16[64,1024]{1,0:T(8,128)(2,1)S(1)} %get-tuple-element.23), channel_id=1, source_target_pairs={{0,120},{1,121},{2,122},{3,123},{4,124},{5,125},{6,126},{7,127},{8... | collective-permute-start | bytes 393224 | tf_op jit(solution)/shard_map/ppermute | solution.py:196
  124.7 29.6 %collective-permute-start.11 = (bf16[16,3584]{1,0:T(8,128)(2,1)S(1)}, bf16[16,3584]{1,0:T(8,128)(2,1)S(1)}, u32[]{:S(2)}, u32[]{:S(2)}) collective-permute-start(bf16[16,3584]{1,0:T(8,128)(2,1)S(1)} %collective-permute-done.10), channel_id=1, source_target_pairs={{0,32},{1,33},{2,34},{3,35},{4,36},{5,37},{6,38},{7,39},{8,40},{9,... | collective-permute-start | bytes 344072 | tf_op jit(solution)/shard_map/ppermute | solution.py:205
  146.4 9.4 %collective-permute-start.12 = (bf16[32,128]{1,0:T(8,128)(2,1)S(1)}, bf16[32,128]{1,0:T(8,128)(2,1)S(1)}, u32[]{:S(2)}, u32[]{:S(2)}) collective-permute-start(bf16[32,128]{1,0:T(8,128)(2,1)S(1)} %get-tuple-element.18), channel_id=1, source_target_pairs={{32,0},{33,1},{34,2},{35,3},{36,4},{37,5},{38,6},{39,7},{40,8},{41... | collective-permute-start | bytes 24584 | tf_op jit(solution)/shard_map/ppermute | solution.py:205

commit v7 on v6

--- a/solution.py
+++ b/solution.py
@@ -100,34 +100,22 @@
     return parts
 
 
-def fetch_blocks(weight_ref, fetched_ref, sems):
+def serve_kernel(r0_ref, r1_ref, r2_ref, r3_ref, weight_ref, out_ref, fetched_ref, held_ref, sems):
+    rows = r0_ref.shape[0]
     count = sems.shape[0]
     step = weight_ref.shape[0] // count
     blocks = [pl.ds(j * step, step) for j in range(count)]
     fetches = [pltpu.make_async_copy(weight_ref.at[blocks[j]], fetched_ref.at[blocks[j]], sems.at[j]) for j in range(count)]
-    for fetch in fetches:
-        fetch.start()
-    return list(zip(fetches, blocks))
-
-
-def serve_three_kernel(r0_ref, r1_ref, r2_ref, weight_ref, out_ref, fetched_ref, held_ref, sems):
-    rows = r0_ref.shape[0]
-    fetches = fetch_blocks(weight_ref, fetched_ref, sems)
-    for k, ref in enumerate((r0_ref, r1_ref, r2_ref)):
+    fetches[0].start()
+    fetches[1].start()
+    for k, ref in enumerate((r0_ref, r1_ref, r2_ref, r3_ref)):
         held_ref[k * rows:(k + 1) * rows] = ref[...]
-    for fetch, block in fetches:
-        fetch.wait()
-        for k, part in enumerate(serve_part(fetched_ref[block, :], held_ref[...], rows)):
-            out_ref[:, k, :, block] = part
-
-
-def serve_last_kernel(three_ref, r3_ref, weight_ref, out_ref, fetched_ref, sems):
-    rows = r3_ref.shape[0]
-    fetches = fetch_blocks(weight_ref, fetched_ref, sems)
-    out_ref[:, :3] = three_ref[...]
-    for fetch, block in fetches:
-        fetch.wait()
-        out_ref[:, 3, :, block] = serve_part(fetched_ref[block, :], r3_ref[...], rows)[0]
+    for j in range(count):
+        fetches[j].wait()
+        if j + 2 < count:
+            fetches[j + 2].start()
+        for k, part in enumerate(serve_part(fetched_ref[blocks[j], :], held_ref[...], rows)):
+            out_ref[:, k, :, blocks[j]] = part
 
 
 def back_kernel(meta_ref, chosen_ref, scores_ref, hidden_ref, r0_ref, r1_ref, r2_ref, r3_ref, act_ref, score_ref, score_bf_ref):
@@ -210,15 +198,10 @@
     def spread(value):
         return exchange(value.reshape(nxc, slots, width)).reshape(rows, width)
 
-    def serve_three(*values):
-        scratch = [pltpu.VMEM((hidden_width, width), bf16), pltpu.VMEM((3 * rows, width), bf16), pltpu.SemaphoreType.DMA((2,))]
-        outs = [("held", (nxc, 3, slots, hidden_width), bf16)]
-        return call(serve_three_kernel, outs, *held(*values), ("far", weight), scratch=scratch)[0]
-
-    def serve_last(*values):
-        scratch = [pltpu.VMEM((hidden_width, width), bf16), pltpu.SemaphoreType.DMA((4,))]
+    def serve(*values):
+        scratch = [pltpu.VMEM((hidden_width, width), bf16), pltpu.VMEM((4 * rows, width), bf16), pltpu.SemaphoreType.DMA((4,))]
         outs = [("held", (nxc, 4, slots, hidden_width), bf16)]
-        return call(serve_last_kernel, outs, *held(*values), ("far", weight), scratch=scratch)[0]
+        return call(serve_kernel, outs, *held(*values), ("far", weight), scratch=scratch)[0]
 
     def held(*values):
         return [("held", v) for v in values]
@@ -240,21 +223,19 @@
     early1 = along_z(early, -1)
     first = exchange(first.reshape(nxc, 2, slots, width))
     late1 = along_z(late, -1)
-    rest = along_z(rest, nzl)
+    rest = along_z(rest, (nz - nzl) // 2)
     early2 = along_z(early1, -1)
     near, up = part(first, 0), part(first, 1)
     up = along_z(up, 1)
     one = call(pack_one_kernel, [("held", (rows, width), bf16)], *held(early1, late1))[0]
     one = spread(one)
     late4 = to_end(late1, 3)
-    rest = along_z(rest, nzl)
+    rest4 = to_end(rest, nzl + (nz - nzl) // 2)
     two = call(pack_two_kernel, [("held", (rows, width), bf16)], *held(early2))[0]
     two = spread(two)
     early4 = to_end(early2, 2)
-    three = serve_three(near, up, one)
-    served = serve_last(three, two)
+    served = serve(near, up, one, two)
     served = exchange(served)
-    rest4 = to_end(rest, nz - nzl)
     r0, r1, r3, r2 = (part(served, k) for k in range(4))
     r2 = along_z(r2, 2)
     r1 = along_z(r1, -1)

time: 159 us -> 154 us (0.969)
  the two profiles are of different devices: /device:TPU:50 before, /device:TPU:10 now
where the time goes in v7:
time: 154 us
  starting transfers between devices  79.5 us (52%)
  waiting for transfers between devices  55.1 us (36%)
  Pallas kernels  17 us (11%)
    ppermute x8, starting transfers between devices, along_z(): return lax.ppermute(value, axes, lanes(pairs))  41.5 us
    ppermute x8, waiting for transfers between devices, along_z(): return lax.ppermute(value, axes, lanes(pairs))  41.2 us
    all_to_all x4, starting transfers between devices, exchange(): return lax.all_to_all(value, group, split_axis=0, concat_axis=0, tiled=True)  19.3 us
    ppermute x4, starting transfers between devices, to_end(): return lax.ppermute(value, axes, lanes(pairs))  18.6 us
    pallas_call x6, Pallas kernels, call(): pl.pallas_call(kernel, out_shape=tuple((space[how](shape, dtype) for how,...  17 us
    ppermute x4, waiting for transfers between devices, to_end(): return lax.ppermute(value, axes, lanes(pairs))  7.5 us
    all_to_all x4, waiting for transfers between devices, exchange(): return lax.all_to_all(value, group, split_axis=0, concat_axis=0, tiled=True)  6.41 us
  transfers between devices with their start and end apart: 16, of which 9 were waited for; matrix products, arithmetic and copies ran while one was open for 1% of the time, Pallas kernels for 3%

profile of v7, /device:TPU:10, one launch (start us, length us, event | category | flops | bytes accessed | tf_op | source)
XLA Modules:
  0.0 153.7 jit_solution(17481028347337976644)
XLA Ops:
  0.6 3.0 %shard_map.103 = (bf16[128,3584]{1,0:T(8,128)(2,1)}, bf16[72,3584]{1,0:T(8,128)(2,1)S(1)}, bf16[48,3584]{1,0:T(8,128)(2,1)S(1)}, bf16[16,3584]{1,0:T(8,128)(2,1)S(1)}, s32[8,128]{1,0:T(8,128)}) custom-call(s32[1,128]{1,0:T(1,128)} %chosen_ref.3, s32[1,128]{1,0:T(1,128)} %places_ref.1, s32[32,32]{1,0:T(8,128)} %bitcast.35, bf16[128,3584]{1,0:T(8,128)(2,1)} %bitcast.32), custom_call_target="tpu_custom_call" | custom-call | tf_op jit(solution)/shard_map/pallas_call | solution.py:159
  3.7 4.8 %all-to-all-start = ((bf16[8,2,8,3584]{3,2,1,0:T(8,128)(2,1)}), bf16[8,2,8,3584]{3,2,1,0:T(8,128)(2,1)}, u32[]{:S(2)}, u32[]{:S(2)}) async-start(bf16[8,2,8,3584]{3,2,1,0:T(8,128)(2,1)} %bitcast.5), calls=%async_computation | async-start | bytes 1835008 | tf_op jit(solution)/shard_map/all_to_all | solution.py:196
  8.5 18.2 %collective-permute-start.1 = (bf16[72,3584]{1,0:T(8,128)(2,1)S(1)}, bf16[72,3584]{1,0:T(8,128)(2,1)S(1)}, u32[]{:S(2)}, u32[]{:S(2)}) collective-permute-start(bf16[72,3584]{1,0:T(8,128)(2,1)S(1)} %get-tuple-element.13), channel_id=1, source_target_pairs={{0,120},{1,121},{2,122},{3,123},{4,124},{5,125},{6,126},{7,127},{8... | collective-permute-start | bytes 1548296 | tf_op jit(solution)/shard_map/ppermute | solution.py:184
  26.7 2.5 %collective-permute-start.2 = (bf16[48,3584]{1,0:T(8,128)(2,1)S(1)}, bf16[48,3584]{1,0:T(8,128)(2,1)S(1)}, u32[]{:S(2)}, u32[]{:S(2)}) collective-permute-start(bf16[48,3584]{1,0:T(8,128)(2,1)S(1)} %get-tuple-element.14), channel_id=1, source_target_pairs={{0,120},{1,121},{2,122},{3,123},{4,124},{5,125},{6,126},{7,127},{8... | collective-permute-start | bytes 1032200 | tf_op jit(solution)/shard_map/ppermute | solution.py:184
  29.2 9.6 %collective-permute-done.1.early_ref = bf16[72,3584]{1,0:T(8,128)(2,1)S(1)} collective-permute-done((bf16[72,3584]{1,0:T(8,128)(2,1)S(1)}, bf16[72,3584]{1,0:T(8,128)(2,1)S(1)}, u32[]{:S(2)}, u32[]{:S(2)}) %collective-permute-start.1) | collective-permute-done | bytes 516128 | tf_op jit(solution)/shard_map/ppermute | solution.py:184
  38.8 5.6 %collective-permute-start.3 = (bf16[72,3584]{1,0:T(8,128)(2,1)S(1)}, bf16[72,3584]{1,0:T(8,128)(2,1)S(1)}, u32[]{:S(2)}, u32[]{:S(2)}) collective-permute-start(bf16[72,3584]{1,0:T(8,128)(2,1)S(1)} %collective-permute-done.1.early_ref), channel_id=1, source_target_pairs={{0,120},{1,121},{2,122},{3,123},{4,124},{5,125},{6,126},{7,127},{8... | collective-permute-start | bytes 1548296 | tf_op jit(solution)/shard_map/ppermute | solution.py:184
  44.4 1.8 %collective-permute-done.2.late_ref = bf16[48,3584]{1,0:T(8,128)(2,1)S(1)} collective-permute-done((bf16[48,3584]{1,0:T(8,128)(2,1)S(1)}, bf16[48,3584]{1,0:T(8,128)(2,1)S(1)}, u32[]{:S(2)}, u32[]{:S(2)}) %collective-permute-start.2) | collective-permute-done | bytes 344096 | tf_op jit(solution)/shard_map/ppermute | solution.py:184
  46.2 1.2 shard_map.104
  47.4 0.0 all-to-all-done
  47.4 4.8 %all-to-all-start.1 = ((bf16[8,8,3584]{2,1,0:T(8,128)(2,1)}), bf16[8,8,3584]{2,1,0:T(8,128)(2,1)S(1)}, u32[]{:S(2)}, u32[]{:S(2)}) async-start(bf16[8,8,3584]{2,1,0:T(8,128)(2,1)} %bitcast.8), calls=%async_computation.1 | async-start | bytes 917504 | tf_op jit(solution)/shard_map/all_to_all | solution.py:196
  52.2 1.2 slice_bitcast_fusion
  53.5 0.0 copy-start
  53.5 2.1 %collective-permute-start = (bf16[64,3584]{1,0:T(8,128)(2,1)S(1)}, bf16[64,3584]{1,0:T(8,128)(2,1)S(1)}, u32[]{:S(2)}, u32[]{:S(2)}) collective-permute-start(bf16[64,3584]{1,0:T(8,128)(2,1)S(1)} %get-tuple-element.19), channel_id=1, source_target_pairs={{0,8},{1,9},{2,10},{3,11},{4,12},{5,13},{6,14},{7,15},{8,16},{9,17... | collective-permute-start | bytes 1376264 | tf_op jit(solution)/shard_map/ppermute | solution.py:184
  55.5 0.9 collective-permute-done.3.early_ref
  56.4 1.0 shard_map.105
  57.4 3.0 %all-to-all-done.1 = bf16[8,8,3584]{2,1,0:T(8,128)(2,1)S(1)} async-done(((bf16[8,8,3584]{2,1,0:T(8,128)(2,1)}), bf16[8,8,3584]{2,1,0:T(8,128)(2,1)S(1)}, u32[]{:S(2)}, u32[]{:S(2)}) %all-to-all-start.1) | async-done | bytes 458784 | tf_op jit(solution)/shard_map/all_to_all | solution.py:196
  60.4 4.8 %all-to-all-start.2 = ((bf16[8,8,3584]{2,1,0:T(8,128)(2,1)}), bf16[8,8,3584]{2,1,0:T(8,128)(2,1)S(1)}, u32[]{:S(2)}, u32[]{:S(2)}) async-start(bf16[8,8,3584]{2,1,0:T(8,128)(2,1)} %bitcast.10), calls=%async_computation.2 | async-start | bytes 917504 | tf_op jit(solution)/shard_map/all_to_all | solution.py:196
  65.2 4.7 %collective-permute-done.r1_ref = bf16[64,3584]{1,0:T(8,128)(2,1)S(1)} collective-permute-done((bf16[64,3584]{1,0:T(8,128)(2,1)S(1)}, bf16[64,3584]{1,0:T(8,128)(2,1)S(1)}, u32[]{:S(2)}, u32[]{:S(2)}) %collective-permute-start) | collective-permute-done | bytes 458784 | tf_op jit(solution)/shard_map/ppermute | solution.py:184
  70.0 3.4 %all-to-all-done.2 = bf16[8,8,3584]{2,1,0:T(8,128)(2,1)S(1)} async-done(((bf16[8,8,3584]{2,1,0:T(8,128)(2,1)}), bf16[8,8,3584]{2,1,0:T(8,128)(2,1)S(1)}, u32[]{:S(2)}, u32[]{:S(2)}) %all-to-all-start.2) | async-done | bytes 458784 | tf_op jit(solution)/shard_map/all_to_all | solution.py:196
  73.4 7.1 %shard_map.106 = bf16[8,4,8,1024]{3,2,1,0:T(8,128)(2,1)} custom-call(bf16[64,3584]{1,0:T(8,128)(2,1)S(1)} %get-tuple-element.20.r0_ref, bf16[64,3584]{1,0:T(8,128)(2,1)S(1)} %collective-permute-done.r1_ref, bf16[64,3584]{1,0:T(8,128)(2,1)S(1)} %bitcast.29, bf16[64,3584]{1,0:T(8,128)(2,1)S(1)} %bitcast.30, bf16[1024,3584]{1,0:T(8,128)(2,1)} %bitcast.31), custom_call_target="tpu_custom_call" | custom-call | tf_op jit(solution)/shard_map/pallas_call | solution.py:159
  80.6 4.9 %all-to-all-start.3 = ((bf16[8,4,8,1024]{3,2,1,0:T(8,128)(2,1)}), bf16[8,4,8,1024]{3,2,1,0:T(8,128)(2,1)S(1)}, u32[]{:S(2)}, u32[]{:S(2)}) async-start(bf16[8,4,8,1024]{3,2,1,0:T(8,128)(2,1)} %shard_map.106), calls=%async_computation.3 | async-start | bytes 1048576 | tf_op jit(solution)/shard_map/all_to_all | solution.py:196
  85.4 4.2 %collective-permute-start.7 = (bf16[72,3584]{1,0:T(8,128)(2,1)S(1)}, bf16[72,3584]{1,0:T(8,128)(2,1)S(1)}, u32[]{:S(2)}, u32[]{:S(2)}) collective-permute-start(bf16[72,3584]{1,0:T(8,128)(2,1)S(1)} %collective-permute-done.3.early_ref), channel_id=1, source_target_pairs={{16,0},{17,1},{18,2},{19,3},{20,4},{21,5},{22,6},{23,7},{24,8},{25... | collective-permute-start | bytes 1548296 | tf_op jit(solution)/shard_map/ppermute | solution.py:193
  89.7 1.9 %collective-permute-start.9 = (bf16[16,3584]{1,0:T(8,128)(2,1)S(1)}, bf16[16,3584]{1,0:T(8,128)(2,1)S(1)}, u32[]{:S(2)}, u32[]{:S(2)}) collective-permute-start(bf16[16,3584]{1,0:T(8,128)(2,1)S(1)} %get-tuple-element.17), channel_id=1, source_target_pairs={{0,48},{1,49},{2,50},{3,51},{4,52},{5,53},{6,54},{7,55},{8,56},{9,... | collective-permute-start | bytes 344072 | tf_op jit(solution)/shard_map/ppermute | solution.py:184
  91.6 4.9 %collective-permute-start.8 = (bf16[48,3584]{1,0:T(8,128)(2,1)S(1)}, bf16[48,3584]{1,0:T(8,128)(2,1)S(1)}, u32[]{:S(2)}, u32[]{:S(2)}) collective-permute-start(bf16[48,3584]{1,0:T(8,128)(2,1)S(1)} %collective-permute-done.2.late_ref), channel_id=1, source_target_pairs={{24,0},{25,1},{26,2},{27,3},{28,4},{29,5},{30,6},{31,7},{32,8},{33... | collective-permute-start | bytes 1032200 | tf_op jit(solution)/shard_map/ppermute | solution.py:193
  96.5 0.0 all-to-all-done.3
  96.5 1.9 %collective-permute-start.6 = (bf16[64,1024]{1,0:T(8,128)(2,1)S(1)}, bf16[64,1024]{1,0:T(8,128)(2,1)S(1)}, u32[]{:S(2)}, u32[]{:S(2)}) collective-permute-start(bf16[64,1024]{1,0:T(8,128)(2,1)S(1)} %get-tuple-element.21), channel_id=1, source_target_pairs={{0,8},{1,9},{2,10},{3,11},{4,12},{5,13},{6,14},{7,15},{8,16},{9,17... | collective-permute-start | bytes 393224 | tf_op jit(solution)/shard_map/ppermute | solution.py:184
  98.5 3.4 %collective-permute-start.5 = (bf16[64,1024]{1,0:T(8,128)(2,1)S(1)}, bf16[64,1024]{1,0:T(8,128)(2,1)S(1)}, u32[]{:S(2)}, u32[]{:S(2)}) collective-permute-start(bf16[64,1024]{1,0:T(8,128)(2,1)S(1)} %get-tuple-element.22), channel_id=1, source_target_pairs={{0,16},{1,17},{2,18},{3,19},{4,20},{5,21},{6,22},{7,23},{8,24},{9,... | collective-permute-start | bytes 393224 | tf_op jit(solution)/shard_map/ppermute | solution.py:184
  101.9 2.6 %collective-permute-done.9 = bf16[16,3584]{1,0:T(8,128)(2,1)S(1)} collective-permute-done((bf16[16,3584]{1,0:T(8,128)(2,1)S(1)}, bf16[16,3584]{1,0:T(8,128)(2,1)S(1)}, u32[]{:S(2)}, u32[]{:S(2)}) %collective-permute-start.9) | collective-permute-done | bytes 114720 | tf_op jit(solution)/shard_map/ppermute | solution.py:184
  104.5 5.9 %collective-permute-start.4 = (bf16[64,1024]{1,0:T(8,128)(2,1)S(1)}, bf16[64,1024]{1,0:T(8,128)(2,1)S(1)}, u32[]{:S(2)}, u32[]{:S(2)}) collective-permute-start(bf16[64,1024]{1,0:T(8,128)(2,1)S(1)} %get-tuple-element.23), channel_id=1, source_target_pairs={{0,120},{1,121},{2,122},{3,123},{4,124},{5,125},{6,126},{7,127},{8... | collective-permute-start | bytes 393224 | tf_op jit(solution)/shard_map/ppermute | solution.py:184
  110.4 0.0 collective-permute-done.6.r3_ref
  110.4 7.6 %collective-permute-start.10 = (bf16[16,3584]{1,0:T(8,128)(2,1)S(1)}, bf16[16,3584]{1,0:T(8,128)(2,1)S(1)}, u32[]{:S(2)}, u32[]{:S(2)}) collective-permute-start(bf16[16,3584]{1,0:T(8,128)(2,1)S(1)} %collective-permute-done.9), channel_id=1, source_target_pairs={{0,48},{1,49},{2,50},{3,51},{4,52},{5,53},{6,54},{7,55},{8,56},{9,... | collective-permute-start | bytes 344072 | tf_op jit(solution)/shard_map/ppermute | solution.py:193
  118.1 0.0 collective-permute-done.5.r2_ref
  118.1 21.6 %collective-permute-done.4.r1_ref = bf16[64,1024]{1,0:T(8,128)(2,1)S(1)} collective-permute-done((bf16[64,1024]{1,0:T(8,128)(2,1)S(1)}, bf16[64,1024]{1,0:T(8,128)(2,1)S(1)}, u32[]{:S(2)}, u32[]{:S(2)}) %collective-permute-start.4) | collective-permute-done | bytes 131104 | tf_op jit(solution)/shard_map/ppermute | solution.py:184
  139.6 2.3 %shard_map.107 = (bf16[128,1024]{1,0:T(8,128)(2,1)}, f32[32,128]{1,0:T(8,128)}, bf16[32,128]{1,0:T(8,128)(2,1)S(1)}) custom-call(s32[8,128]{1,0:T(8,128)} %get-tuple-element.11.meta_ref, s32[1,128]{1,0:T(1,128)} %chosen_ref.3, f32[32,128]{1,0:T(8,128)} %bitcast.36, bf16[128,1024]{1,0:T(8,128)(2,1)} %bitcast.34, ...), custom_call_target="tpu_custom_call" | custom-call | tf_op jit(solution)/shard_map/pallas_call | solution.py:159
  142.0 1.9 %collective-permute-start.11 = (bf16[32,128]{1,0:T(8,128)(2,1)S(1)}, bf16[32,128]{1,0:T(8,128)(2,1)S(1)}, u32[]{:S(2)}, u32[]{:S(2)}) collective-permute-start(bf16[32,128]{1,0:T(8,128)(2,1)S(1)} %get-tuple-element.18), channel_id=1, source_target_pairs={{32,0},{33,1},{34,2},{35,3},{36,4},{37,5},{38,6},{39,7},{40,8},{41... | collective-permute-start | bytes 24584 | tf_op jit(solution)/shard_map/ppermute | solution.py:193
  143.9 0.0 collective-permute-done.10.rest_ref
  143.9 0.0 collective-permute-done.8.late_ref
  143.9 0.0 collective-permute-done.7.early_ref
  143.9 7.5 %collective-permute-done.11.score_ref = bf16[32,128]{1,0:T(8,128)(2,1)S(1)} collective-permute-done((bf16[32,128]{1,0:T(8,128)(2,1)S(1)}, bf16[32,128]{1,0:T(8,128)(2,1)S(1)}, u32[]{:S(2)}, u32[]{:S(2)}) %collective-permute-start.11) | collective-permute-done | bytes 8224 | tf_op jit(solution)/shard_map/ppermute | solution.py:193
  151.4 0.0 copy-done
  151.4 2.2 %shard_map.108 = bf16[128,3584]{1,0:T(8,128)(2,1)} custom-call(bf16[72,3584]{1,0:T(8,128)(2,1)S(1)} %collective-permute-done.7.early_ref, bf16[48,3584]{1,0:T(8,128)(2,1)S(1)} %collective-permute-done.8.late_ref, bf16[16,3584]{1,0:T(8,128)(2,1)S(1)} %collective-permute-done.10.rest_ref, bf16[32,128]{1,0:T(8,128)(2,1)S(1)} %collective-permute-done.11.score_ref, ...), custom_call_target="tpu_custom_call" | custom-call | tf_op jit(solution)/shard_map/pallas_call | solution.py:159
  (1 shorter events, 0.0 us)
Async XLA Ops:
  3.7 43.8 %all-to-all-start = ((bf16[8,2,8,3584]{3,2,1,0:T(8,128)(2,1)}), bf16[8,2,8,3584]{3,2,1,0:T(8,128)(2,1)}, u32[]{:S(2)}, u32[]{:S(2)}) async-start(bf16[8,2,8,3584]{3,2,1,0:T(8,128)(2,1)} %bitcast.5), calls=%async_computation | async-start | bytes 1835008 | tf_op jit(solution)/shard_map/all_to_all | solution.py:196
  8.5 30.3 %collective-permute-start.1 = (bf16[72,3584]{1,0:T(8,128)(2,1)S(1)}, bf16[72,3584]{1,0:T(8,128)(2,1)S(1)}, u32[]{:S(2)}, u32[]{:S(2)}) collective-permute-start(bf16[72,3584]{1,0:T(8,128)(2,1)S(1)} %get-tuple-element.13), channel_id=1, source_target_pairs={{0,120},{1,121},{2,122},{3,123},{4,124},{5,125},{6,126},{7,127},{8... | collective-permute-start | bytes 1548296 | tf_op jit(solution)/shard_map/ppermute | solution.py:184
  26.7 19.5 %collective-permute-start.2 = (bf16[48,3584]{1,0:T(8,128)(2,1)S(1)}, bf16[48,3584]{1,0:T(8,128)(2,1)S(1)}, u32[]{:S(2)}, u32[]{:S(2)}) collective-permute-start(bf16[48,3584]{1,0:T(8,128)(2,1)S(1)} %get-tuple-element.14), channel_id=1, source_target_pairs={{0,120},{1,121},{2,122},{3,123},{4,124},{5,125},{6,126},{7,127},{8... | collective-permute-start | bytes 1032200 | tf_op jit(solution)/shard_map/ppermute | solution.py:184
  38.8 17.6 %collective-permute-start.3 = (bf16[72,3584]{1,0:T(8,128)(2,1)S(1)}, bf16[72,3584]{1,0:T(8,128)(2,1)S(1)}, u32[]{:S(2)}, u32[]{:S(2)}) collective-permute-start(bf16[72,3584]{1,0:T(8,128)(2,1)S(1)} %collective-permute-done.1.early_ref), channel_id=1, source_target_pairs={{0,120},{1,121},{2,122},{3,123},{4,124},{5,125},{6,126},{7,127},{8... | collective-permute-start | bytes 1548296 | tf_op jit(solution)/shard_map/ppermute | solution.py:184
  47.4 13.0 %all-to-all-start.1 = ((bf16[8,8,3584]{2,1,0:T(8,128)(2,1)}), bf16[8,8,3584]{2,1,0:T(8,128)(2,1)S(1)}, u32[]{:S(2)}, u32[]{:S(2)}) async-start(bf16[8,8,3584]{2,1,0:T(8,128)(2,1)} %bitcast.8), calls=%async_computation.1 | async-start | bytes 917504 | tf_op jit(solution)/shard_map/all_to_all | solution.py:196
  53.5 97.9 %copy-start = (bf16[32,3584]{1,0:T(8,128)(2,1)S(1)}, bf16[32,3584]{1,0:T(8,128)(2,1)}, u32[]{:S(2)}) copy-start(bf16[32,3584]{1,0:T(8,128)(2,1)} %router_ref.1) | copy-start | bytes 688132
  53.5 16.5 %collective-permute-start = (bf16[64,3584]{1,0:T(8,128)(2,1)S(1)}, bf16[64,3584]{1,0:T(8,128)(2,1)S(1)}, u32[]{:S(2)}, u32[]{:S(2)}) collective-permute-start(bf16[64,3584]{1,0:T(8,128)(2,1)S(1)} %get-tuple-element.19), channel_id=1, source_target_pairs={{0,8},{1,9},{2,10},{3,11},{4,12},{5,13},{6,14},{7,15},{8,16},{9,17... | collective-permute-start | bytes 1376264 | tf_op jit(solution)/shard_map/ppermute | solution.py:184
  60.4 13.0 %all-to-all-start.2 = ((bf16[8,8,3584]{2,1,0:T(8,128)(2,1)}), bf16[8,8,3584]{2,1,0:T(8,128)(2,1)S(1)}, u32[]{:S(2)}, u32[]{:S(2)}) async-start(bf16[8,8,3584]{2,1,0:T(8,128)(2,1)} %bitcast.10), calls=%async_computation.2 | async-start | bytes 917504 | tf_op jit(solution)/shard_map/all_to_all | solution.py:196
  80.6 15.9 %all-to-all-start.3 = ((bf16[8,4,8,1024]{3,2,1,0:T(8,128)(2,1)}), bf16[8,4,8,1024]{3,2,1,0:T(8,128)(2,1)S(1)}, u32[]{:S(2)}, u32[]{:S(2)}) async-start(bf16[8,4,8,1024]{3,2,1,0:T(8,128)(2,1)} %shard_map.106), calls=%async_computation.3 | async-start | bytes 1048576 | tf_op jit(solution)/shard_map/all_to_all | solution.py:196
  85.4 58.5 %collective-permute-start.7 = (bf16[72,3584]{1,0:T(8,128)(2,1)S(1)}, bf16[72,3584]{1,0:T(8,128)(2,1)S(1)}, u32[]{:S(2)}, u32[]{:S(2)}) collective-permute-start(bf16[72,3584]{1,0:T(8,128)(2,1)S(1)} %collective-permute-done.3.early_ref), channel_id=1, source_target_pairs={{16,0},{17,1},{18,2},{19,3},{20,4},{21,5},{22,6},{23,7},{24,8},{25... | collective-permute-start | bytes 1548296 | tf_op jit(solution)/shard_map/ppermute | solution.py:193
  89.7 14.8 %collective-permute-start.9 = (bf16[16,3584]{1,0:T(8,128)(2,1)S(1)}, bf16[16,3584]{1,0:T(8,128)(2,1)S(1)}, u32[]{:S(2)}, u32[]{:S(2)}) collective-permute-start(bf16[16,3584]{1,0:T(8,128)(2,1)S(1)} %get-tuple-element.17), channel_id=1, source_target_pairs={{0,48},{1,49},{2,50},{3,51},{4,52},{5,53},{6,54},{7,55},{8,56},{9,... | collective-permute-start | bytes 344072 | tf_op jit(solution)/shard_map/ppermute | solution.py:184
  91.6 52.3 %collective-permute-start.8 = (bf16[48,3584]{1,0:T(8,128)(2,1)S(1)}, bf16[48,3584]{1,0:T(8,128)(2,1)S(1)}, u32[]{:S(2)}, u32[]{:S(2)}) collective-permute-start(bf16[48,3584]{1,0:T(8,128)(2,1)S(1)} %collective-permute-done.2.late_ref), channel_id=1, source_target_pairs={{24,0},{25,1},{26,2},{27,3},{28,4},{29,5},{30,6},{31,7},{32,8},{33... | collective-permute-start | bytes 1032200 | tf_op jit(solution)/shard_map/ppermute | solution.py:193
  96.5 13.9 %collective-permute-start.6 = (bf16[64,1024]{1,0:T(8,128)(2,1)S(1)}, bf16[64,1024]{1,0:T(8,128)(2,1)S(1)}, u32[]{:S(2)}, u32[]{:S(2)}) collective-permute-start(bf16[64,1024]{1,0:T(8,128)(2,1)S(1)} %get-tuple-element.21), channel_id=1, source_target_pairs={{0,8},{1,9},{2,10},{3,11},{4,12},{5,13},{6,14},{7,15},{8,16},{9,17... | collective-permute-start | bytes 393224 | tf_op jit(solution)/shard_map/ppermute | solution.py:184
  98.5 19.6 %collective-permute-start.5 = (bf16[64,1024]{1,0:T(8,128)(2,1)S(1)}, bf16[64,1024]{1,0:T(8,128)(2,1)S(1)}, u32[]{:S(2)}, u32[]{:S(2)}) collective-permute-start(bf16[64,1024]{1,0:T(8,128)(2,1)S(1)} %get-tuple-element.22), channel_id=1, source_target_pairs={{0,16},{1,17},{2,18},{3,19},{4,20},{5,21},{6,22},{7,23},{8,24},{9,... | collective-permute-start | bytes 393224 | tf_op jit(solution)/shard_map/ppermute | solution.py:184
  104.5 35.1 %collective-permute-start.4 = (bf16[64,1024]{1,0:T(8,128)(2,1)S(1)}, bf16[64,1024]{1,0:T(8,128)(2,1)S(1)}, u32[]{:S(2)}, u32[]{:S(2)}) collective-permute-start(bf16[64,1024]{1,0:T(8,128)(2,1)S(1)} %get-tuple-element.23), channel_id=1, source_target_pairs={{0,120},{1,121},{2,122},{3,123},{4,124},{5,125},{6,126},{7,127},{8... | collective-permute-start | bytes 393224 | tf_op jit(solution)/shard_map/ppermute | solution.py:184
  110.4 33.5 %collective-permute-start.10 = (bf16[16,3584]{1,0:T(8,128)(2,1)S(1)}, bf16[16,3584]{1,0:T(8,128)(2,1)S(1)}, u32[]{:S(2)}, u32[]{:S(2)}) collective-permute-start(bf16[16,3584]{1,0:T(8,128)(2,1)S(1)} %collective-permute-done.9), channel_id=1, source_target_pairs={{0,48},{1,49},{2,50},{3,51},{4,52},{5,53},{6,54},{7,55},{8,56},{9,... | collective-permute-start | bytes 344072 | tf_op jit(solution)/shard_map/ppermute | solution.py:193
  142.0 9.4 %collective-permute-start.11 = (bf16[32,128]{1,0:T(8,128)(2,1)S(1)}, bf16[32,128]{1,0:T(8,128)(2,1)S(1)}, u32[]{:S(2)}, u32[]{:S(2)}) collective-permute-start(bf16[32,128]{1,0:T(8,128)(2,1)S(1)} %get-tuple-element.18), channel_id=1, source_target_pairs={{32,0},{33,1},{34,2},{35,3},{36,4},{37,5},{38,6},{39,7},{40,8},{41... | collective-permute-start | bytes 24584 | tf_op jit(solution)/shard_map/ppermute | solution.py:193

commit v8 on v5

--- a/solution.py
+++ b/solution.py
@@ -60,8 +60,7 @@
     ordered = jnp.dot(perm, tok, preferred_element_type=jnp.float32).astype(jnp.bfloat16)
     early_ref[:half] = ordered[:half]
     early_ref[half:] = jnp.zeros((8, width), jnp.bfloat16)
-    table = jnp.where(row_id < 2, moved, jnp.where(row_id == 2, rank, 0.0)).astype(jnp.bfloat16)
-    early_ref[half:, :tokens] = table
+    early_ref[half:, :tokens] = moved.astype(jnp.bfloat16)
     late_ref[...] = ordered[half:]
     target = jnp.where(live & (offset < 2), (2 * dest + offset) * slots + places, -1)
     pick = as_pick(lax.broadcasted_iota(jnp.int32, (rows, tokens), 0) == target)
@@ -69,7 +68,7 @@
     back = jnp.where(row_id == 0, slot_of(0), -1)
     for k in (1, 2, 3):
         back = jnp.where(row_id == k, slot_of(k), back)
-    meta_ref[...] = back
+    meta_ref[...] = jnp.where(row_id == 4, rank.astype(jnp.int32), back)
 
 
 def pack_one_kernel(early_ref, late_ref, out_ref):
@@ -95,16 +94,18 @@
     step = weight_ref.shape[0] // count
     blocks = [pl.ds(j * step, step) for j in range(count)]
     fetches = [pltpu.make_async_copy(weight_ref.at[blocks[j]], fetched_ref.at[blocks[j]], sems.at[j]) for j in range(count)]
-    for fetch in fetches:
-        fetch.start()
+    fetches[0].start()
+    fetches[1].start()
     for k, ref in enumerate((r0_ref, r1_ref, r2_ref, r3_ref)):
         held_ref[k * rows:(k + 1) * rows] = ref[...]
-    for fetch, block in zip(fetches, blocks):
-        fetch.wait()
-        found = lax.dot_general(fetched_ref[block, :], held_ref[...], NT, preferred_element_type=jnp.float32).T
+    for j in range(count):
+        fetches[j].wait()
+        if j + 2 < count:
+            fetches[j + 2].start()
+        found = lax.dot_general(fetched_ref[blocks[j], :], held_ref[...], NT, preferred_element_type=jnp.float32).T
         for k in range(4):
             part = found[k * rows:(k + 1) * rows].reshape(rows // slots, slots, step)
-            out_ref[:, k, :, block] = part.astype(jnp.bfloat16)
+            out_ref[:, k, :, blocks[j]] = part.astype(jnp.bfloat16)
 
 
 def back_kernel(meta_ref, chosen_ref, scores_ref, hidden_ref, r0_ref, r1_ref, r2_ref, r3_ref, act_ref, score_ref, score_bf_ref):
@@ -125,16 +126,19 @@
     slope = route_row * route_scale * sigmoid_vals * (1.0 - sigmoid_vals)
     score = jnp.where(onehot, slope, 0.0)
     score_ref[...] = score
-    score_bf_ref[...] = score.astype(jnp.bfloat16)
+    score_bf_ref[:experts] = score.astype(jnp.bfloat16)
+    order = jnp.broadcast_to(meta_ref[4:5, :].astype(jnp.float32), (8, tokens))
+    score_bf_ref[experts:] = order.astype(jnp.bfloat16)
 
 
 def up_kernel(early_ref, late_ref, score_ref, router_ref, out_ref):
-    half = late_ref.shape[0]
-    tokens = 2 * half
-    rank = column(early_ref[half:, :tokens].astype(jnp.float32)[2:3, :], tokens).astype(jnp.int32)
+    half = early_ref.shape[0]
+    tokens = out_ref.shape[0]
+    experts = router_ref.shape[0]
+    rank = column(score_ref[experts:, :].astype(jnp.float32)[:1, :], tokens).astype(jnp.int32)
     pick = as_pick(lax.broadcasted_iota(jnp.int32, (tokens, tokens), 1) == rank)
-    scores = score_ref[...].astype(jnp.float32).T.astype(jnp.bfloat16)
-    out = jnp.dot(pick[:, :half], early_ref[:half], preferred_element_type=jnp.float32)
+    scores = score_ref[:experts, :].astype(jnp.float32).T.astype(jnp.bfloat16)
+    out = jnp.dot(pick[:, :half], early_ref[...], preferred_element_type=jnp.float32)
     out = out + jnp.dot(pick[:, half:], late_ref[...], preferred_element_type=jnp.float32)
     out = out + jnp.dot(scores, router_ref[...], preferred_element_type=jnp.float32)
     out_ref[...] = out.astype(jnp.bfloat16)
@@ -220,7 +224,7 @@
     late4 = to_end(late1, 3)
     two = call(pack_two_kernel, [("held", (rows, width), bf16)], *held(early2))[0]
     two = spread(two)
-    early4 = to_end(early2, 2)
+    early4 = to_end(early2[:half], 2)
     served = serve(near, up, one, two)
     served = exchange(served)
     r0, r1, r3, r2 = (part(served, k) for k in range(4))
@@ -231,7 +235,7 @@
     outs = [
         ("near", (tokens, hidden_width), bf16),
         ("near", (experts, tokens), jnp.float32),
-        ("held", (experts, tokens), bf16),
+        ("held", (experts + 8, tokens), bf16),
     ]
     ins = near_by(meta, expert_ids, scores[0].T, hidden_act[0]) + held(r0, r1, r2, r3)
     act, score, score_bf = call(back_kernel, outs, *ins)

time: 164 us -> 162 us (0.988)
  the two profiles are of different devices: /device:TPU:10 before, /device:TPU:58 now
where the time goes in v8:
time: 162 us; the launch traced here: 161 us
  waiting for transfers between devices  71.8 us (44%)
  starting transfers between devices  70.8 us (44%)
  Pallas kernels  16.7 us (10%)
    ppermute x7, waiting for transfers between devices, along_z(): return lax.ppermute(value, axes, lanes(pairs))  59.3 us
    ppermute x7, starting transfers between devices, along_z(): return lax.ppermute(value, axes, lanes(pairs))  37.8 us
    all_to_all x4, starting transfers between devices, exchange(): return lax.all_to_all(value, group, split_axis=0, concat_axis=0, tiled=True)  19.3 us
    pallas_call x6, Pallas kernels, call(): pl.pallas_call(kernel, out_shape=tuple((space[how](shape, dtype) for how,...  16.7 us
    ppermute x3, starting transfers between devices, to_end(): return lax.ppermute(value, axes, lanes(pairs))  13.7 us
    all_to_all x4, waiting for transfers between devices, exchange(): return lax.all_to_all(value, group, split_axis=0, concat_axis=0, tiled=True)  6.71 us
    ppermute x3, waiting for transfers between devices, to_end(): return lax.ppermute(value, axes, lanes(pairs))  5.8 us
  transfers between devices with their start and end apart: 14, of which 9 were waited for; matrix products, arithmetic and copies ran while one was open for 1% of the time, Pallas kernels for 3%

profile of v8, /device:TPU:58, one launch (start us, length us, event | category | flops | bytes accessed | tf_op | source)
XLA Modules:
  0.0 161.1 jit_solution(2795615585752104016)
XLA Ops:
  0.6 3.0 %shard_map.103 = (bf16[128,3584]{1,0:T(8,128)(2,1)}, bf16[72,3584]{1,0:T(8,128)(2,1)S(1)}, bf16[64,3584]{1,0:T(8,128)(2,1)S(1)}, s32[8,128]{1,0:T(8,128)}) custom-call(s32[1,128]{1,0:T(1,128)} %chosen_ref.3, s32[1,128]{1,0:T(1,128)} %places_ref.1, s32[32,32]{1,0:T(8,128)} %bitcast.35, bf16[128,3584]{1,0:T(8,128)(2,1)} %bitcast.33), custom_call_target="tpu_custom_call" | custom-call | tf_op jit(solution)/shard_map/pallas_call | solution.py:150
  3.7 4.8 %all-to-all-start = ((bf16[8,2,8,3584]{3,2,1,0:T(8,128)(2,1)}), bf16[8,2,8,3584]{3,2,1,0:T(8,128)(2,1)S(1)}, u32[]{:S(2)}, u32[]{:S(2)}) async-start(bf16[8,2,8,3584]{3,2,1,0:T(8,128)(2,1)} %bitcast.5), calls=%async_computation | async-start | bytes 1835008 | tf_op jit(solution)/shard_map/all_to_all | solution.py:186
  8.5 18.2 %collective-permute-start.1 = (bf16[72,3584]{1,0:T(8,128)(2,1)S(1)}, bf16[72,3584]{1,0:T(8,128)(2,1)S(1)}, u32[]{:S(2)}, u32[]{:S(2)}) collective-permute-start(bf16[72,3584]{1,0:T(8,128)(2,1)S(1)} %get-tuple-element.12), channel_id=1, source_target_pairs={{0,120},{1,121},{2,122},{3,123},{4,124},{5,125},{6,126},{7,127},{8... | collective-permute-start | bytes 1548296 | tf_op jit(solution)/shard_map/ppermute | solution.py:174
  26.7 2.5 %collective-permute-start.2 = (bf16[64,3584]{1,0:T(8,128)(2,1)S(1)}, bf16[64,3584]{1,0:T(8,128)(2,1)S(1)}, u32[]{:S(2)}, u32[]{:S(2)}) collective-permute-start(bf16[64,3584]{1,0:T(8,128)(2,1)S(1)} %get-tuple-element.13), channel_id=1, source_target_pairs={{0,120},{1,121},{2,122},{3,123},{4,124},{5,125},{6,126},{7,127},{8... | collective-permute-start | bytes 1376264 | tf_op jit(solution)/shard_map/ppermute | solution.py:174
  29.2 9.6 %collective-permute-done.1.early_ref = bf16[72,3584]{1,0:T(8,128)(2,1)S(1)} collective-permute-done((bf16[72,3584]{1,0:T(8,128)(2,1)S(1)}, bf16[72,3584]{1,0:T(8,128)(2,1)S(1)}, u32[]{:S(2)}, u32[]{:S(2)}) %collective-permute-start.1) | collective-permute-done | bytes 516128 | tf_op jit(solution)/shard_map/ppermute | solution.py:174
  38.8 5.6 %collective-permute-start.3 = (bf16[72,3584]{1,0:T(8,128)(2,1)S(1)}, bf16[72,3584]{1,0:T(8,128)(2,1)S(1)}, u32[]{:S(2)}, u32[]{:S(2)}) collective-permute-start(bf16[72,3584]{1,0:T(8,128)(2,1)S(1)} %collective-permute-done.1.early_ref), channel_id=1, source_target_pairs={{0,120},{1,121},{2,122},{3,123},{4,124},{5,125},{6,126},{7,127},{8... | collective-permute-start | bytes 1548296 | tf_op jit(solution)/shard_map/ppermute | solution.py:174
  44.4 4.2 %collective-permute-done.2.late_ref = bf16[64,3584]{1,0:T(8,128)(2,1)S(1)} collective-permute-done((bf16[64,3584]{1,0:T(8,128)(2,1)S(1)}, bf16[64,3584]{1,0:T(8,128)(2,1)S(1)}, u32[]{:S(2)}, u32[]{:S(2)}) %collective-permute-start.2) | collective-permute-done | bytes 458784 | tf_op jit(solution)/shard_map/ppermute | solution.py:174
  48.7 1.2 shard_map.104
  49.9 0.0 all-to-all-done
  49.9 4.8 %all-to-all-start.1 = ((bf16[8,8,3584]{2,1,0:T(8,128)(2,1)}), bf16[8,8,3584]{2,1,0:T(8,128)(2,1)S(1)}, u32[]{:S(2)}, u32[]{:S(2)}) async-start(bf16[8,8,3584]{2,1,0:T(8,128)(2,1)} %bitcast.8), calls=%async_computation.1 | async-start | bytes 917504 | tf_op jit(solution)/shard_map/all_to_all | solution.py:186
  54.7 0.8 slice_bitcast_fusion
  55.5 1.9 %collective-permute-start = (bf16[64,3584]{1,0:T(8,128)(2,1)}, bf16[64,3584]{1,0:T(8,128)(2,1)S(1)}, u32[]{:S(2)}, u32[]{:S(2)}) collective-permute-start(bf16[64,3584]{1,0:T(8,128)(2,1)} %get-tuple-element.17), channel_id=1, source_target_pairs={{0,8},{1,9},{2,10},{3,11},{4,12},{5,13},{6,14},{7,15},{8,16},{9,17... | collective-permute-start | bytes 1376264 | tf_op jit(solution)/shard_map/ppermute | solution.py:174
  57.4 1.4 collective-permute-done.3.early_ref
  58.9 1.0 shard_map.105
  59.9 0.0 copy-start
  59.9 2.9 %all-to-all-done.1 = bf16[8,8,3584]{2,1,0:T(8,128)(2,1)S(1)} async-done(((bf16[8,8,3584]{2,1,0:T(8,128)(2,1)}), bf16[8,8,3584]{2,1,0:T(8,128)(2,1)S(1)}, u32[]{:S(2)}, u32[]{:S(2)}) %all-to-all-start.1) | async-done | bytes 458784 | tf_op jit(solution)/shard_map/all_to_all | solution.py:186
  62.8 4.8 %all-to-all-start.2 = ((bf16[8,8,3584]{2,1,0:T(8,128)(2,1)}), bf16[8,8,3584]{2,1,0:T(8,128)(2,1)S(1)}, u32[]{:S(2)}, u32[]{:S(2)}) async-start(bf16[8,8,3584]{2,1,0:T(8,128)(2,1)} %bitcast.10), calls=%async_computation.2 | async-start | bytes 917504 | tf_op jit(solution)/shard_map/all_to_all | solution.py:186
  67.7 4.4 %collective-permute-done.r1_ref = bf16[64,3584]{1,0:T(8,128)(2,1)S(1)} collective-permute-done((bf16[64,3584]{1,0:T(8,128)(2,1)}, bf16[64,3584]{1,0:T(8,128)(2,1)S(1)}, u32[]{:S(2)}, u32[]{:S(2)}) %collective-permute-start) | collective-permute-done | bytes 458784 | tf_op jit(solution)/shard_map/ppermute | solution.py:174
  72.1 3.8 %all-to-all-done.2 = bf16[8,8,3584]{2,1,0:T(8,128)(2,1)S(1)} async-done(((bf16[8,8,3584]{2,1,0:T(8,128)(2,1)}), bf16[8,8,3584]{2,1,0:T(8,128)(2,1)S(1)}, u32[]{:S(2)}, u32[]{:S(2)}) %all-to-all-start.2) | async-done | bytes 458784 | tf_op jit(solution)/shard_map/all_to_all | solution.py:186
  75.9 7.1 %shard_map.106 = bf16[8,4,8,1024]{3,2,1,0:T(8,128)(2,1)} custom-call(bf16[64,3584]{1,0:T(8,128)(2,1)S(1)} %get-tuple-element.18.r0_ref, bf16[64,3584]{1,0:T(8,128)(2,1)S(1)} %collective-permute-done.r1_ref, bf16[64,3584]{1,0:T(8,128)(2,1)S(1)} %bitcast.29, bf16[64,3584]{1,0:T(8,128)(2,1)S(1)} %bitcast.30, bf16[1024,3584]{1,0:T(8,128)(2,1)} %bitcast.31), custom_call_target="tpu_custom_call" | custom-call | tf_op jit(solution)/shard_map/pallas_call | solution.py:150
  83.0 4.9 %all-to-all-start.3 = ((bf16[8,4,8,1024]{3,2,1,0:T(8,128)(2,1)}), bf16[8,4,8,1024]{3,2,1,0:T(8,128)(2,1)S(1)}, u32[]{:S(2)}, u32[]{:S(2)}) async-start(bf16[8,4,8,1024]{3,2,1,0:T(8,128)(2,1)} %shard_map.106), calls=%async_computation.3 | async-start | bytes 1048576 | tf_op jit(solution)/shard_map/all_to_all | solution.py:186
  87.9 5.1 %collective-permute-start.8 = (bf16[64,3584]{1,0:T(8,128)(2,1)S(1)}, bf16[64,3584]{1,0:T(8,128)(2,1)S(1)}, u32[]{:S(2)}, u32[]{:S(2)}) collective-permute-start(bf16[64,3584]{1,0:T(8,128)(2,1)S(1)} %collective-permute-done.2.late_ref), channel_id=1, source_target_pairs={{24,0},{25,1},{26,2},{27,3},{28,4},{29,5},{30,6},{31,7},{32,8},{33... | collective-permute-start | bytes 1376264 | tf_op jit(solution)/shard_map/ppermute | solution.py:183
  93.0 4.9 %collective-permute-start.7 = (bf16[64,3584]{1,0:T(8,128)(2,1)S(1)}, bf16[64,3584]{1,0:T(8,128)(2,1)S(1)}, u32[]{:S(2)}, u32[]{:S(2)}) collective-permute-start(bf16[64,3584]{1,0:T(8,128)(2,1)S(1)} %slice.34), channel_id=1, source_target_pairs={{16,0},{17,1},{18,2},{19,3},{20,4},{21,5},{22,6},{23,7},{24,8},{25... | collective-permute-start | bytes 1376264 | tf_op jit(solution)/shard_map/ppermute | solution.py:183
  97.9 0.0 all-to-all-done.3
  98.0 1.9 %collective-permute-start.6 = (bf16[64,1024]{1,0:T(8,128)(2,1)S(1)}, bf16[64,1024]{1,0:T(8,128)(2,1)S(1)}, u32[]{:S(2)}, u32[]{:S(2)}) collective-permute-start(bf16[64,1024]{1,0:T(8,128)(2,1)S(1)} %get-tuple-element.19), channel_id=1, source_target_pairs={{0,8},{1,9},{2,10},{3,11},{4,12},{5,13},{6,14},{7,15},{8,16},{9,17... | collective-permute-start | bytes 393224 | tf_op jit(solution)/shard_map/ppermute | solution.py:174
  99.9 3.3 %collective-permute-start.5 = (bf16[64,1024]{1,0:T(8,128)(2,1)S(1)}, bf16[64,1024]{1,0:T(8,128)(2,1)S(1)}, u32[]{:S(2)}, u32[]{:S(2)}) collective-permute-start(bf16[64,1024]{1,0:T(8,128)(2,1)S(1)} %get-tuple-element.20), channel_id=1, source_target_pairs={{0,16},{1,17},{2,18},{3,19},{4,20},{5,21},{6,22},{7,23},{8,24},{9,... | collective-permute-start | bytes 393224 | tf_op jit(solution)/shard_map/ppermute | solution.py:174
  103.3 4.3 %collective-permute-start.4 = (bf16[64,1024]{1,0:T(8,128)(2,1)S(1)}, bf16[64,1024]{1,0:T(8,128)(2,1)S(1)}, u32[]{:S(2)}, u32[]{:S(2)}) collective-permute-start(bf16[64,1024]{1,0:T(8,128)(2,1)S(1)} %get-tuple-element.21), channel_id=1, source_target_pairs={{0,120},{1,121},{2,122},{3,123},{4,124},{5,125},{6,126},{7,127},{8... | collective-permute-start | bytes 393224 | tf_op jit(solution)/shard_map/ppermute | solution.py:174
  107.6 0.0 collective-permute-done.6.r3_ref
  107.6 4.8 %collective-permute-done.5.r2_ref = bf16[64,1024]{1,0:T(8,128)(2,1)S(1)} collective-permute-done((bf16[64,1024]{1,0:T(8,128)(2,1)S(1)}, bf16[64,1024]{1,0:T(8,128)(2,1)S(1)}, u32[]{:S(2)}, u32[]{:S(2)}) %collective-permute-start.5) | collective-permute-done | bytes 131104 | tf_op jit(solution)/shard_map/ppermute | solution.py:174
  112.4 34.8 %collective-permute-done.4.r1_ref = bf16[64,1024]{1,0:T(8,128)(2,1)S(1)} collective-permute-done((bf16[64,1024]{1,0:T(8,128)(2,1)S(1)}, bf16[64,1024]{1,0:T(8,128)(2,1)S(1)}, u32[]{:S(2)}, u32[]{:S(2)}) %collective-permute-start.4) | collective-permute-done | bytes 131104 | tf_op jit(solution)/shard_map/ppermute | solution.py:174
  147.2 2.3 %shard_map.107 = (bf16[128,1024]{1,0:T(8,128)(2,1)}, f32[32,128]{1,0:T(8,128)}, bf16[40,128]{1,0:T(8,128)(2,1)S(1)}) custom-call(s32[8,128]{1,0:T(8,128)} %get-tuple-element.10.meta_ref, s32[1,128]{1,0:T(1,128)} %chosen_ref.3, f32[32,128]{1,0:T(8,128)} %bitcast.36, bf16[128,1024]{1,0:T(8,128)(2,1)} %bitcast.34, ...), custom_call_target="tpu_custom_call" | custom-call | tf_op jit(solution)/shard_map/pallas_call | solution.py:150
  149.5 3.7 %collective-permute-start.9 = (bf16[40,128]{1,0:T(8,128)(2,1)S(1)}, bf16[40,128]{1,0:T(8,128)(2,1)S(1)}, u32[]{:S(2)}, u32[]{:S(2)}) collective-permute-start(bf16[40,128]{1,0:T(8,128)(2,1)S(1)} %get-tuple-element.16), channel_id=1, source_target_pairs={{32,0},{33,1},{34,2},{35,3},{36,4},{37,5},{38,6},{39,7},{40,8},{41... | collective-permute-start | bytes 30728 | tf_op jit(solution)/shard_map/ppermute | solution.py:183
  153.3 0.0 collective-permute-done.8.late_ref
  153.3 0.0 collective-permute-done.7.early_ref
  153.3 5.8 %collective-permute-done.9.score_ref = bf16[40,128]{1,0:T(8,128)(2,1)S(1)} collective-permute-done((bf16[40,128]{1,0:T(8,128)(2,1)S(1)}, bf16[40,128]{1,0:T(8,128)(2,1)S(1)}, u32[]{:S(2)}, u32[]{:S(2)}) %collective-permute-start.9) | collective-permute-done | bytes 10272 | tf_op jit(solution)/shard_map/ppermute | solution.py:183
  159.1 0.0 copy-done
  159.1 2.0 %shard_map.108 = bf16[128,3584]{1,0:T(8,128)(2,1)} custom-call(bf16[64,3584]{1,0:T(8,128)(2,1)S(1)} %collective-permute-done.7.early_ref, bf16[64,3584]{1,0:T(8,128)(2,1)S(1)} %collective-permute-done.8.late_ref, bf16[40,128]{1,0:T(8,128)(2,1)S(1)} %collective-permute-done.9.score_ref, bf16[32,3584]{1,0:T(8,128)(2,1)S(1)} %copy-done), custom_call_target="tpu_custom_call" | custom-call | tf_op jit(solution)/shard_map/pallas_call | solution.py:150
  (2 shorter events, 0.1 us)
Async XLA Ops:
  3.7 46.2 %all-to-all-start = ((bf16[8,2,8,3584]{3,2,1,0:T(8,128)(2,1)}), bf16[8,2,8,3584]{3,2,1,0:T(8,128)(2,1)S(1)}, u32[]{:S(2)}, u32[]{:S(2)}) async-start(bf16[8,2,8,3584]{3,2,1,0:T(8,128)(2,1)} %bitcast.5), calls=%async_computation | async-start | bytes 1835008 | tf_op jit(solution)/shard_map/all_to_all | solution.py:186
  8.5 30.3 %collective-permute-start.1 = (bf16[72,3584]{1,0:T(8,128)(2,1)S(1)}, bf16[72,3584]{1,0:T(8,128)(2,1)S(1)}, u32[]{:S(2)}, u32[]{:S(2)}) collective-permute-start(bf16[72,3584]{1,0:T(8,128)(2,1)S(1)} %get-tuple-element.12), channel_id=1, source_target_pairs={{0,120},{1,121},{2,122},{3,123},{4,124},{5,125},{6,126},{7,127},{8... | collective-permute-start | bytes 1548296 | tf_op jit(solution)/shard_map/ppermute | solution.py:174
  26.7 21.9 %collective-permute-start.2 = (bf16[64,3584]{1,0:T(8,128)(2,1)S(1)}, bf16[64,3584]{1,0:T(8,128)(2,1)S(1)}, u32[]{:S(2)}, u32[]{:S(2)}) collective-permute-start(bf16[64,3584]{1,0:T(8,128)(2,1)S(1)} %get-tuple-element.13), channel_id=1, source_target_pairs={{0,120},{1,121},{2,122},{3,123},{4,124},{5,125},{6,126},{7,127},{8... | collective-permute-start | bytes 1376264 | tf_op jit(solution)/shard_map/ppermute | solution.py:174
  38.8 20.0 %collective-permute-start.3 = (bf16[72,3584]{1,0:T(8,128)(2,1)S(1)}, bf16[72,3584]{1,0:T(8,128)(2,1)S(1)}, u32[]{:S(2)}, u32[]{:S(2)}) collective-permute-start(bf16[72,3584]{1,0:T(8,128)(2,1)S(1)} %collective-permute-done.1.early_ref), channel_id=1, source_target_pairs={{0,120},{1,121},{2,122},{3,123},{4,124},{5,125},{6,126},{7,127},{8... | collective-permute-start | bytes 1548296 | tf_op jit(solution)/shard_map/ppermute | solution.py:174
  49.9 13.0 %all-to-all-start.1 = ((bf16[8,8,3584]{2,1,0:T(8,128)(2,1)}), bf16[8,8,3584]{2,1,0:T(8,128)(2,1)S(1)}, u32[]{:S(2)}, u32[]{:S(2)}) async-start(bf16[8,8,3584]{2,1,0:T(8,128)(2,1)} %bitcast.8), calls=%async_computation.1 | async-start | bytes 917504 | tf_op jit(solution)/shard_map/all_to_all | solution.py:186
  55.5 16.6 %collective-permute-start = (bf16[64,3584]{1,0:T(8,128)(2,1)}, bf16[64,3584]{1,0:T(8,128)(2,1)S(1)}, u32[]{:S(2)}, u32[]{:S(2)}) collective-permute-start(bf16[64,3584]{1,0:T(8,128)(2,1)} %get-tuple-element.17), channel_id=1, source_target_pairs={{0,8},{1,9},{2,10},{3,11},{4,12},{5,13},{6,14},{7,15},{8,16},{9,17... | collective-permute-start | bytes 1376264 | tf_op jit(solution)/shard_map/ppermute | solution.py:174
  59.9 99.2 %copy-start = (bf16[32,3584]{1,0:T(8,128)(2,1)S(1)}, bf16[32,3584]{1,0:T(8,128)(2,1)}, u32[]{:S(2)}) copy-start(bf16[32,3584]{1,0:T(8,128)(2,1)} %router_ref.1) | copy-start | bytes 688132
  62.8 13.0 %all-to-all-start.2 = ((bf16[8,8,3584]{2,1,0:T(8,128)(2,1)}), bf16[8,8,3584]{2,1,0:T(8,128)(2,1)S(1)}, u32[]{:S(2)}, u32[]{:S(2)}) async-start(bf16[8,8,3584]{2,1,0:T(8,128)(2,1)} %bitcast.10), calls=%async_computation.2 | async-start | bytes 917504 | tf_op jit(solution)/shard_map/all_to_all | solution.py:186
  83.0 14.9 %all-to-all-start.3 = ((bf16[8,4,8,1024]{3,2,1,0:T(8,128)(2,1)}), bf16[8,4,8,1024]{3,2,1,0:T(8,128)(2,1)S(1)}, u32[]{:S(2)}, u32[]{:S(2)}) async-start(bf16[8,4,8,1024]{3,2,1,0:T(8,128)(2,1)} %shard_map.106), calls=%async_computation.3 | async-start | bytes 1048576 | tf_op jit(solution)/shard_map/all_to_all | solution.py:186
  87.9 65.4 %collective-permute-start.8 = (bf16[64,3584]{1,0:T(8,128)(2,1)S(1)}, bf16[64,3584]{1,0:T(8,128)(2,1)S(1)}, u32[]{:S(2)}, u32[]{:S(2)}) collective-permute-start(bf16[64,3584]{1,0:T(8,128)(2,1)S(1)} %collective-permute-done.2.late_ref), channel_id=1, source_target_pairs={{24,0},{25,1},{26,2},{27,3},{28,4},{29,5},{30,6},{31,7},{32,8},{33... | collective-permute-start | bytes 1376264 | tf_op jit(solution)/shard_map/ppermute | solution.py:183
  93.0 60.2 %collective-permute-start.7 = (bf16[64,3584]{1,0:T(8,128)(2,1)S(1)}, bf16[64,3584]{1,0:T(8,128)(2,1)S(1)}, u32[]{:S(2)}, u32[]{:S(2)}) collective-permute-start(bf16[64,3584]{1,0:T(8,128)(2,1)S(1)} %slice.34), channel_id=1, source_target_pairs={{16,0},{17,1},{18,2},{19,3},{20,4},{21,5},{22,6},{23,7},{24,8},{25... | collective-permute-start | bytes 1376264 | tf_op jit(solution)/shard_map/ppermute | solution.py:183
  98.0 9.6 %collective-permute-start.6 = (bf16[64,1024]{1,0:T(8,128)(2,1)S(1)}, bf16[64,1024]{1,0:T(8,128)(2,1)S(1)}, u32[]{:S(2)}, u32[]{:S(2)}) collective-permute-start(bf16[64,1024]{1,0:T(8,128)(2,1)S(1)} %get-tuple-element.19), channel_id=1, source_target_pairs={{0,8},{1,9},{2,10},{3,11},{4,12},{5,13},{6,14},{7,15},{8,16},{9,17... | collective-permute-start | bytes 393224 | tf_op jit(solution)/shard_map/ppermute | solution.py:174
  99.9 12.5 %collective-permute-start.5 = (bf16[64,1024]{1,0:T(8,128)(2,1)S(1)}, bf16[64,1024]{1,0:T(8,128)(2,1)S(1)}, u32[]{:S(2)}, u32[]{:S(2)}) collective-permute-start(bf16[64,1024]{1,0:T(8,128)(2,1)S(1)} %get-tuple-element.20), channel_id=1, source_target_pairs={{0,16},{1,17},{2,18},{3,19},{4,20},{5,21},{6,22},{7,23},{8,24},{9,... | collective-permute-start | bytes 393224 | tf_op jit(solution)/shard_map/ppermute | solution.py:174
  103.3 44.0 %collective-permute-start.4 = (bf16[64,1024]{1,0:T(8,128)(2,1)S(1)}, bf16[64,1024]{1,0:T(8,128)(2,1)S(1)}, u32[]{:S(2)}, u32[]{:S(2)}) collective-permute-start(bf16[64,1024]{1,0:T(8,128)(2,1)S(1)} %get-tuple-element.21), channel_id=1, source_target_pairs={{0,120},{1,121},{2,122},{3,123},{4,124},{5,125},{6,126},{7,127},{8... | collective-permute-start | bytes 393224 | tf_op jit(solution)/shard_map/ppermute | solution.py:174
  149.5 9.5 %collective-permute-start.9 = (bf16[40,128]{1,0:T(8,128)(2,1)S(1)}, bf16[40,128]{1,0:T(8,128)(2,1)S(1)}, u32[]{:S(2)}, u32[]{:S(2)}) collective-permute-start(bf16[40,128]{1,0:T(8,128)(2,1)S(1)} %get-tuple-element.16), channel_id=1, source_target_pairs={{32,0},{33,1},{34,2},{35,3},{36,4},{37,5},{38,6},{39,7},{40,8},{41... | collective-permute-start | bytes 30728 | tf_op jit(solution)/shard_map/ppermute | solution.py:183
